TPU v7x, 512 devices: a whole 4x8x8 slice. The times are simulated.
512 devices in a mesh: row: 32 (over y, x), col: 16 (over z, core).
Axes of the slice: x: 4, y: 8, z: 8, core: 2. Of those that a mesh axis runs over, the one named last changes fastest.
Arguments:
- weights: bfloat16 [8192, 8192], P('row', 'col'), may hold values from 0.0099487305 to 1
- tile_mask: int32 [64, 64], P('row', 'col'), may hold values from 0 to 1, as said below
Outputs:
- flow: float32 [8192, 8192], P('row', 'col')
Inputs may be any that keep to these rules, and one draw needn't show every extreme that they name: `tile_mask`: each column of tiles holds exactly 8 ones, the diagonal tile among them.
All inputs are finite; a program needn't handle non-finite values.
Results may differ from a plain program's by a relative error of at most 0.00095.
Values may be sent and summed in bfloat16 or wider, within the bound.
No kernel may reach another device: no remote copies, remote signals or barrier semaphores. Data moves between devices by JAX's collectives and lax.ppermute only.
A program may use at most 64 MiB of HBM per device.

v0:
```python
import jax
import jax.numpy as jnp
from jax import lax
from jax.sharding import PartitionSpec as P

KEEP = 8


def from_everyone(shard, axis):
    copies = jnp.broadcast_to(shard, (lax.axis_size(axis), *shard.shape))
    return lax.all_to_all(copies, axis, split_axis=0, concat_axis=0, tiled=True)


def of_everyone(shard, axis):
    return from_everyone(shard, axis).sum(axis=0)


def laid_out(tiles, dim):
    shape = list(tiles.shape[1:])
    shape[dim] *= tiles.shape[0]
    return jnp.moveaxis(tiles, 0, dim).reshape(shape)


def collect(shard, axis, dim):
    tiles = from_everyone(shard, axis)
    return laid_out(tiles, dim)


def cut_along(shard, dim, size):
    before, after = (shard.shape[:dim], shard.shape[dim + 1 :])
    return jnp.moveaxis(shard.reshape(*before, size, -1, *after), dim, 0)


def sum_at_owner(shard, axis, dim):
    tiles = cut_along(shard, dim, lax.axis_size(axis))
    arrived = lax.all_to_all(tiles, axis, split_axis=0, concat_axis=0, tiled=True)
    return arrived.astype(jnp.float32).sum(axis=0)


def filled_up(lines, size):
    spare = -lines.shape[0] % size
    if not spare:
        return lines
    return jnp.concatenate([lines, jnp.zeros((spare, *lines.shape[1:]), lines.dtype)])


def total_of(shard, axes):
    lines = shard.reshape(-1, shard.shape[-1])
    own = sum_at_owner(filled_up(lines, lax.axis_size(axes)), axes, 0)
    whole = collect(own.astype(jnp.bfloat16), axes, 0)
    return whole[: len(lines)].reshape(shard.shape).astype(jnp.float32)


def on_device(weights, tile_mask):
    tile_rows, tile_cols = tile_mask.shape
    row_count, col_count = weights.shape
    tile_size = row_count // tile_rows
    shaped = weights.astype(jnp.float32).reshape(tile_rows, tile_size, tile_cols, tile_size)
    masked = (shaped * tile_mask.astype(jnp.float32)[:, None, :, None]).reshape(
        row_count, col_count
    )
    degree = of_everyone(jnp.sum(masked, axis=0), "row")
    markov = (masked / degree[None, :]).astype(jnp.bfloat16)
    column_mask = collect(tile_mask, "row", 0)
    all_tiles = column_mask.shape[0]
    rank = jnp.cumsum(column_mask, axis=0) - column_mask
    slots = lax.broadcasted_iota(jnp.int32, (all_tiles, tile_cols, KEEP), 2)
    chosen = jnp.logical_and(column_mask[:, :, None] == 1, rank[:, :, None] == slots).astype(
        jnp.int32
    )
    tile_ids = lax.broadcasted_iota(jnp.int32, (all_tiles, tile_cols, KEEP), 0)
    source_ids = jnp.sum(tile_ids * chosen, axis=0)
    base = lax.axis_index("row") * tile_rows
    own_slots = lax.dynamic_slice_in_dim(chosen, base, tile_rows, 0).astype(jnp.bfloat16)
    local_tiles = markov.reshape(tile_rows, tile_size, tile_cols, tile_size)
    placed = jnp.einsum(
        "lcs,lacb->csab", own_slots, local_tiles, preferred_element_type=jnp.float32
    )
    gathered_tiles = total_of(placed.astype(jnp.bfloat16), "row").astype(jnp.bfloat16)
    left_panel = lax.all_gather(markov, "col", axis=1, tiled=True)
    left_tiles = left_panel.reshape(row_count, all_tiles, tile_size)
    selected = jnp.take(left_tiles, source_ids, axis=1)
    expanded = jnp.einsum(
        "rcsa,csab->rcb", selected, gathered_tiles, preferred_element_type=jnp.float32
    )
    expanded = expanded.reshape(row_count, col_count)
    inflated = expanded * expanded
    mass = of_everyone(jnp.sum(inflated, axis=0), "row")
    nodes = row_count * lax.axis_size("row")
    return inflated / mass[None, :] * nodes


def solution(mesh):
    placed = (P("row", "col"), P("row", "col"))
    return jax.shard_map(
        on_device, mesh=mesh, in_specs=placed, out_specs=P("row", "col"), check_vma=False
    )
```

profile of v0, /device:TPU:128, one launch (start us, length us, event | category | flops | bytes accessed | tf_op | source)
XLA Modules:
  0.0 133.4 jit_solution(13419072680064312521)
XLA Ops:
  6.5 0.0 copy-start
  6.5 0.0 all-gather.2.cloned.1.call-start
  6.5 0.8 convert_element_type.25
  7.3 0.1 copy.42
  7.4 1.1 copy.41
  8.5 0.2 mul.35
  8.7 0.1 fusion.11
  8.9 19.7 %all_to_all.27 = f32[32,1,512]{2,1,0:T(1,128)S(1)} all-to-all(f32[32,1,512]{2,1,0:T(1,128)S(1)} %broadcast_in_dim.29), channel_id=1, replica_groups=mesh['row'=32,'col'=16] {'row'}, dimensions={0} | all-to-all | bytes 131072 | tf_op jit(solution)/shard_map/all_to_all | solution.py:11
  28.6 0.1 reduce_sum.60
  28.7 0.8 divide_convert_fusion
  29.5 0.0 all-gather.2.cloned.1.call-update
  29.5 0.0 copy-done
  29.5 0.6 broadcast_in_dim.28
  30.2 3.8 %all-to-all-start = ((s32[32,2,4]{2,1,0:T(2,128)}), s32[32,2,4]{2,1,0:T(2,128)S(1)}, u32[]{:S(2)}, u32[]{:S(2)}) async-start(s32[32,2,4]{2,1,0:T(2,128)} %broadcast_in_dim.28), calls=%async_computation | async-start | bytes 65536 | tf_op jit(solution)/shard_map/all_to_all | solution.py:11
  34.0 9.8 %all-to-all-done = s32[32,2,4]{2,1,0:T(2,128)S(1)} async-done(((s32[32,2,4]{2,1,0:T(2,128)}), s32[32,2,4]{2,1,0:T(2,128)S(1)}, u32[]{:S(2)}, u32[]{:S(2)}) %all-to-all-start) | async-done | bytes 1056 | tf_op jit(solution)/shard_map/all_to_all | solution.py:11
  43.8 0.1 reduce_window_sum.11
  43.9 0.1 copy.39
  44.0 0.1 copy.40
  44.1 0.2 fusion.12
  44.2 1.0 reshape.64
  45.2 0.3 copy.44
  45.6 0.5 convolution_convert_fusion
  46.1 0.2 copy.45
  46.3 29.5 %all_to_all.28 = bf16[32,128,128]{2,1,0:T(8,128)(2,1)S(1)} all-to-all(bf16[32,128,128]{2,1,0:T(8,128)(2,1)S(1)} %bitcast.49), channel_id=1, replica_groups=mesh['row'=32,'col'=16] {'row'}, dimensions={0} | all-to-all | bytes 2097152 | tf_op jit(solution)/shard_map/all_to_all | solution.py:36
  75.8 0.2 reduce_sum.61
  76.0 0.1 copy.46
  76.1 1.3 broadcast_in_dim.30
  77.4 4.8 %all-to-all-start.3 = ((bf16[32,128,128]{1,2,0:T(8,128)(2,1)}), bf16[32,128,128]{1,2,0:T(8,128)(2,1)S(1)}, u32[]{:S(2)}, u32[]{:S(2)}) async-start(bf16[32,128,128]{1,2,0:T(8,128)(2,1)} %broadcast_in_dim.30), calls=%async_computation.3 | async-start | bytes 2097152 | tf_op jit(solution)/shard_map/all_to_all | solution.py:11
  82.3 0.1 select_reduce_fusion
  82.4 0.1 reshape.68
  82.5 0.0 all-gather.2.cloned.1.call-done
  82.6 6.4 %copy.47 = bf16[256,64,128]{2,0,1:T(8,128)(2,1)} copy(bf16[256,64,128]{0,2,1:T(8,128)(2,1)} %bitcast.48) | data formatting | bytes 8388608 | tf_op jit(solution)/shard_map/reshape | solution.py:81
  88.9 3.1 %gather_fusion = bf16[32,256,128]{2,1,0:T(8,128)(2,1)S(1)} fusion(bf16[256,64,128]{2,0,1:T(8,128)(2,1)} %copy.47, s32[1024]{0:T(1024)S(1)} %pad_clamp_fusion), kind=kCustom, calls=%fused_computation | custom fusion | bytes 4194432 | tf_op jit(solution)/shard_map/jit(_take)/gather | solution.py:82
  92.1 15.9 %all-to-all-done.3 = bf16[32,128,128]{1,2,0:T(8,128)(2,1)S(1)} async-done(((bf16[32,128,128]{1,2,0:T(8,128)(2,1)}), bf16[32,128,128]{1,2,0:T(8,128)(2,1)S(1)}, u32[]{:S(2)}, u32[]{:S(2)}) %all-to-all-start.3) | async-done | bytes 1048608 | tf_op jit(solution)/shard_map/all_to_all | solution.py:11
  108.0 1.7 %fusion.18 = (f32[4,128]{1,0:T(4,128)S(1)}, f32[4,128,256]{2,1,0:T(8,128)}) fusion(bf16[4,8,128,128]{2,3,1,0:T(8,128)(2,1)S(1)} %bitcast.51, bf16[4,8,256,128]{3,2,1,0:T(8,128)(2,1)S(1)} %bitcast.50, pred[4,8]{1,0:T(4,128)(4,1)S(1)} %compare_and_fusion), kind=kOutput, calls=%fused_computation.26 | convolution fusion | flops 269745664 | bytes 3672096 | tf_op jit(solution)/shard_map/rcsa,csab->rcb/dot_general | solution.py:83
  109.7 0.7 broadcast_in_dim.34
  110.3 5.3 %all-to-all-start.4 = ((f32[32,1,512]{2,1,0:T(1,128)}), f32[32,1,512]{2,1,0:T(1,128)S(1)}, u32[]{:S(2)}, u32[]{:S(2)}) async-start(f32[32,1,512]{2,1,0:T(1,128)} %broadcast_in_dim.34), calls=%async_computation.4 | async-start | bytes 131072 | tf_op jit(solution)/shard_map/all_to_all | solution.py:11
  115.6 1.2 copy.49
  116.9 8.7 %all-to-all-done.4 = f32[32,1,512]{2,1,0:T(1,128)S(1)} async-done(((f32[32,1,512]{2,1,0:T(1,128)}), f32[32,1,512]{2,1,0:T(1,128)S(1)}, u32[]{:S(2)}, u32[]{:S(2)}) %all-to-all-start.4) | async-done | bytes 65568 | tf_op jit(solution)/shard_map/all_to_all | solution.py:11
  125.6 0.1 reduce_sum.65
  125.7 0.9 divide_multiply_fusion
  (6 shorter events, 0.1 us)
Async XLA Ops:
  6.5 23.0 %copy-start = (s32[2,4]{1,0:T(2,128)S(1)}, s32[2,4]{1,0:T(2,128)}, u32[]{:S(2)}) copy-start(s32[2,4]{1,0:T(2,128)} %param.3) | copy-start | bytes 100
  6.5 76.0 %all-gather.2.cloned.1.call-start = ((), (), s32[]{:S(2)}) async-start(), calls=%async_computation.5 | async-start | bytes 4456448 | tf_op jit(solution)/shard_map/all_gather | solution.py:80
  30.2 13.6 %all-to-all-start = ((s32[32,2,4]{2,1,0:T(2,128)}), s32[32,2,4]{2,1,0:T(2,128)S(1)}, u32[]{:S(2)}, u32[]{:S(2)}) async-start(s32[32,2,4]{2,1,0:T(2,128)} %broadcast_in_dim.28), calls=%async_computation | async-start | bytes 65536 | tf_op jit(solution)/shard_map/all_to_all | solution.py:11
  77.4 30.5 %all-to-all-start.3 = ((bf16[32,128,128]{1,2,0:T(8,128)(2,1)}), bf16[32,128,128]{1,2,0:T(8,128)(2,1)S(1)}, u32[]{:S(2)}, u32[]{:S(2)}) async-start(bf16[32,128,128]{1,2,0:T(8,128)(2,1)} %broadcast_in_dim.30), calls=%async_computation.3 | async-start | bytes 2097152 | tf_op jit(solution)/shard_map/all_to_all | solution.py:11
  110.3 15.3 %all-to-all-start.4 = ((f32[32,1,512]{2,1,0:T(1,128)}), f32[32,1,512]{2,1,0:T(1,128)S(1)}, u32[]{:S(2)}, u32[]{:S(2)}) async-start(f32[32,1,512]{2,1,0:T(1,128)} %broadcast_in_dim.34), calls=%async_computation.4 | async-start | bytes 131072 | tf_op jit(solution)/shard_map/all_to_all | solution.py:11
Sparse Core Ops, SparseCore 0:
  29.7 40.1 all-gather.1
where the time goes:
time: 134 us; the launch traced here: 133 us
  blocking collectives  49.2 us (37%)
  waiting for transfers between devices  34.4 us (26%)
  local copies, waits for them, and re-layouts  16.7 us (12%)
  starting transfers between devices  14 us (10%)
  between operations  13.5 us (10%)
  other arithmetic  3.34 us (2%)
  matrix products  2.2 us (2%)
    all_to_all x3, waiting for transfers between devices, from_everyone(): return lax.all_to_all(copies, axis, split_axis=0, concat_axis=0, tiled=True)  34.4 us
    all_to_all x1, blocking collectives, sum_at_owner(): lax.all_to_all(tiles, axis, split_axis=0, concat_axis=0, tiled=True)  29.5 us
    all_to_all x1, blocking collectives, from_everyone(): return lax.all_to_all(copies, axis, split_axis=0, concat_axis=0, tiled=True)  19.7 us
    all_to_all x3, starting transfers between devices, from_everyone(): return lax.all_to_all(copies, axis, split_axis=0, concat_axis=0, tiled=True)  14 us
    reshape x1, local copies, waits for them, and re-layouts, on_device(): left_tiles = left_panel.reshape(row_count, all_tiles, tile_size)  6.38 us
    gather x1, local copies, waits for them, and re-layouts, on_device(): selected = jnp.take(left_tiles, source_ids, axis=1)  3.14 us
  transfers between devices with their start and end apart: 4, of which 3 were waited for; matrix products, arithmetic and copies ran while one was open for 12% of the time, Pallas kernels for 0%

commit v1 on v0

v1 whole, which is shorter than its diff:
```python
import jax
import jax.numpy as jnp
from jax import lax
from jax.experimental import pallas as pl
from jax.experimental.pallas import tpu as pltpu
from jax.sharding import Mesh, PartitionSpec as P

KEEP = 8
TILE = 128
SLICE = 16
NY, NX, NZ, NC = 8, 4, 8, 2
ROWS = NY * NX
ROW = ("y", "x")
F32, BF16 = jnp.float32, jnp.bfloat16
VMEM = pl.BlockSpec(memory_space=pltpu.VMEM)
SMEM = pl.BlockSpec(memory_space=pltpu.SMEM)


def exchange(blocks, axis):
    return lax.all_to_all(blocks, axis, split_axis=0, concat_axis=0, tiled=True)


def to_everyone(block, axis, size):
    return exchange(jnp.broadcast_to(block, (size, *block.shape)), axis)


def swap_cores(block):
    return lax.ppermute(block, "core", [(0, 1), (1, 0)])


def split3(v):
    parts = []
    for _ in range(3):
        part = v.astype(BF16)
        parts.append(part)
        v = v - part.astype(F32)
    return parts


def prepare_kernel(mask_ref, w_ref, upper_ref, lower_ref, sent_ref):
    lane = lax.broadcasted_iota(jnp.int32, (1, TILE), 1)
    on_row = jnp.zeros((1, TILE), F32)
    sums = []
    for c in range(4):
        cols = pl.ds(c * TILE, TILE)
        total = jnp.zeros((1, TILE), F32)
        for t in range(2):
            panel = (upper_ref, lower_ref)[t]
            on = mask_ref[t, c].astype(F32)
            on_row = jnp.where(lane == t * 4 + c, on, on_row)
            tile = w_ref[pl.ds(t * TILE, TILE), cols].astype(F32) * on
            total = total + jnp.sum(tile, axis=0, keepdims=True)
            tile = tile.astype(BF16)
            panel[:, cols] = tile
            for e in range(8):
                sent_ref[8 * c + e, pl.ds(t * SLICE, SLICE)] = tile[e * SLICE : (e + 1) * SLICE]
        sums.append(split3(total))
    rows = [sums[c][p].astype(F32) for p in range(3) for c in range(4)]
    extra = jnp.concatenate([*rows, on_row, jnp.zeros((3, TILE), F32)], axis=0).astype(BF16)
    for d in range(ROWS):
        sent_ref[d, pl.ds(2 * SLICE, SLICE)] = extra


def prepare(mask, weights):
    return pl.pallas_call(
        prepare_kernel,
        out_shape=(
            jax.ShapeDtypeStruct((TILE, 4 * TILE), BF16),
            jax.ShapeDtypeStruct((TILE, 4 * TILE), BF16),
            jax.ShapeDtypeStruct((ROWS, 3 * SLICE, TILE), BF16),
        ),
        in_specs=[SMEM, VMEM],
        out_specs=(VMEM,) * 3,
        name="prepare",
    )(mask, weights)


def place_kernel(own_ref, ids_ref, got_ref, lower_ref, placed_ref, extended_ref):
    extra = jnp.zeros((SLICE, TILE), F32)
    for r in range(ROWS):
        extra = extra + got_ref[r, pl.ds(2 * SLICE, SLICE)].astype(F32)
    degree = extra[0:4] + (extra[4:8] + extra[8:12])
    own = own_ref[0]
    mine = jnp.zeros((1, TILE), F32)
    for c in range(4):
        mine = jnp.where(own == c, degree[c : c + 1], mine)
    extended_ref[pl.ds(0, TILE)] = lower_ref[...]
    for c in range(4):
        parts = [part.astype(F32) for part in split3(degree[c : c + 1])]
        block = jnp.concatenate([*parts, jnp.zeros((13, TILE), F32)], axis=0)
        extended_ref[pl.ds(TILE, SLICE), pl.ds(c * TILE, TILE)] = block.astype(BF16)
    for s in range(KEEP):
        k = ids_ref[s, own]
        start = pl.multiple_of((k % 2) * SLICE, SLICE)
        tile = got_ref[k // 2, pl.ds(start, SLICE)].astype(F32)
        placed_ref[s] = (tile / mine).astype(BF16)


def place(own, ids, got, lower):
    return pl.pallas_call(
        place_kernel,
        out_shape=(
            jax.ShapeDtypeStruct((KEEP, SLICE, TILE), BF16),
            jax.ShapeDtypeStruct((TILE + SLICE, 4 * TILE), BF16),
        ),
        in_specs=[SMEM, SMEM, VMEM, VMEM],
        out_specs=(VMEM, VMEM),
        name="place",
    )(own, ids, got, lower)


def expand_kernel(core_ref, ids_ref, upper_ref, upper_o_ref, lower_ref, lower_o_ref, right_ref, out_ref, mass_ref):
    core = core_ref[0]
    for c in range(4):
        cols = pl.ds(c * TILE, TILE)
        totals = [jnp.zeros((TILE, TILE), F32), jnp.zeros((TILE, TILE), F32)]
        for s in range(KEEP):
            k = ids_ref[s, c]
            column = k // 4
            z = column // 2
            ours = column % 2 == core
            inside = pl.ds(pl.multiple_of((k % 4) * TILE, TILE), TILE)
            parts = jnp.where(
                ours,
                lower_ref[z, pl.ds(TILE, SLICE), inside].astype(F32),
                lower_o_ref[z, pl.ds(TILE, SLICE), inside].astype(F32),
            )
            inverse = 1.0 / (parts[0:1] + (parts[1:2] + parts[2:3]))
            right = right_ref[pl.ds(8 * c, 8), s].reshape(TILE, TILE)
            for t in range(2):
                mine, other = ((upper_ref, upper_o_ref), (lower_ref, lower_o_ref))[t]
                left = jnp.where(
                    ours,
                    mine[z, pl.ds(0, TILE), inside].astype(F32),
                    other[z, pl.ds(0, TILE), inside].astype(F32),
                )
                left = (left * inverse).astype(BF16)
                totals[t] = totals[t] + jnp.dot(left, right, preferred_element_type=F32)
        part = jnp.zeros((1, TILE), F32)
        for t in range(2):
            squared = totals[t] * totals[t]
            out_ref[pl.ds(t * TILE, TILE), cols] = squared
            part = part + jnp.sum(squared, axis=0, keepdims=True)
        mass_ref[:, cols] = part


def expand(core, ids, upper, upper_o, lower, lower_o, right):
    return pl.pallas_call(
        expand_kernel,
        out_shape=(
            jax.ShapeDtypeStruct((2 * TILE, 4 * TILE), F32),
            jax.ShapeDtypeStruct((1, 4 * TILE), F32),
        ),
        in_specs=[SMEM, SMEM] + [VMEM] * 5,
        out_specs=(VMEM, VMEM),
        name="expand",
    )(core, ids, upper, upper_o, lower, lower_o, right)


def on_device(weights, tile_mask):
    upper, lower, sent = prepare(tile_mask, weights)
    upper_z = lax.all_gather(upper, "z")
    got = exchange(sent, ROW)
    there = (got[:, 44, :8].reshape(64, 4) > 0).astype(jnp.int32)
    rank = jnp.cumsum(there, axis=0) - there
    tile_ids = lax.broadcasted_iota(jnp.int32, (KEEP, 64, 4), 1)
    ranks = lax.broadcasted_iota(jnp.int32, (KEEP, 64, 4), 0)
    chosen = (there == 1)[None] & (rank[None] == ranks)
    ids = jnp.sum(jnp.where(chosen, tile_ids, 0), axis=1)
    own = (lax.axis_index("y") // 2).reshape(1)
    core = lax.axis_index("core")
    placed, lower = place(own, ids, got, lower)
    lower_z = lax.all_gather(lower, "z")
    right = to_everyone(placed, ROW, ROWS)
    inflated, mass = expand(
        core.reshape(1), ids, upper_z, swap_cores(upper_z), lower_z, swap_cores(lower_z), right
    )
    mass = to_everyone(mass, ROW, ROWS).sum(axis=0)
    nodes = 64 * TILE
    return inflated * (nodes / mass)


def solution(mesh):
    split = Mesh(mesh.devices.reshape(NY, NX, NZ, NC), ("y", "x", "z", "core"))
    placed = P(ROW, ("z", "core"))
    return jax.shard_map(
        on_device, mesh=split, in_specs=(placed, placed), out_specs=placed, check_vma=False
    )
```

time: 134 us -> 160 us (1.19)
  the two profiles are of different devices: /device:TPU:128 before, /device:TPU:1 now
where the time goes in v1:
time: 160 us; the launch traced here: 159 us
  waiting for transfers between devices  82.4 us (52%)
  starting transfers between devices  30 us (19%)
  blocking collectives  17.9 us (11%)
  between operations  13.5 us (8%)
  Pallas kernels  7.99 us (5%)
  local copies, waits for them, and re-layouts  5 us (3%)
  other arithmetic  2.32 us (1%)
    all_gather x1, waiting for transfers between devices, on_device(): upper_z = lax.all_gather(upper, 'z')  34.7 us
    all_gather x1, waiting for transfers between devices, on_device(): lower_z = lax.all_gather(lower, 'z')  30.8 us
    all_to_all x1, blocking collectives, exchange(): return lax.all_to_all(blocks, axis, split_axis=0, concat_axis=0, tiled=True)  17.9 us
    all_to_all x2, starting transfers between devices, exchange(): return lax.all_to_all(blocks, axis, split_axis=0, concat_axis=0, tiled=True)  15.5 us
    ppermute x2, starting transfers between devices, swap_cores(): return lax.ppermute(block, 'core', [(0, 1), (1, 0)])  14.4 us
    all_to_all x2, waiting for transfers between devices, exchange(): return lax.all_to_all(blocks, axis, split_axis=0, concat_axis=0, tiled=True)  13.8 us
    pallas_call x1, Pallas kernels, expand(): pl.pallas_call(expand_kernel, out_shape=(jax.ShapeDtypeStruct((2 * TILE,...  4.39 us
  transfers between devices with their start and end apart: 6, of which 4 were waited for; matrix products, arithmetic and copies ran while one was open for 1% of the time, Pallas kernels for 0%

profile of v1, /device:TPU:1, one launch (start us, length us, event | category | flops | bytes accessed | tf_op | source)
XLA Modules:
  0.0 159.1 jit_solution(8745934728599551350)
XLA Ops:
  6.5 1.8 %prepare.1 = (bf16[128,512]{1,0:T(8,128)(2,1)}, bf16[128,512]{1,0:T(8,128)(2,1)}, bf16[32,48,128]{2,1,0:T(8,128)(2,1)}) custom-call(s32[2,4]{1,0:T(2,128)} %mask_ref.1, bf16[256,512]{1,0:T(8,128)(2,1)} %w_ref.1), custom_call_target="tpu_custom_call" | custom-call | tf_op jit(solution)/shard_map/prepare/pallas_call | solution.py:65
  8.4 10.5 %all-to-all-start = ((bf16[32,48,128]{2,1,0:T(8,128)(2,1)}), bf16[32,48,128]{2,1,0:T(8,128)(2,1)S(1)}, u32[]{:S(2)}, u32[]{:S(2)}) async-start(bf16[32,48,128]{2,1,0:T(8,128)(2,1)} %get-tuple-element.12), calls=%async_computation | async-start | bytes 786432 | tf_op jit(solution)/shard_map/all_to_all | solution.py:20
  18.9 0.0 all-gather.7.cloned.1.call-start
  18.9 13.8 %all-to-all-done.got_ref = bf16[32,48,128]{2,1,0:T(8,128)(2,1)S(1)} async-done(((bf16[32,48,128]{2,1,0:T(8,128)(2,1)}), bf16[32,48,128]{2,1,0:T(8,128)(2,1)S(1)}, u32[]{:S(2)}, u32[]{:S(2)}) %all-to-all-start) | async-done | bytes 393248 | tf_op jit(solution)/shard_map/all_to_all | solution.py:20
  32.7 0.0 copy-start.1
  32.7 0.1 fusion
  32.8 0.1 reshape.40
  32.8 0.1 reduce_window_sum.11
  32.9 0.1 copy.7
  33.0 0.1 copy.8
  33.1 0.2 select_reduce_fusion
  33.3 0.7 copy.10.ids_ref
  34.0 0.0 copy-done.1
  34.0 1.8 %place.1 = (bf16[8,16,128]{2,1,0:T(8,128)(2,1)}, bf16[144,512]{1,0:T(8,128)(2,1)}) custom-call(s32[1]{0:T(128)} %bitcast.2.own_ref, s32[8,4]{1,0:T(8,128)} %copy.10.ids_ref, bf16[32,48,128]{2,1,0:T(8,128)(2,1)} %copy-done.1, bf16[128,512]{1,0:T(8,128)(2,1)} %get-tuple-element.14.lower_ref), custom_call_target="tpu_custom_call" | custom-call | tf_op jit(solution)/shard_map/place/pallas_call | solution.py:100
  35.7 0.0 all-gather.7.cloned.1.call-update
  35.7 0.0 all-gather.5.cloned.1.call-start
  35.8 0.7 all-gather.5.cloned.1.call-update
  36.5 2.0 %broadcast_in_dim.13 = bf16[32,8,16,128]{3,2,1,0:T(8,128)(2,1)} broadcast(bf16[8,16,128]{2,1,0:T(8,128)(2,1)} %get-tuple-element.16), dimensions={1,2,3} | broadcast | bytes 1081344 | tf_op jit(solution)/shard_map/broadcast_in_dim | solution.py:24
  38.5 5.0 %all-to-all-start.1 = ((bf16[32,8,16,128]{3,2,1,0:T(8,128)(2,1)}), bf16[32,8,16,128]{3,2,1,0:T(8,128)(2,1)S(1)}, u32[]{:S(2)}, u32[]{:S(2)}) async-start(bf16[32,8,16,128]{3,2,1,0:T(8,128)(2,1)} %broadcast_in_dim.13), calls=%async_computation.1 | async-start | bytes 2097152 | tf_op jit(solution)/shard_map/all_to_all | solution.py:20
  43.5 30.8 %all-gather.7.cloned.1.call-done = bf16[1152,512]{1,0:T(8,128)(2,1)} async-done(((bf16[144,512]{1,0:T(8,128)(2,1)}), bf16[1152,512]{1,0:T(8,128)(2,1)}) %all-gather.7.cloned.1.call-update) | async-done | bytes 1179664 | tf_op jit(solution)/shard_map/all_gather | solution.py:173
  74.3 7.2 %collective-permute-start.1 = (bf16[8,144,512]{2,1,0:T(8,128)(2,1)}, bf16[8,144,512]{2,1,0:T(8,128)(2,1)S(1)}, u32[]{:S(2)}, u32[]{:S(2)}) collective-permute-start(bf16[8,144,512]{2,1,0:T(8,128)(2,1)} %bitcast.5), channel_id=1, source_target_pairs={{0,1},{1,0},{2,3},{3,2},{4,5},{5,4},{6,7},{7,6},{8,9},{9,8},{10,11... | collective-permute-start | bytes 3538952 | tf_op jit(solution)/shard_map/ppermute | solution.py:28
  81.5 34.7 %all-gather.5.cloned.1.call-done = bf16[1024,512]{1,0:T(8,128)(2,1)} async-done(((bf16[128,512]{1,0:T(8,128)(2,1)}), bf16[1024,512]{1,0:T(8,128)(2,1)}) %all-gather.5.cloned.1.call-update) | async-done | bytes 1048592 | tf_op jit(solution)/shard_map/all_gather | solution.py:162
  116.2 7.2 %collective-permute-start = (bf16[8,128,512]{2,1,0:T(8,128)(2,1)}, bf16[8,128,512]{2,1,0:T(8,128)(2,1)S(1)}, u32[]{:S(2)}, u32[]{:S(2)}) collective-permute-start(bf16[8,128,512]{2,1,0:T(8,128)(2,1)} %bitcast.7), channel_id=1, source_target_pairs={{0,1},{1,0},{2,3},{3,2},{4,5},{5,4},{6,7},{7,6},{8,9},{9,8},{10,11... | collective-permute-start | bytes 3145736 | tf_op jit(solution)/shard_map/ppermute | solution.py:28
  123.4 0.0 all-to-all-done.1.right_ref
  123.4 0.0 copy-start
  123.5 2.5 %collective-permute-done.upper_o_ref = bf16[8,128,512]{2,1,0:T(8,128)(2,1)S(1)} collective-permute-done((bf16[8,128,512]{2,1,0:T(8,128)(2,1)}, bf16[8,128,512]{2,1,0:T(8,128)(2,1)S(1)}, u32[]{:S(2)}, u32[]{:S(2)}) %collective-permute-start) | collective-permute-done | bytes 1048608 | tf_op jit(solution)/shard_map/ppermute | solution.py:28
  125.9 0.0 copy-start.3
  125.9 0.0 collective-permute-done.1.lower_o_ref
  125.9 0.0 copy-start.2
  125.9 0.0 copy-done
  125.9 0.9 copy-done.3
  126.9 0.4 copy-done.2
  127.3 4.4 %expand.1 = (f32[256,512]{1,0:T(8,128)}, f32[1,512]{1,0:T(1,128)}) custom-call(s32[1]{0:T(128)} %bitcast.core_ref, s32[8,4]{1,0:T(8,128)} %copy.10.ids_ref, bf16[8,128,512]{2,1,0:T(8,128)(2,1)} %bitcast.8, bf16[8,128,512]{2,1,0:T(8,128)(2,1)} %copy-done.3, bf16[8,144,512]{2,1,0:T(8,128)(2,1)} %bitcast.6, bf16[8,144,512]{2,1,0:T(8,128)(2,1)} %copy-done.2, ...), custom_call_target="tpu_custom_call" | custom-call | tf_op jit(solution)/shard_map/expand/pallas_call | solution.py:148
  131.7 0.7 broadcast_in_dim.14
  132.4 17.9 %all_to_all.15 = f32[32,1,512]{2,1,0:T(1,128)S(1)} all-to-all(f32[32,1,512]{2,1,0:T(1,128)S(1)} %broadcast_in_dim.14), channel_id=1, replica_groups=mesh['y'=8,'x'=4,'z'=8,'core'=2] {'y','x'}, dimensions={0} | all-to-all | bytes 131072 | tf_op jit(solution)/shard_map/all_to_all | solution.py:20
  150.3 0.1 reduce_sum.19
  150.4 1.9 %broadcast_multiply_fusion = f32[256,512]{1,0:T(8,128)} fusion(f32[256,512]{1,0:T(8,128)} %get-tuple-element.17, f32[512]{0:T(512)S(1)} %broadcast_divide_fusion), kind=kLoop, calls=%fused_computation | loop fusion | flops 131072 | bytes 1050624 | tf_op jit(solution)/shard_map/mul | solution.py:180
  (3 shorter events, 0.0 us)
Async XLA Ops:
  8.4 24.3 %all-to-all-start = ((bf16[32,48,128]{2,1,0:T(8,128)(2,1)}), bf16[32,48,128]{2,1,0:T(8,128)(2,1)S(1)}, u32[]{:S(2)}, u32[]{:S(2)}) async-start(bf16[32,48,128]{2,1,0:T(8,128)(2,1)} %get-tuple-element.12), calls=%async_computation | async-start | bytes 786432 | tf_op jit(solution)/shard_map/all_to_all | solution.py:20
  18.9 55.5 %all-gather.7.cloned.1.call-start = ((), (), s32[]{:S(2)}) async-start(), calls=%async_computation.4 | async-start | bytes 1327104 | tf_op jit(solution)/shard_map/all_gather | solution.py:173
  32.7 1.3 copy-start.1
  35.7 80.5 %all-gather.5.cloned.1.call-start = ((), (), s32[]{:S(2)}) async-start(), calls=%async_computation.3 | async-start | bytes 1179648 | tf_op jit(solution)/shard_map/all_gather | solution.py:162
  38.5 85.0 %all-to-all-start.1 = ((bf16[32,8,16,128]{3,2,1,0:T(8,128)(2,1)}), bf16[32,8,16,128]{3,2,1,0:T(8,128)(2,1)S(1)}, u32[]{:S(2)}, u32[]{:S(2)}) async-start(bf16[32,8,16,128]{3,2,1,0:T(8,128)(2,1)} %broadcast_in_dim.13), calls=%async_computation.1 | async-start | bytes 2097152 | tf_op jit(solution)/shard_map/all_to_all | solution.py:20
  74.3 51.6 %collective-permute-start.1 = (bf16[8,144,512]{2,1,0:T(8,128)(2,1)}, bf16[8,144,512]{2,1,0:T(8,128)(2,1)S(1)}, u32[]{:S(2)}, u32[]{:S(2)}) collective-permute-start(bf16[8,144,512]{2,1,0:T(8,128)(2,1)} %bitcast.5), channel_id=1, source_target_pairs={{0,1},{1,0},{2,3},{3,2},{4,5},{5,4},{6,7},{7,6},{8,9},{9,8},{10,11... | collective-permute-start | bytes 3538952 | tf_op jit(solution)/shard_map/ppermute | solution.py:28
  116.2 9.7 %collective-permute-start = (bf16[8,128,512]{2,1,0:T(8,128)(2,1)}, bf16[8,128,512]{2,1,0:T(8,128)(2,1)S(1)}, u32[]{:S(2)}, u32[]{:S(2)}) collective-permute-start(bf16[8,128,512]{2,1,0:T(8,128)(2,1)} %bitcast.7), channel_id=1, source_target_pairs={{0,1},{1,0},{2,3},{3,2},{4,5},{5,4},{6,7},{7,6},{8,9},{9,8},{10,11... | collective-permute-start | bytes 3145736 | tf_op jit(solution)/shard_map/ppermute | solution.py:28
  123.4 2.5 %copy-start = (bf16[32,8,16,128]{3,2,1,0:T(8,128)(2,1)}, bf16[32,8,16,128]{3,2,1,0:T(8,128)(2,1)S(1)}, u32[]{:S(2)}) copy-start(bf16[32,8,16,128]{3,2,1,0:T(8,128)(2,1)S(1)} %all-to-all-done.1.right_ref) | copy-start | bytes 3145732
  125.9 1.0 copy-start.3
  125.9 1.4 copy-start.2
Sparse Core Ops, SparseCore 0:
  35.9 38.4 all-gather.6
  76.4 39.7 all-gather.4

commit v2 on v1

v2 whole, which is shorter than its diff:
```python
import jax
import jax.numpy as jnp
from jax import lax
from jax.experimental import pallas as pl
from jax.experimental.pallas import tpu as pltpu
from jax.sharding import Mesh, PartitionSpec as P

KEEP = 8
TILE = 128
SLICE = 16
NY, NX, NZ, NC = 8, 4, 8, 2
ROWS = NY * NX
ROW = ("y", "x")
F32, BF16 = jnp.float32, jnp.bfloat16
VMEM = pl.BlockSpec(memory_space=pltpu.VMEM)
SMEM = pl.BlockSpec(memory_space=pltpu.SMEM)


def exchange(blocks, axis):
    return lax.all_to_all(blocks, axis, split_axis=0, concat_axis=0, tiled=True)


def split3(v):
    parts = []
    for _ in range(3):
        part = v.astype(BF16)
        parts.append(part)
        v = v - part.astype(F32)
    return parts


def prepare_kernel(mask_ref, w_ref, panel_ref, sent_ref):
    lane = lax.broadcasted_iota(jnp.int32, (1, TILE), 1)
    on_row = jnp.zeros((1, TILE), F32)
    sums = []
    for c in range(4):
        cols = pl.ds(c * TILE, TILE)
        total = jnp.zeros((1, TILE), F32)
        for t in range(2):
            on = mask_ref[t, c].astype(F32)
            on_row = jnp.where(lane == t * 4 + c, on, on_row)
            tile = w_ref[pl.ds(t * TILE, TILE), cols].astype(F32) * on
            total = total + jnp.sum(tile, axis=0, keepdims=True)
            tile = tile.astype(BF16)
            panel_ref[pl.ds(t * TILE, TILE), cols] = tile
            for e in range(8):
                sent_ref[8 * c + e, pl.ds(t * SLICE, SLICE)] = tile[e * SLICE : (e + 1) * SLICE]
        sums.append(split3(total))
    rows = [sums[c][p].astype(F32) for p in range(3) for c in range(4)]
    extra = jnp.concatenate([*rows, on_row, jnp.zeros((3, TILE), F32)], axis=0).astype(BF16)
    for d in range(ROWS):
        sent_ref[d, pl.ds(2 * SLICE, SLICE)] = extra


def prepare(mask, weights):
    return pl.pallas_call(
        prepare_kernel,
        out_shape=(
            jax.ShapeDtypeStruct((2 * TILE, 4 * TILE), BF16),
            jax.ShapeDtypeStruct((ROWS, 3 * SLICE, TILE), BF16),
        ),
        in_specs=[SMEM, VMEM],
        out_specs=(VMEM,) * 2,
        name="prepare",
    )(mask, weights)


def place_kernel(own_ref, ids_ref, got_ref, placed_ref, degree_ref):
    extra = jnp.zeros((SLICE, TILE), F32)
    for r in range(ROWS):
        extra = extra + got_ref[r, pl.ds(2 * SLICE, SLICE)].astype(F32)
    degree = extra[0:4] + (extra[4:8] + extra[8:12])
    degree_ref[...] = degree
    own = own_ref[0]
    mine = jnp.zeros((1, TILE), F32)
    for c in range(4):
        mine = jnp.where(own == c, degree[c : c + 1], mine)
    for s in range(KEEP):
        k = ids_ref[s, own]
        start = pl.multiple_of((k % 2) * SLICE, SLICE)
        tile = got_ref[k // 2, pl.ds(start, SLICE)].astype(F32)
        tile = (tile / mine).astype(BF16)
        for r in range(ROWS):
            placed_ref[r, s] = tile


def place(own, ids, got):
    return pl.pallas_call(
        place_kernel,
        out_shape=(
            jax.ShapeDtypeStruct((ROWS, KEEP, SLICE, TILE), BF16),
            jax.ShapeDtypeStruct((4, TILE), F32),
        ),
        in_specs=[SMEM, SMEM, VMEM],
        out_specs=(VMEM, VMEM),
        name="place",
    )(own, ids, got)


def expand_kernel(col_ref, ids_ref, degree_ref, panel_ref, right_ref, out_ref, mass_ref):
    col = col_ref[0]
    for c in range(4):
        cols = pl.ds(c * TILE, TILE)
        total = jnp.zeros((2 * TILE, TILE), F32)
        for s in range(KEEP):
            k = ids_ref[s, c]
            inside = pl.ds(pl.multiple_of((k % 4) * TILE, TILE), TILE)
            inverse = 1.0 / degree_ref[(k // 4) ^ col, pl.ds(k % 4, 1), :]
            right = right_ref[pl.ds(8 * c, 8), s].reshape(TILE, TILE)
            left = (panel_ref[k // 4, :, inside].astype(F32) * inverse).astype(BF16)
            total = total + jnp.dot(left, right, preferred_element_type=F32)
        total = total * total
        out_ref[:, cols] = total
        part = jnp.sum(total, axis=0, keepdims=True)
        for r in range(ROWS):
            mass_ref[r, :, cols] = part


def expand(col, ids, degree, panel, right):
    return pl.pallas_call(
        expand_kernel,
        out_shape=(
            jax.ShapeDtypeStruct((2 * TILE, 4 * TILE), F32),
            jax.ShapeDtypeStruct((ROWS, 1, 4 * TILE), F32),
        ),
        in_specs=[SMEM, SMEM] + [VMEM] * 3,
        out_specs=(VMEM, VMEM),
        name="expand",
    )(col, ids, degree, panel, right)


def spread(block, axis, size):
    step = 1
    while step < size:
        other = lax.ppermute(block, axis, [(i, i ^ step) for i in range(size)])
        block = jnp.concatenate([block, other])
        step *= 2
    return block


def on_device(weights, tile_mask):
    masked, sent = prepare(tile_mask, weights)
    panel = lax.all_gather(masked, ("z", "core"))
    got = exchange(sent, ROW)
    there = (got[:, 44, :8].reshape(64, 4) > 0).astype(jnp.int32)
    rank = jnp.cumsum(there, axis=0) - there
    tile_ids = lax.broadcasted_iota(jnp.int32, (KEEP, 64, 4), 1)
    ranks = lax.broadcasted_iota(jnp.int32, (KEEP, 64, 4), 0)
    chosen = (there == 1)[None] & (rank[None] == ranks)
    ids = jnp.sum(jnp.where(chosen, tile_ids, 0), axis=1)
    own = (lax.axis_index("y") // 2).reshape(1)
    col = lax.axis_index(("z", "core")).reshape(1)
    placed, degree = place(own, ids, got)
    right = exchange(placed, ROW)
    degree = spread(spread(degree[None], "core", NC), "z", NZ)
    inflated, mass = expand(col, ids, degree, panel, right)
    mass = exchange(mass, ROW).sum(axis=0)
    nodes = 64 * TILE
    return inflated * (nodes / mass)


def solution(mesh):
    split = Mesh(mesh.devices.reshape(NY, NX, NZ, NC), ("y", "x", "z", "core"))
    placed = P(ROW, ("z", "core"))
    return jax.shard_map(
        on_device, mesh=split, in_specs=(placed, placed), out_specs=placed, check_vma=False
    )
```

time: 160 us -> 105 us (0.66)
  the two profiles are of different devices: /device:TPU:1 before, /device:TPU:8 now
where the time goes in v2:
time: 105 us; the launch traced here: 104 us
  starting transfers between devices  36.6 us (35%)
  waiting for transfers between devices  20.3 us (19%)
  blocking collectives  18.8 us (18%)
  between operations  13.5 us (13%)
  Pallas kernels  8.06 us (8%)
  other arithmetic  4.35 us (4%)
  local copies, waits for them, and re-layouts  2.57 us (2%)
    ppermute x4, starting transfers between devices, spread(): other = lax.ppermute(block, axis, [(i, i ^ step) for i in range(size)])  21.6 us
    all_to_all x1, blocking collectives, exchange(): return lax.all_to_all(blocks, axis, split_axis=0, concat_axis=0, tiled=True)  18.8 us
    all_to_all x2, starting transfers between devices, exchange(): return lax.all_to_all(blocks, axis, split_axis=0, concat_axis=0, tiled=True)  15 us
    all_to_all x2, waiting for transfers between devices, exchange(): return lax.all_to_all(blocks, axis, split_axis=0, concat_axis=0, tiled=True)  14.7 us
    ppermute x4, waiting for transfers between devices, spread(): other = lax.ppermute(block, axis, [(i, i ^ step) for i in range(size)])  5.53 us
    pallas_call x1, Pallas kernels, expand(): pl.pallas_call(expand_kernel, out_shape=(jax.ShapeDtypeStruct((2 * TILE,...  4.02 us
    pallas_call x1, Pallas kernels, place(): pl.pallas_call(place_kernel, out_shape=(jax.ShapeDtypeStruct((ROWS, KEEP,...  2.16 us
  transfers between devices with their start and end apart: 7, of which 5 were waited for; matrix products, arithmetic and copies ran while one was open for 4% of the time, Pallas kernels for 2%

profile of v2, /device:TPU:8, one launch (start us, length us, event | category | flops | bytes accessed | tf_op | source)
XLA Modules:
  0.0 104.2 jit_solution(12452358399299422978)
XLA Ops:
  6.5 0.0 all-gather.3.cloned.1.call-start
  6.5 1.9 %prepare.1 = (bf16[256,512]{1,0:T(8,128)(2,1)}, bf16[32,48,128]{2,1,0:T(8,128)(2,1)}) custom-call(s32[2,4]{1,0:T(2,128)} %mask_ref.1, bf16[256,512]{1,0:T(8,128)(2,1)} %w_ref.1), custom_call_target="tpu_custom_call" | custom-call | tf_op jit(solution)/shard_map/prepare/pallas_call | solution.py:56
  8.4 0.0 all-gather.3.cloned.1.call-update
  8.4 10.2 %all-to-all-start = ((bf16[32,48,128]{2,1,0:T(8,128)(2,1)}), bf16[32,48,128]{2,1,0:T(8,128)(2,1)S(1)}, u32[]{:S(2)}, u32[]{:S(2)}) async-start(bf16[32,48,128]{2,1,0:T(8,128)(2,1)} %get-tuple-element.11), calls=%async_computation | async-start | bytes 786432 | tf_op jit(solution)/shard_map/all_to_all | solution.py:20
  18.6 14.7 %all-to-all-done.got_ref = bf16[32,48,128]{2,1,0:T(8,128)(2,1)S(1)} async-done(((bf16[32,48,128]{2,1,0:T(8,128)(2,1)}), bf16[32,48,128]{2,1,0:T(8,128)(2,1)S(1)}, u32[]{:S(2)}, u32[]{:S(2)}) %all-to-all-start) | async-done | bytes 393248 | tf_op jit(solution)/shard_map/all_to_all | solution.py:20
  33.3 0.0 copy-start.1
  33.3 0.1 fusion
  33.4 0.1 reshape.39
  33.5 0.1 reduce_window_sum.11
  33.6 0.1 copy.4
  33.7 0.1 copy.3
  33.8 0.2 select_reduce_fusion
  33.9 0.7 copy.6.ids_ref
  34.6 0.0 copy-done.1
  34.6 2.2 %place.1 = (bf16[32,8,16,128]{3,2,1,0:T(8,128)(2,1)}, f32[4,128]{1,0:T(4,128)}) custom-call(s32[1]{0:T(128)} %bitcast.1.own_ref, s32[8,4]{1,0:T(8,128)} %copy.6.ids_ref, bf16[32,48,128]{2,1,0:T(8,128)(2,1)} %copy-done.1), custom_call_target="tpu_custom_call" | custom-call | tf_op jit(solution)/shard_map/place/pallas_call | solution.py:88
  36.8 4.9 %all-to-all-start.1 = ((bf16[32,8,16,128]{3,2,1,0:T(8,128)(2,1)}), bf16[32,8,16,128]{3,2,1,0:T(8,128)(2,1)S(1)}, u32[]{:S(2)}, u32[]{:S(2)}) async-start(bf16[32,8,16,128]{3,2,1,0:T(8,128)(2,1)} %get-tuple-element.14), calls=%async_computation.1 | async-start | bytes 2097152 | tf_op jit(solution)/shard_map/all_to_all | solution.py:20
  41.7 1.9 %collective-permute-start = (f32[1,4,128]{2,1,0:T(4,128)}, f32[1,4,128]{2,1,0:T(4,128)S(1)}, u32[]{:S(2)}, u32[]{:S(2)}) collective-permute-start(f32[1,4,128]{2,1,0:T(4,128)} %bitcast.6), channel_id=1, source_target_pairs={{0,1},{1,0},{2,3},{3,2},{4,5},{5,4},{6,7},{7,6},{8,9},{9,8},{10,11... | collective-permute-start | bytes 6152 | tf_op jit(solution)/shard_map/ppermute | solution.py:135
  43.6 0.7 constant_dynamic-update-slice_fusion.4
  44.3 0.7 collective-permute-done
  44.9 0.7 pad_maximum_fusion.2
  45.6 4.3 %collective-permute-start.1 = (f32[2,4,128]{2,1,0:T(4,128)S(1)}, f32[2,4,128]{2,1,0:T(4,128)S(1)}, u32[]{:S(2)}, u32[]{:S(2)}) collective-permute-start(f32[2,4,128]{2,1,0:T(4,128)S(1)} %pad_maximum_fusion.2), channel_id=1, source_target_pairs={{0,2},{2,0},{4,6},{6,4},{8,10},{10,8},{12,14},{14,12},{1,3},{3,1},... | collective-permute-start | bytes 12296 | tf_op jit(solution)/shard_map/ppermute | solution.py:135
  49.9 1.6 %collective-permute-done.1 = f32[2,4,128]{2,1,0:T(4,128)S(1)} collective-permute-done((f32[2,4,128]{2,1,0:T(4,128)S(1)}, f32[2,4,128]{2,1,0:T(4,128)S(1)}, u32[]{:S(2)}, u32[]{:S(2)}) %collective-permute-start.1) | collective-permute-done | bytes 4128 | tf_op jit(solution)/shard_map/ppermute | solution.py:135
  51.5 0.7 pad_maximum_fusion.1
  52.1 6.1 %collective-permute-start.2 = (f32[4,4,128]{2,1,0:T(4,128)S(1)}, f32[4,4,128]{2,1,0:T(4,128)S(1)}, u32[]{:S(2)}, u32[]{:S(2)}) collective-permute-start(f32[4,4,128]{2,1,0:T(4,128)S(1)} %pad_maximum_fusion.1), channel_id=1, source_target_pairs={{0,4},{2,6},{4,0},{6,2},{8,12},{10,14},{12,8},{14,10},{1,5},{3,7},... | collective-permute-start | bytes 24584 | tf_op jit(solution)/shard_map/ppermute | solution.py:135
  58.2 1.6 %collective-permute-done.2 = f32[4,4,128]{2,1,0:T(4,128)S(1)} collective-permute-done((f32[4,4,128]{2,1,0:T(4,128)S(1)}, f32[4,4,128]{2,1,0:T(4,128)S(1)}, u32[]{:S(2)}, u32[]{:S(2)}) %collective-permute-start.2) | collective-permute-done | bytes 8224 | tf_op jit(solution)/shard_map/ppermute | solution.py:135
  59.8 0.7 pad_maximum_fusion
  60.5 9.3 %collective-permute-start.3 = (f32[8,4,128]{2,1,0:T(4,128)S(1)}, f32[8,4,128]{2,1,0:T(4,128)S(1)}, u32[]{:S(2)}, u32[]{:S(2)}) collective-permute-start(f32[8,4,128]{2,1,0:T(4,128)S(1)} %pad_maximum_fusion), channel_id=1, source_target_pairs={{0,8},{2,10},{4,12},{6,14},{8,0},{10,2},{12,4},{14,6},{1,9},{3,11}... | collective-permute-start | bytes 49160 | tf_op jit(solution)/shard_map/ppermute | solution.py:135
  69.8 1.7 %collective-permute-done.3 = f32[8,4,128]{2,1,0:T(4,128)S(1)} collective-permute-done((f32[8,4,128]{2,1,0:T(4,128)S(1)}, f32[8,4,128]{2,1,0:T(4,128)S(1)}, u32[]{:S(2)}, u32[]{:S(2)}) %collective-permute-start.3) | collective-permute-done | bytes 16416 | tf_op jit(solution)/shard_map/ppermute | solution.py:135
  71.5 0.0 copy-start.2
  71.5 0.0 all-to-all-done.1.right_ref
  71.5 0.0 copy-start
  71.5 0.0 all-gather.3.cloned.1.call-done
  71.6 0.6 copy-done.2
  72.1 0.4 copy-done
  72.5 4.0 %expand.1 = (f32[256,512]{1,0:T(8,128)}, f32[32,1,512]{2,1,0:T(1,128)}) custom-call(s32[1]{0:T(128)} %bitcast.col_ref, s32[8,4]{1,0:T(8,128)} %copy.6.ids_ref, f32[16,4,128]{2,1,0:T(4,128)} %copy-done.2, bf16[16,256,512]{2,1,0:T(8,128)(2,1)} %bitcast.5, bf16[32,8,16,128]{3,2,1,0:T(8,128)(2,1)} %copy-done), custom_call_target="tpu_custom_call" | custom-call | tf_op jit(solution)/shard_map/expand/pallas_call | solution.py:120
  76.5 18.8 %all_to_all.15 = f32[32,1,512]{2,1,0:T(1,128)S(1)} all-to-all(f32[32,1,512]{2,1,0:T(1,128)} %get-tuple-element.16), channel_id=1, replica_groups=mesh['y'=8,'x'=4,'z'=8,'core'=2] {'y','x'}, dimensions={0} | all-to-all | bytes 131072 | tf_op jit(solution)/shard_map/all_to_all | solution.py:20
  95.3 0.1 reduce_sum.19
  95.4 1.9 %broadcast_multiply_fusion = f32[256,512]{1,0:T(8,128)} fusion(f32[256,512]{1,0:T(8,128)} %get-tuple-element.15, f32[512]{0:T(512)S(1)} %broadcast_divide_fusion), kind=kLoop, calls=%fused_computation | loop fusion | flops 131072 | bytes 1050624 | tf_op jit(solution)/shard_map/mul | solution.py:159
  (7 shorter events, 0.1 us)
Async XLA Ops:
  6.5 65.0 %all-gather.3.cloned.1.call-start = ((), (), s32[]{:S(2)}) async-start(), calls=%async_computation.3 | async-start | bytes 4456448 | tf_op jit(solution)/shard_map/all_gather | solution.py:143
  8.4 24.9 %all-to-all-start = ((bf16[32,48,128]{2,1,0:T(8,128)(2,1)}), bf16[32,48,128]{2,1,0:T(8,128)(2,1)S(1)}, u32[]{:S(2)}, u32[]{:S(2)}) async-start(bf16[32,48,128]{2,1,0:T(8,128)(2,1)} %get-tuple-element.11), calls=%async_computation | async-start | bytes 786432 | tf_op jit(solution)/shard_map/all_to_all | solution.py:20
  33.3 1.3 %copy-start.1 = (bf16[32,48,128]{2,1,0:T(8,128)(2,1)}, bf16[32,48,128]{2,1,0:T(8,128)(2,1)S(1)}, u32[]{:S(2)}) copy-start(bf16[32,48,128]{2,1,0:T(8,128)(2,1)S(1)} %all-to-all-done.got_ref) | copy-start | bytes 1179652
  36.8 34.8 %all-to-all-start.1 = ((bf16[32,8,16,128]{3,2,1,0:T(8,128)(2,1)}), bf16[32,8,16,128]{3,2,1,0:T(8,128)(2,1)S(1)}, u32[]{:S(2)}, u32[]{:S(2)}) async-start(bf16[32,8,16,128]{3,2,1,0:T(8,128)(2,1)} %get-tuple-element.14), calls=%async_computation.1 | async-start | bytes 2097152 | tf_op jit(solution)/shard_map/all_to_all | solution.py:20
  41.7 3.3 %collective-permute-start = (f32[1,4,128]{2,1,0:T(4,128)}, f32[1,4,128]{2,1,0:T(4,128)S(1)}, u32[]{:S(2)}, u32[]{:S(2)}) collective-permute-start(f32[1,4,128]{2,1,0:T(4,128)} %bitcast.6), channel_id=1, source_target_pairs={{0,1},{1,0},{2,3},{3,2},{4,5},{5,4},{6,7},{7,6},{8,9},{9,8},{10,11... | collective-permute-start | bytes 6152 | tf_op jit(solution)/shard_map/ppermute | solution.py:135
  45.6 5.9 %collective-permute-start.1 = (f32[2,4,128]{2,1,0:T(4,128)S(1)}, f32[2,4,128]{2,1,0:T(4,128)S(1)}, u32[]{:S(2)}, u32[]{:S(2)}) collective-permute-start(f32[2,4,128]{2,1,0:T(4,128)S(1)} %pad_maximum_fusion.2), channel_id=1, source_target_pairs={{0,2},{2,0},{4,6},{6,4},{8,10},{10,8},{12,14},{14,12},{1,3},{3,1},... | collective-permute-start | bytes 12296 | tf_op jit(solution)/shard_map/ppermute | solution.py:135
  52.1 7.7 %collective-permute-start.2 = (f32[4,4,128]{2,1,0:T(4,128)S(1)}, f32[4,4,128]{2,1,0:T(4,128)S(1)}, u32[]{:S(2)}, u32[]{:S(2)}) collective-permute-start(f32[4,4,128]{2,1,0:T(4,128)S(1)} %pad_maximum_fusion.1), channel_id=1, source_target_pairs={{0,4},{2,6},{4,0},{6,2},{8,12},{10,14},{12,8},{14,10},{1,5},{3,7},... | collective-permute-start | bytes 24584 | tf_op jit(solution)/shard_map/ppermute | solution.py:135
  60.5 11.0 %collective-permute-start.3 = (f32[8,4,128]{2,1,0:T(4,128)S(1)}, f32[8,4,128]{2,1,0:T(4,128)S(1)}, u32[]{:S(2)}, u32[]{:S(2)}) collective-permute-start(f32[8,4,128]{2,1,0:T(4,128)S(1)} %pad_maximum_fusion), channel_id=1, source_target_pairs={{0,8},{2,10},{4,12},{6,14},{8,0},{10,2},{12,4},{14,6},{1,9},{3,11}... | collective-permute-start | bytes 49160 | tf_op jit(solution)/shard_map/ppermute | solution.py:135
  71.5 0.6 copy-start.2
  71.5 1.0 copy-start
Sparse Core Ops, SparseCore 0:
  9.4 49.9 all-gather.2

commit v3 on v2

v3 whole, which is shorter than its diff:
```python
import jax
import jax.numpy as jnp
from jax import lax
from jax.experimental import pallas as pl
from jax.experimental.pallas import tpu as pltpu
from jax.sharding import Mesh, PartitionSpec as P

KEEP = 8
TILE = 128
SLICE = 16
NY, NX, NZ, NC = 8, 4, 8, 2
ROWS = NY * NX
ROW = ("y", "x")
F32, BF16 = jnp.float32, jnp.bfloat16
VMEM = pl.BlockSpec(memory_space=pltpu.VMEM)
SMEM = pl.BlockSpec(memory_space=pltpu.SMEM)


def exchange(blocks, axis):
    return lax.all_to_all(blocks, axis, split_axis=0, concat_axis=0, tiled=True)


def near(x):
    return pltpu.with_memory_space_constraint(x, pltpu.VMEM)


def split3(v):
    parts = []
    for _ in range(3):
        part = v.astype(BF16)
        parts.append(part)
        v = v - part.astype(F32)
    return parts


def prepare_kernel(mask_ref, w_ref, panel_ref, sent_ref):
    lane = lax.broadcasted_iota(jnp.int32, (1, TILE), 1)
    packed = jnp.zeros((1, TILE), F32)
    sums, masks = [], []
    for c in range(4):
        cols = pl.ds(c * TILE, TILE)
        total = jnp.zeros((1, TILE), F32)
        for t in range(2):
            on = mask_ref[t, c].astype(F32)
            masks.append(jnp.full((1, TILE), on, F32))
            packed = jnp.where(lane == t * 4 + c, on, packed)
            tile = w_ref[pl.ds(t * TILE, TILE), cols].astype(F32) * on
            total = total + jnp.sum(tile, axis=0, keepdims=True)
            tile = tile.astype(BF16)
            panel_ref[pl.ds(t * TILE, TILE), cols] = tile
            for e in range(8):
                sent_ref[8 * c + e, pl.ds(t * SLICE, SLICE)] = tile[e * SLICE : (e + 1) * SLICE]
        sums.append(split3(total))
    rows = [sums[c][p].astype(F32) for p in range(3) for c in range(4)]
    for c in range(4):
        extra = jnp.concatenate([*rows, packed, packed, *masks[2 * c : 2 * c + 2]], axis=0).astype(BF16)
        for e in range(8):
            sent_ref[8 * c + e, pl.ds(2 * SLICE, SLICE)] = extra


def prepare(mask, weights):
    return pl.pallas_call(
        prepare_kernel,
        out_shape=(
            jax.ShapeDtypeStruct((2 * TILE, 4 * TILE), BF16),
            pltpu.VMEM((ROWS, 3 * SLICE, TILE), BF16),
        ),
        in_specs=[SMEM, VMEM],
        out_specs=(VMEM,) * 2,
        name="prepare",
    )(mask, weights)


def place_kernel(own_ref, got_ref, placed_ref, degree_ref, slot_ref):
    total = jnp.zeros((SLICE, TILE), F32)
    masks = []
    for r in range(ROWS):
        extra = got_ref[r, pl.ds(2 * SLICE, SLICE)].astype(F32)
        total = total + extra
        masks.append(extra[14:16])
    degree = total[0:4] + (total[4:8] + total[8:12])
    degree_ref[...] = degree
    there = jnp.concatenate(masks, axis=0)
    above = lax.broadcasted_iota(jnp.int32, (64, 64), 0) > lax.broadcasted_iota(jnp.int32, (64, 64), 1)
    rank = jnp.dot(above.astype(BF16), there.astype(BF16), preferred_element_type=F32)
    slot_ref[...] = jnp.where(there > 0, rank, -1.0)
    own = own_ref[0]
    mine = jnp.zeros((1, TILE), F32)
    for c in range(4):
        mine = jnp.where(own == c, degree[c : c + 1], mine)
    kept = [jnp.zeros((SLICE, TILE), F32) for _ in range(KEEP)]
    for k in range(64):
        tile = got_ref[k // 2, pl.ds((k % 2) * SLICE, SLICE)].astype(F32)
        slot = jnp.broadcast_to(slot_ref[pl.ds(k, 1)], (SLICE, TILE))
        for s in range(KEEP):
            kept[s] = jnp.where(slot == s, tile, kept[s])
    for s in range(KEEP):
        tile = (kept[s] / mine).astype(BF16)
        for r in range(ROWS):
            placed_ref[r, s] = tile


def place(own, got):
    return pl.pallas_call(
        place_kernel,
        out_shape=(
            pltpu.VMEM((ROWS, KEEP, SLICE, TILE), BF16),
            pltpu.VMEM((4, TILE), F32),
        ),
        in_specs=[SMEM, VMEM],
        out_specs=(VMEM, VMEM),
        scratch_shapes=[pltpu.VMEM((64, TILE), F32)],
        name="place",
    )(own, near(got))


def expand_kernel(ids_ref, degree_ref, panel_ref, right_ref, out_ref, mass_ref):
    for c in range(4):
        cols = pl.ds(c * TILE, TILE)
        total = jnp.zeros((2 * TILE, TILE), F32)
        for pair in range(KEEP // 2):
            lefts, rights = [], []
            for s in (2 * pair, 2 * pair + 1):
                k = ids_ref[s, c]
                inside = pl.ds(pl.multiple_of((k % 4) * TILE, TILE), TILE)
                inverse = 1.0 / degree_ref[k // 4, pl.ds(k % 4, 1), :]
                lefts.append((panel_ref[k // 4, :, inside].astype(F32) * inverse).astype(BF16))
                rights.append(right_ref[pl.ds(8 * c, 8), s].reshape(TILE, TILE))
            total = total + jnp.dot(
                jnp.concatenate(lefts, axis=1),
                jnp.concatenate(rights, axis=0),
                preferred_element_type=F32,
            )
        total = total * total
        out_ref[:, cols] = total
        part = jnp.sum(total, axis=0, keepdims=True)
        for r in range(ROWS):
            mass_ref[r, :, cols] = part


def expand(ids, degree, panel, right):
    return pl.pallas_call(
        expand_kernel,
        out_shape=(
            pltpu.VMEM((2 * TILE, 4 * TILE), F32),
            pltpu.VMEM((ROWS, 1, 4 * TILE), F32),
        ),
        in_specs=[SMEM] + [VMEM] * 3,
        out_specs=(VMEM, VMEM),
        name="expand",
    )(ids, degree, panel, near(right))


def scale_kernel(inflated_ref, mass_ref, flow_ref):
    mass = jnp.sum(mass_ref[...], axis=0)
    flow_ref[...] = inflated_ref[...] * (64.0 * TILE / mass)


def scale(inflated, mass):
    return pl.pallas_call(
        scale_kernel,
        out_shape=jax.ShapeDtypeStruct((2 * TILE, 4 * TILE), F32),
        in_specs=[VMEM, VMEM],
        out_specs=VMEM,
        name="scale",
    )(near(inflated), near(mass))


def on_device(weights, tile_mask):
    masked, sent = prepare(tile_mask, weights)
    panel = lax.all_gather(masked, ("z", "core"))
    got = exchange(sent, ROW)
    own = (lax.axis_index("y") // 2).reshape(1)
    placed, degree = place(own, got)
    right = exchange(placed, ROW)
    degree = lax.all_gather(degree, ("z", "core"))
    there = (got[:, 44, :8].reshape(64, 4) > 0).astype(jnp.int32)
    rank = jnp.cumsum(there, axis=0) - there
    tile_ids = lax.broadcasted_iota(jnp.int32, (KEEP, 64, 4), 1)
    ranks = lax.broadcasted_iota(jnp.int32, (KEEP, 64, 4), 0)
    chosen = (there == 1)[None] & (rank[None] == ranks)
    ids = jnp.sum(jnp.where(chosen, tile_ids, 0), axis=1)
    inflated, mass = expand(ids, degree, panel, right)
    return scale(inflated, exchange(mass, ROW))


def solution(mesh):
    split = Mesh(mesh.devices.reshape(NY, NX, NZ, NC), ("y", "x", "z", "core"))
    placed = P(ROW, ("z", "core"))
    return jax.shard_map(
        on_device, mesh=split, in_specs=(placed, placed), out_specs=placed, check_vma=False
    )
```

time: 105 us -> 95.9 us (0.913)
  the two profiles are of different devices: /device:TPU:8 before, /device:TPU:1 now
where the time goes in v3:
time: 95.9 us; the launch traced here: 95.6 us
  blocking collectives  44.3 us (46%)
  starting transfers between devices  15.5 us (16%)
  waiting for transfers between devices  13.8 us (14%)
  between operations  13.4 us (14%)
  Pallas kernels  7.2 us (8%)
    all_gather x1, blocking collectives, on_device(): degree = lax.all_gather(degree, ('z', 'core'))  26.1 us
    all_to_all x1, blocking collectives, exchange(): return lax.all_to_all(blocks, axis, split_axis=0, concat_axis=0, tiled=True)  18.2 us
    all_to_all x2, starting transfers between devices, exchange(): return lax.all_to_all(blocks, axis, split_axis=0, concat_axis=0, tiled=True)  15.5 us
    all_to_all x2, waiting for transfers between devices, exchange(): return lax.all_to_all(blocks, axis, split_axis=0, concat_axis=0, tiled=True)  13.8 us
    pallas_call x1, Pallas kernels, expand(): pl.pallas_call(expand_kernel, out_shape=(pltpu.VMEM((2 * TILE, 4 * TILE),...  2.97 us
  transfers between devices with their start and end apart: 3, of which 1 were waited for; matrix products, arithmetic and copies ran while one was open for 1% of the time, Pallas kernels for 2%

profile of v3, /device:TPU:1, one launch (start us, length us, event | category | flops | bytes accessed | tf_op | source)
XLA Modules:
  0.0 95.6 jit_solution(12564783056989803521)
XLA Ops:
  6.5 0.0 all-gather.5.cloned.1.call-start
  6.5 1.9 %prepare.1 = (bf16[256,512]{1,0:T(8,128)(2,1)}, bf16[32,48,128]{2,1,0:T(8,128)(2,1)}) custom-call(s32[2,4]{1,0:T(2,128)} %mask_ref.1, bf16[256,512]{1,0:T(8,128)(2,1)} %w_ref.1), custom_call_target="tpu_custom_call" | custom-call | tf_op jit(solution)/shard_map/prepare/pallas_call | solution.py:62
  8.4 0.0 all-gather.5.cloned.1.call-update
  8.4 10.5 %all-to-all-start = ((bf16[32,48,128]{2,1,0:T(8,128)(2,1)}), bf16[32,48,128]{2,1,0:T(8,128)(2,1)S(1)}, u32[]{:S(2)}, u32[]{:S(2)}) async-start(bf16[32,48,128]{2,1,0:T(8,128)(2,1)} %get-tuple-element.11), calls=%async_computation | async-start | bytes 786432 | tf_op jit(solution)/shard_map/all_to_all | solution.py:20
  19.0 13.8 %all-to-all-done.got_ref = bf16[32,48,128]{2,1,0:T(8,128)(2,1)S(1)} async-done(((bf16[32,48,128]{2,1,0:T(8,128)(2,1)}), bf16[32,48,128]{2,1,0:T(8,128)(2,1)S(1)}, u32[]{:S(2)}, u32[]{:S(2)}) %all-to-all-start) | async-done | bytes 393248 | tf_op jit(solution)/shard_map/all_to_all | solution.py:20
  32.8 1.5 %place.1 = (bf16[32,8,16,128]{3,2,1,0:T(8,128)(2,1)}, f32[4,128]{1,0:T(4,128)S(1)}) custom-call(s32[1]{0:T(128)} %bitcast.own_ref, bf16[32,48,128]{2,1,0:T(8,128)(2,1)S(1)} %all-to-all-done.got_ref), custom_call_target="tpu_custom_call" | custom-call | tf_op jit(solution)/shard_map/place/pallas_call | solution.py:104
  34.2 5.0 %all-to-all-start.1 = ((bf16[32,8,16,128]{3,2,1,0:T(8,128)(2,1)}), bf16[32,8,16,128]{3,2,1,0:T(8,128)(2,1)S(1)}, u32[]{:S(2)}, u32[]{:S(2)}) async-start(bf16[32,8,16,128]{3,2,1,0:T(8,128)(2,1)} %get-tuple-element.14), calls=%async_computation.1 | async-start | bytes 2097152 | tf_op jit(solution)/shard_map/all_to_all | solution.py:20
  39.3 0.1 fusion
  39.3 0.1 reshape.30
  39.4 0.1 reduce_window_sum.11
  39.5 0.1 copy.4
  39.6 0.1 copy.3
  39.7 0.2 select_reduce_fusion
  39.9 0.7 copy.5.ids_ref
  40.5 26.1 %all-gather.2.degree_ref = f32[16,4,128]{2,1,0:T(4,128)} all-gather(f32[1,4,128]{2,1,0:T(4,128)S(1)} %bitcast.3), channel_id=2, replica_groups=mesh['y'=8,'x'=4,'z'=8,'core'=2] {'z','core'}, dimensions={0}, use_global_device_ids=true | all-gather | bytes 34816 | tf_op jit(solution)/shard_map/all_gather | solution.py:176
  66.7 0.0 all-to-all-done.1.right_ref
  66.7 0.0 all-gather.5.cloned.1.call-done
  66.7 3.0 %expand.1 = (f32[256,512]{1,0:T(8,128)S(1)}, f32[32,1,512]{2,1,0:T(1,128)S(1)}) custom-call(s32[8,4]{1,0:T(8,128)} %copy.5.ids_ref, f32[16,4,128]{2,1,0:T(4,128)} %all-gather.2.degree_ref, bf16[16,256,512]{2,1,0:T(8,128)(2,1)} %bitcast.4, bf16[32,8,16,128]{3,2,1,0:T(8,128)(2,1)S(1)} %all-to-all-done.1.right_ref), custom_call_target="tpu_custom_call" | custom-call | tf_op jit(solution)/shard_map/expand/pallas_call | solution.py:142
  69.7 18.2 %all_to_all.15.mass_ref = f32[32,1,512]{2,1,0:T(1,128)S(1)} all-to-all(f32[32,1,512]{2,1,0:T(1,128)S(1)} %get-tuple-element.16), channel_id=1, replica_groups=mesh['y'=8,'x'=4,'z'=8,'core'=2] {'y','x'}, dimensions={0} | all-to-all | bytes 131072 | tf_op jit(solution)/shard_map/all_to_all | solution.py:20
  87.8 0.9 scale.1
  (2 shorter events, 0.0 us)
Async XLA Ops:
  6.5 60.1 %all-gather.5.cloned.1.call-start = ((), (), s32[]{:S(2)}) async-start(), calls=%async_computation.3 | async-start | bytes 4456448 | tf_op jit(solution)/shard_map/all_gather | solution.py:171
  8.4 24.3 %all-to-all-start = ((bf16[32,48,128]{2,1,0:T(8,128)(2,1)}), bf16[32,48,128]{2,1,0:T(8,128)(2,1)S(1)}, u32[]{:S(2)}, u32[]{:S(2)}) async-start(bf16[32,48,128]{2,1,0:T(8,128)(2,1)} %get-tuple-element.11), calls=%async_computation | async-start | bytes 786432 | tf_op jit(solution)/shard_map/all_to_all | solution.py:20
  34.2 32.4 %all-to-all-start.1 = ((bf16[32,8,16,128]{3,2,1,0:T(8,128)(2,1)}), bf16[32,8,16,128]{3,2,1,0:T(8,128)(2,1)S(1)}, u32[]{:S(2)}, u32[]{:S(2)}) async-start(bf16[32,8,16,128]{3,2,1,0:T(8,128)(2,1)} %get-tuple-element.14), calls=%async_computation.1 | async-start | bytes 2097152 | tf_op jit(solution)/shard_map/all_to_all | solution.py:20
Sparse Core Ops, SparseCore 0:
  9.4 51.0 all-gather.4

commit v4 on v3

--- a/solution.py
+++ b/solution.py
@@ -11,7 +11,8 @@
 NY, NX, NZ, NC = 8, 4, 8, 2
 ROWS = NY * NX
 ROW = ("y", "x")
-F32, BF16 = jnp.float32, jnp.bfloat16
+F32, BF16, I16 = jnp.float32, jnp.bfloat16, jnp.int16
+UNIT = 16384.0
 VMEM = pl.BlockSpec(memory_space=pltpu.VMEM)
 SMEM = pl.BlockSpec(memory_space=pltpu.SMEM)
 
@@ -46,8 +47,8 @@
             packed = jnp.where(lane == t * 4 + c, on, packed)
             tile = w_ref[pl.ds(t * TILE, TILE), cols].astype(F32) * on
             total = total + jnp.sum(tile, axis=0, keepdims=True)
+            panel_ref[pl.ds(t * TILE, TILE), cols] = (tile * UNIT).astype(jnp.int32).astype(I16)
             tile = tile.astype(BF16)
-            panel_ref[pl.ds(t * TILE, TILE), cols] = tile
             for e in range(8):
                 sent_ref[8 * c + e, pl.ds(t * SLICE, SLICE)] = tile[e * SLICE : (e + 1) * SLICE]
         sums.append(split3(total))
@@ -62,7 +63,7 @@
     return pl.pallas_call(
         prepare_kernel,
         out_shape=(
-            jax.ShapeDtypeStruct((2 * TILE, 4 * TILE), BF16),
+            pltpu.VMEM((2 * TILE, 4 * TILE), I16),
             pltpu.VMEM((ROWS, 3 * SLICE, TILE), BF16),
         ),
         in_specs=[SMEM, VMEM],
@@ -71,7 +72,7 @@
     )(mask, weights)
 
 
-def place_kernel(own_ref, got_ref, placed_ref, degree_ref, slot_ref):
+def place_kernel(own_ref, got_ref, panel_ref, placed_ref, full_ref, slot_ref):
     total = jnp.zeros((SLICE, TILE), F32)
     masks = []
     for r in range(ROWS):
@@ -79,7 +80,12 @@
         total = total + extra
         masks.append(extra[14:16])
     degree = total[0:4] + (total[4:8] + total[8:12])
-    degree_ref[...] = degree
+    full_ref[pl.ds(0, 2 * TILE)] = panel_ref[...]
+    for c in range(4):
+        high = jnp.floor(degree[c : c + 1] * 16.0)
+        low = (degree[c : c + 1] * 16.0 - high) * UNIT
+        rows = jnp.concatenate([high, low, jnp.zeros((6, TILE), F32)], axis=0)
+        full_ref[pl.ds(2 * TILE, 8), pl.ds(c * TILE, TILE)] = rows.astype(jnp.int32).astype(I16)
     there = jnp.concatenate(masks, axis=0)
     above = lax.broadcasted_iota(jnp.int32, (64, 64), 0) > lax.broadcasted_iota(jnp.int32, (64, 64), 1)
     rank = jnp.dot(above.astype(BF16), there.astype(BF16), preferred_element_type=F32)
@@ -100,21 +106,21 @@
             placed_ref[r, s] = tile
 
 
-def place(own, got):
+def place(own, got, panel):
     return pl.pallas_call(
         place_kernel,
         out_shape=(
             pltpu.VMEM((ROWS, KEEP, SLICE, TILE), BF16),
-            pltpu.VMEM((4, TILE), F32),
+            pltpu.VMEM((2 * TILE + 8, 4 * TILE), I16),
         ),
-        in_specs=[SMEM, VMEM],
+        in_specs=[SMEM, VMEM, VMEM],
         out_specs=(VMEM, VMEM),
         scratch_shapes=[pltpu.VMEM((64, TILE), F32)],
         name="place",
-    )(own, near(got))
-
-
-def expand_kernel(ids_ref, degree_ref, panel_ref, right_ref, out_ref, mass_ref):
+    )(own, near(got), near(panel))
+
+
+def expand_kernel(ids_ref, panel_ref, right_ref, out_ref, mass_ref):
     for c in range(4):
         cols = pl.ds(c * TILE, TILE)
         total = jnp.zeros((2 * TILE, TILE), F32)
@@ -123,8 +129,10 @@
             for s in (2 * pair, 2 * pair + 1):
                 k = ids_ref[s, c]
                 inside = pl.ds(pl.multiple_of((k % 4) * TILE, TILE), TILE)
-                inverse = 1.0 / degree_ref[k // 4, pl.ds(k % 4, 1), :]
-                lefts.append((panel_ref[k // 4, :, inside].astype(F32) * inverse).astype(BF16))
+                parts = panel_ref[k // 4, pl.ds(2 * TILE, 8), inside].astype(jnp.int32).astype(F32)
+                inverse = (16.0 / UNIT) / (parts[0:1] + parts[1:2] / UNIT)
+                left = panel_ref[k // 4, pl.ds(0, 2 * TILE), inside].astype(jnp.int32).astype(F32)
+                lefts.append((left * inverse).astype(BF16))
                 rights.append(right_ref[pl.ds(8 * c, 8), s].reshape(TILE, TILE))
             total = total + jnp.dot(
                 jnp.concatenate(lefts, axis=1),
@@ -138,17 +146,18 @@
             mass_ref[r, :, cols] = part
 
 
-def expand(ids, degree, panel, right):
+def expand(ids, panel, right):
     return pl.pallas_call(
         expand_kernel,
         out_shape=(
             pltpu.VMEM((2 * TILE, 4 * TILE), F32),
             pltpu.VMEM((ROWS, 1, 4 * TILE), F32),
         ),
-        in_specs=[SMEM] + [VMEM] * 3,
+        in_specs=[SMEM] + [VMEM] * 2,
         out_specs=(VMEM, VMEM),
+        compiler_params=pltpu.CompilerParams(vmem_limit_bytes=24 * 2**20),
         name="expand",
-    )(ids, degree, panel, near(right))
+    )(ids, near(panel), near(right))
 
 
 def scale_kernel(inflated_ref, mass_ref, flow_ref):
@@ -168,19 +177,18 @@
 
 def on_device(weights, tile_mask):
     masked, sent = prepare(tile_mask, weights)
-    panel = lax.all_gather(masked, ("z", "core"))
     got = exchange(sent, ROW)
     own = (lax.axis_index("y") // 2).reshape(1)
-    placed, degree = place(own, got)
+    placed, full = place(own, got, masked)
     right = exchange(placed, ROW)
-    degree = lax.all_gather(degree, ("z", "core"))
+    panel = lax.all_gather(full, ("z", "core"))
     there = (got[:, 44, :8].reshape(64, 4) > 0).astype(jnp.int32)
     rank = jnp.cumsum(there, axis=0) - there
     tile_ids = lax.broadcasted_iota(jnp.int32, (KEEP, 64, 4), 1)
     ranks = lax.broadcasted_iota(jnp.int32, (KEEP, 64, 4), 0)
     chosen = (there == 1)[None] & (rank[None] == ranks)
     ids = jnp.sum(jnp.where(chosen, tile_ids, 0), axis=1)
-    inflated, mass = expand(ids, degree, panel, right)
+    inflated, mass = expand(ids, panel, right)
     return scale(inflated, exchange(mass, ROW))
 
 

time: 95.9 us -> 97.9 us (1.021)
  blocking collectives: 44.3 us -> 59.5 us
  between operations: 13.4 us -> 0.05 us
  local copies, waits for them, and re-layouts: 0.91 us -> 2.54 us
  Pallas kernels: 7.2 us -> 5.68 us
    all_gather x1, blocking collectives: 26.1 us -> 41.4 us  [on_device(): panel = lax.all_gather(full, ('z', 'core'))]
    unnamed x0 -> x2, local copies, waits for them, and re-layouts: none -> 2.23 us
    pallas_call x1, Pallas kernels: 2.97 us -> 1.49 us  [expand(): pl.pallas_call(expand_kernel, out_shape=(pltpu.VMEM((2 * TILE, 4 * TILE),...]
  transfers between devices with their start and end apart: 3 -> 2, of which waited for: 1 -> 1; matrix products, arithmetic and copies ran while one was open for 1% -> 0% of each run, Pallas kernels for 2% -> 0%
where the time goes in v4:
time: 97.9 us; the launch traced here: 97.5 us
  blocking collectives  59.5 us (61%)
  starting transfers between devices  15.5 us (16%)
  waiting for transfers between devices  13.8 us (14%)
  Pallas kernels  5.68 us (6%)
  local copies, waits for them, and re-layouts  2.54 us (3%)
    all_gather x1, blocking collectives, on_device(): panel = lax.all_gather(full, ('z', 'core'))  41.4 us
    all_to_all x1, blocking collectives, exchange(): return lax.all_to_all(blocks, axis, split_axis=0, concat_axis=0, tiled=True)  18.1 us
    all_to_all x2, starting transfers between devices, exchange(): return lax.all_to_all(blocks, axis, split_axis=0, concat_axis=0, tiled=True)  15.5 us
    all_to_all x2, waiting for transfers between devices, exchange(): return lax.all_to_all(blocks, axis, split_axis=0, concat_axis=0, tiled=True)  13.8 us
    unnamed x2, local copies, waits for them, and re-layouts  2.23 us
  transfers between devices with their start and end apart: 2, of which 1 were waited for; matrix products, arithmetic and copies ran while one was open for 0% of the time, Pallas kernels for 0%

profile of v4, /device:TPU:1, one launch (start us, length us, event | category | flops | bytes accessed | tf_op | source)
XLA Modules:
  0.0 97.5 jit_solution(11047401941661387782)
XLA Ops:
  0.0 1.8 %prepare.1 = (s16[256,512]{1,0:T(8,128)(2,1)S(1)}, bf16[32,48,128]{2,1,0:T(8,128)(2,1)}) custom-call(s32[2,4]{1,0:T(2,128)} %mask_ref.1, bf16[256,512]{1,0:T(8,128)(2,1)} %w_ref.1), custom_call_target="tpu_custom_call" | custom-call | tf_op jit(solution)/shard_map/prepare/pallas_call | solution.py:63
  1.8 10.5 %all-to-all-start = ((bf16[32,48,128]{2,1,0:T(8,128)(2,1)}), bf16[32,48,128]{2,1,0:T(8,128)(2,1)S(1)}, u32[]{:S(2)}, u32[]{:S(2)}) async-start(bf16[32,48,128]{2,1,0:T(8,128)(2,1)} %get-tuple-element.11), calls=%async_computation | async-start | bytes 786432 | tf_op jit(solution)/shard_map/all_to_all | solution.py:21
  12.3 13.8 %all-to-all-done.got_ref = bf16[32,48,128]{2,1,0:T(8,128)(2,1)S(1)} async-done(((bf16[32,48,128]{2,1,0:T(8,128)(2,1)}), bf16[32,48,128]{2,1,0:T(8,128)(2,1)S(1)}, u32[]{:S(2)}, u32[]{:S(2)}) %all-to-all-start) | async-done | bytes 393248 | tf_op jit(solution)/shard_map/all_to_all | solution.py:21
  26.1 0.1 fusion
  26.2 0.1 reshape.30
  26.3 0.1 reduce_window_sum.11
  26.4 0.1 copy.3
  26.5 0.1 copy.4
  26.5 1.5 %place.1 = (bf16[32,8,16,128]{3,2,1,0:T(8,128)(2,1)}, s16[264,512]{1,0:T(8,128)(2,1)S(1)}) custom-call(s32[1]{0:T(128)} %bitcast.own_ref, bf16[32,48,128]{2,1,0:T(8,128)(2,1)S(1)} %all-to-all-done.got_ref, s16[256,512]{1,0:T(8,128)(2,1)S(1)} %get-tuple-element.12.panel_ref), custom_call_target="tpu_custom_call" | custom-call | tf_op jit(solution)/shard_map/place/pallas_call | solution.py:110
  28.0 5.0 %all-to-all-start.1 = ((bf16[32,8,16,128]{3,2,1,0:T(8,128)(2,1)}), bf16[32,8,16,128]{3,2,1,0:T(8,128)(2,1)S(1)}, u32[]{:S(2)}, u32[]{:S(2)}) async-start(bf16[32,8,16,128]{3,2,1,0:T(8,128)(2,1)} %get-tuple-element.14), calls=%async_computation.1 | async-start | bytes 2097152 | tf_op jit(solution)/shard_map/all_to_all | solution.py:21
  33.1 0.1 select_reduce_fusion
  33.2 0.1 copy.5.ids_ref
  33.3 41.4 %all-gather.2 = s16[4224,512]{1,0:T(8,128)(2,1)} all-gather(s16[264,512]{1,0:T(8,128)(2,1)S(1)} %get-tuple-element.13), channel_id=2, replica_groups=mesh['y'=8,'x'=4,'z'=8,'core'=2] {'z','core'}, dimensions={0}, use_global_device_ids=true | all-gather | bytes 4595712 | tf_op jit(solution)/shard_map/all_gather | solution.py:184
  74.7 0.0 all-to-all-done.1.right_ref
  74.7 0.0 copy-start
  74.7 2.2 %copy-done = s16[4224,512]{1,0:T(8,128)(2,1)S(1)} copy-done((s16[4224,512]{1,0:T(8,128)(2,1)S(1)}, s16[4224,512]{1,0:T(8,128)(2,1)}, u32[]{:S(2)}) %copy-start) | copy-done | bytes 4325400
  77.0 1.5 %expand.1 = (f32[256,512]{1,0:T(8,128)S(1)}, f32[32,1,512]{2,1,0:T(1,128)S(1)}) custom-call(s32[8,4]{1,0:T(8,128)S(1)} %copy.5.ids_ref, s16[16,264,512]{2,1,0:T(8,128)(2,1)S(1)} %bitcast.2, bf16[32,8,16,128]{3,2,1,0:T(8,128)(2,1)S(1)} %all-to-all-done.1.right_ref), custom_call_target="tpu_custom_call" | custom-call | tf_op jit(solution)/shard_map/expand/pallas_call | solution.py:150
  78.5 18.1 %all_to_all.15.mass_ref = f32[32,1,512]{2,1,0:T(1,128)S(1)} all-to-all(f32[32,1,512]{2,1,0:T(1,128)S(1)} %get-tuple-element.16), channel_id=1, replica_groups=mesh['y'=8,'x'=4,'z'=8,'core'=2] {'y','x'}, dimensions={0} | all-to-all | bytes 131072 | tf_op jit(solution)/shard_map/all_to_all | solution.py:21
  96.6 0.9 scale.1
  (2 shorter events, 0.0 us)
Async XLA Ops:
  1.8 24.3 %all-to-all-start = ((bf16[32,48,128]{2,1,0:T(8,128)(2,1)}), bf16[32,48,128]{2,1,0:T(8,128)(2,1)S(1)}, u32[]{:S(2)}, u32[]{:S(2)}) async-start(bf16[32,48,128]{2,1,0:T(8,128)(2,1)} %get-tuple-element.11), calls=%async_computation | async-start | bytes 786432 | tf_op jit(solution)/shard_map/all_to_all | solution.py:21
  28.0 46.7 %all-to-all-start.1 = ((bf16[32,8,16,128]{3,2,1,0:T(8,128)(2,1)}), bf16[32,8,16,128]{3,2,1,0:T(8,128)(2,1)S(1)}, u32[]{:S(2)}, u32[]{:S(2)}) async-start(bf16[32,8,16,128]{3,2,1,0:T(8,128)(2,1)} %get-tuple-element.14), calls=%async_computation.1 | async-start | bytes 2097152 | tf_op jit(solution)/shard_map/all_to_all | solution.py:21
  74.7 2.2 %copy-start = (s16[4224,512]{1,0:T(8,128)(2,1)S(1)}, s16[4224,512]{1,0:T(8,128)(2,1)}, u32[]{:S(2)}) copy-start(s16[4224,512]{1,0:T(8,128)(2,1)} %all-gather.2) | copy-start | bytes 12976132

commit v5 on v4

--- a/solution.py
+++ b/solution.py
@@ -1,3 +1,5 @@
+import functools
+
 import jax
 import jax.numpy as jnp
 from jax import lax
@@ -13,6 +15,12 @@
 ROW = ("y", "x")
 F32, BF16, I16 = jnp.float32, jnp.bfloat16, jnp.int16
 UNIT = 16384.0
+SLOTS = 9
+HALF = TILE // 2
+DEGREE = SLOTS * HALF
+META = DEGREE + 8
+PACKED = META + 8
+COL = ("z", "core")
 VMEM = pl.BlockSpec(memory_space=pltpu.VMEM)
 SMEM = pl.BlockSpec(memory_space=pltpu.SMEM)
 
@@ -51,6 +59,8 @@
             tile = tile.astype(BF16)
             for e in range(8):
                 sent_ref[8 * c + e, pl.ds(t * SLICE, SLICE)] = tile[e * SLICE : (e + 1) * SLICE]
+        rows = jnp.concatenate([*masks[2 * c : 2 * c + 2], jnp.zeros((6, TILE), F32)], axis=0)
+        panel_ref[pl.ds(2 * TILE, 8), cols] = rows.astype(jnp.int32).astype(I16)
         sums.append(split3(total))
     rows = [sums[c][p].astype(F32) for p in range(3) for c in range(4)]
     for c in range(4):
@@ -63,7 +73,7 @@
     return pl.pallas_call(
         prepare_kernel,
         out_shape=(
-            pltpu.VMEM((2 * TILE, 4 * TILE), I16),
+            pltpu.VMEM((2 * TILE + 8, 4 * TILE), I16),
             pltpu.VMEM((ROWS, 3 * SLICE, TILE), BF16),
         ),
         in_specs=[SMEM, VMEM],
@@ -72,20 +82,65 @@
     )(mask, weights)
 
 
-def place_kernel(own_ref, got_ref, panel_ref, placed_ref, full_ref, slot_ref):
+def pack_kernel(core_ref, panel_ref, other_ref, packed_ref):
+    core = core_ref[0]
+    lane = lax.broadcasted_iota(jnp.int32, (1, TILE), 1)
+
+    def both(rows, q):
+        cols = pl.ds((q % 4) * TILE, TILE)
+        mine, other = panel_ref[rows, cols].astype(jnp.int32), other_ref[rows, cols].astype(jnp.int32)
+        return jnp.where(core == q // 4, mine, other)
+
+    count = jnp.zeros((1, TILE), jnp.int32)
+    meta = jnp.zeros((1, TILE), jnp.int32)
+    slots = []
+    for t in range(2):
+        for q in range(8):
+            on = both(pl.ds(2 * TILE, 8), q)[t : t + 1]
+            slot = jnp.where(on > 0, count, -1)
+            count = count + on
+            slots.append(slot)
+            meta = jnp.where(lane == 8 * t + q, slot, meta)
+    for s in range(SLOTS):
+        kept = jnp.zeros((HALF, TILE), jnp.int32)
+        for t in range(2):
+            rows = pl.ds(pl.multiple_of(t * TILE + core * HALF, HALF), HALF)
+            for q in range(8):
+                kept = jnp.where(slots[8 * t + q] == s, both(rows, q), kept)
+        packed_ref[pl.ds(s * HALF, HALF)] = kept.astype(I16)
+    rows = jnp.concatenate([jnp.zeros((8, TILE), jnp.int32), meta, jnp.zeros((7, TILE), jnp.int32)], axis=0)
+    packed_ref[pl.ds(DEGREE, 16)] = rows.astype(I16)
+
+
+def pack(core, panel, other):
+    return pl.pallas_call(
+        pack_kernel,
+        out_shape=pltpu.VMEM((PACKED, TILE), I16),
+        in_specs=[SMEM, VMEM, VMEM],
+        out_specs=VMEM,
+        name="pack",
+    )(core, near(panel), near(other))
+
+
+def place_kernel(own_ref, got_ref, packed_ref, placed_ref, full_ref, slot_ref):
     total = jnp.zeros((SLICE, TILE), F32)
-    masks = []
+    masks, tiles = [], []
     for r in range(ROWS):
         extra = got_ref[r, pl.ds(2 * SLICE, SLICE)].astype(F32)
         total = total + extra
+        tiles.append(extra[12:13])
         masks.append(extra[14:16])
     degree = total[0:4] + (total[4:8] + total[8:12])
-    full_ref[pl.ds(0, 2 * TILE)] = panel_ref[...]
-    for c in range(4):
-        high = jnp.floor(degree[c : c + 1] * 16.0)
-        low = (degree[c : c + 1] * 16.0 - high) * UNIT
-        rows = jnp.concatenate([high, low, jnp.zeros((6, TILE), F32)], axis=0)
-        full_ref[pl.ds(2 * TILE, 8), pl.ds(c * TILE, TILE)] = rows.astype(jnp.int32).astype(I16)
+    high = jnp.floor(degree * 16.0)
+    low = (degree * 16.0 - high) * UNIT
+    tiles = jnp.concatenate([*tiles, jnp.zeros((TILE - ROWS, TILE), F32)], axis=0).astype(BF16)
+    counts = lax.dot_general(
+        jnp.ones((8, TILE), BF16), tiles, (((1,), (1,)), ((), ())), preferred_element_type=F32
+    )
+    meta = packed_ref[pl.ds(META, 8)].astype(jnp.int32).astype(F32)
+    rows = jnp.concatenate([high, low, meta[0:1], counts[0:7]], axis=0)
+    full_ref[pl.ds(0, DEGREE)] = packed_ref[pl.ds(0, DEGREE)]
+    full_ref[pl.ds(DEGREE, 16)] = rows.astype(jnp.int32).astype(I16)
     there = jnp.concatenate(masks, axis=0)
     above = lax.broadcasted_iota(jnp.int32, (64, 64), 0) > lax.broadcasted_iota(jnp.int32, (64, 64), 1)
     rank = jnp.dot(above.astype(BF16), there.astype(BF16), preferred_element_type=F32)
@@ -106,21 +161,26 @@
             placed_ref[r, s] = tile
 
 
-def place(own, got, panel):
+def place(own, got, packed):
     return pl.pallas_call(
         place_kernel,
         out_shape=(
             pltpu.VMEM((ROWS, KEEP, SLICE, TILE), BF16),
-            pltpu.VMEM((2 * TILE + 8, 4 * TILE), I16),
+            pltpu.VMEM((PACKED, TILE), I16),
         ),
         in_specs=[SMEM, VMEM, VMEM],
         out_specs=(VMEM, VMEM),
         scratch_shapes=[pltpu.VMEM((64, TILE), F32)],
         name="place",
-    )(own, near(got), near(panel))
-
-
-def expand_kernel(ids_ref, panel_ref, right_ref, out_ref, mass_ref):
+    )(own, near(got), near(packed))
+
+
+def expand_kernel(dense, ids_ref, slots_ref, full_ref, *refs):
+    panel_ref = refs[0] if dense else None
+    right_ref, out_ref, mass_ref, inverse_ref = refs[-4:]
+    for col in range(NZ * NC):
+        parts = full_ref[col, pl.ds(DEGREE, 8)].astype(jnp.int32).astype(F32)
+        inverse_ref[col] = (16.0 / UNIT) / (parts[0:4] + parts[4:8] / UNIT)
     for c in range(4):
         cols = pl.ds(c * TILE, TILE)
         total = jnp.zeros((2 * TILE, TILE), F32)
@@ -128,11 +188,21 @@
             lefts, rights = [], []
             for s in (2 * pair, 2 * pair + 1):
                 k = ids_ref[s, c]
-                inside = pl.ds(pl.multiple_of((k % 4) * TILE, TILE), TILE)
-                parts = panel_ref[k // 4, pl.ds(2 * TILE, 8), inside].astype(jnp.int32).astype(F32)
-                inverse = (16.0 / UNIT) / (parts[0:1] + parts[1:2] / UNIT)
-                left = panel_ref[k // 4, pl.ds(0, 2 * TILE), inside].astype(jnp.int32).astype(F32)
-                lefts.append((left * inverse).astype(BF16))
+                inverse = inverse_ref[k // 4, pl.ds(k % 4, 1), :]
+                if dense:
+                    inside = pl.ds(pl.multiple_of((k % 4) * TILE, TILE), TILE)
+                    left = panel_ref[k // 4, pl.ds(0, 2 * TILE), inside].astype(jnp.int32).astype(F32)
+                    lefts.append((left * inverse).astype(BF16))
+                else:
+                    parts = []
+                    for t in range(2):
+                        slot = slots_ref[k // 8, 8 * t + k % 8]
+                        start = pl.multiple_of(jnp.maximum(slot, 0) * HALF, HALF)
+                        scaled = jnp.where(slot >= 0, inverse, 0.0)
+                        for core in range(NC):
+                            part = full_ref[(k // 8) * NC + core, pl.ds(start, HALF)].astype(jnp.int32)
+                            parts.append((part.astype(F32) * scaled).astype(BF16))
+                    lefts.append(jnp.concatenate(parts, axis=0))
                 rights.append(right_ref[pl.ds(8 * c, 8), s].reshape(TILE, TILE))
             total = total + jnp.dot(
                 jnp.concatenate(lefts, axis=1),
@@ -146,18 +216,20 @@
             mass_ref[r, :, cols] = part
 
 
-def expand(ids, panel, right):
-    return pl.pallas_call(
-        expand_kernel,
+def expand(ids, slots, full, *panels_and_right):
+    dense = len(panels_and_right) == 2
+    return pl.pallas_call(
+        functools.partial(expand_kernel, dense),
         out_shape=(
             pltpu.VMEM((2 * TILE, 4 * TILE), F32),
             pltpu.VMEM((ROWS, 1, 4 * TILE), F32),
         ),
-        in_specs=[SMEM] + [VMEM] * 2,
+        in_specs=[SMEM, SMEM] + [VMEM] * (1 + len(panels_and_right)),
         out_specs=(VMEM, VMEM),
+        scratch_shapes=[pltpu.VMEM((NZ * NC, 4, TILE), F32)],
         compiler_params=pltpu.CompilerParams(vmem_limit_bytes=24 * 2**20),
-        name="expand",
-    )(ids, near(panel), near(right))
+        name="expand_dense" if dense else "expand",
+    )(ids, slots, full, *panels_and_right)
 
 
 def scale_kernel(inflated_ref, mass_ref, flow_ref):
@@ -176,19 +248,30 @@
 
 
 def on_device(weights, tile_mask):
-    masked, sent = prepare(tile_mask, weights)
+    panel, sent = prepare(tile_mask, weights)
     got = exchange(sent, ROW)
+    other = lax.ppermute(panel, "core", [(0, 1), (1, 0)])
+    packed = pack(lax.axis_index("core").reshape(1), panel, other)
     own = (lax.axis_index("y") // 2).reshape(1)
-    placed, full = place(own, got, masked)
+    placed, full = place(own, got, packed)
     right = exchange(placed, ROW)
-    panel = lax.all_gather(full, ("z", "core"))
+    full = lax.all_gather(full, COL)
     there = (got[:, 44, :8].reshape(64, 4) > 0).astype(jnp.int32)
     rank = jnp.cumsum(there, axis=0) - there
     tile_ids = lax.broadcasted_iota(jnp.int32, (KEEP, 64, 4), 1)
     ranks = lax.broadcasted_iota(jnp.int32, (KEEP, 64, 4), 0)
     chosen = (there == 1)[None] & (rank[None] == ranks)
     ids = jnp.sum(jnp.where(chosen, tile_ids, 0), axis=1)
-    inflated, mass = expand(ids, panel, right)
+    slots = full[::2, META, :16].astype(jnp.int32)
+    counts = full[:, META + 1, :ROWS].astype(jnp.int32).reshape(NZ, NC, ROWS).sum(axis=1)
+
+    def overfull():
+        return expand(ids, slots, full, lax.all_gather(panel, COL), right)
+
+    def fits():
+        return expand(ids, slots, full, right)
+
+    inflated, mass = lax.cond(jnp.max(counts) > SLOTS, overfull, fits)
     return scale(inflated, exchange(mass, ROW))
 
 

time: 97.9 us -> 88 us (0.90)
  blocking collectives: 59.5 us -> 49.7 us
  waiting for transfers between devices: 13.8 us -> 10.3 us
  starting transfers between devices: 15.5 us -> 18.5 us
  local copies, waits for them, and re-layouts: 2.54 us -> 0.32 us
  Pallas kernels: 5.68 us -> 6.98 us
    all_gather x1, blocking collectives: 41.4 us -> 31.6 us  [on_device(): full = lax.all_gather(full, COL)]
    all_to_all x2, waiting for transfers between devices: 13.8 us -> 9.19 us  [exchange(): return lax.all_to_all(blocks, axis, split_axis=0, concat_axis=0, tiled=True)]
    ppermute x0 -> x1, starting transfers between devices: none -> 2.86 us  [on_device(): other = lax.ppermute(panel, 'core', [(0, 1), (1, 0)])]
    unnamed x2 -> x0, local copies, waits for them, and re-layouts: 2.23 us -> none
    pallas_call x2 -> x3, Pallas kernels: 3.3 us -> 4.6 us  [the longest x1 2.18 us: expand(): pl.pallas_call(functools.partial(expand_kernel, dense), out_shape=(pltpu....]
    ppermute x0 -> x1, waiting for transfers between devices: none -> 1.14 us  [on_device(): other = lax.ppermute(panel, 'core', [(0, 1), (1, 0)])]
  transfers between devices with their start and end apart: 2 -> 3, of which waited for: 1 -> 2; matrix products, arithmetic and copies ran while one was open for 0% -> 1% of each run, Pallas kernels for 0% -> 1%
where the time goes in v5:
time: 88 us; the launch traced here: 87.6 us
  blocking collectives  49.7 us (56%)
  starting transfers between devices  18.5 us (21%)
  waiting for transfers between devices  10.3 us (12%)
  Pallas kernels  6.98 us (8%)
  other arithmetic  0.99 us (1%)
    all_gather x1, blocking collectives, on_device(): full = lax.all_gather(full, COL)  31.6 us
    all_to_all x1, blocking collectives, exchange(): return lax.all_to_all(blocks, axis, split_axis=0, concat_axis=0, tiled=True)  18.1 us
    all_to_all x2, starting transfers between devices, exchange(): return lax.all_to_all(blocks, axis, split_axis=0, concat_axis=0, tiled=True)  15.7 us
    all_to_all x2, waiting for transfers between devices, exchange(): return lax.all_to_all(blocks, axis, split_axis=0, concat_axis=0, tiled=True)  9.19 us
    ppermute x1, starting transfers between devices, on_device(): other = lax.ppermute(panel, 'core', [(0, 1), (1, 0)])  2.86 us
    pallas_call x1, Pallas kernels, expand(): pl.pallas_call(functools.partial(expand_kernel, dense), out_shape=(pltpu....  2.18 us
    pallas_call x1, Pallas kernels, prepare(): pl.pallas_call(prepare_kernel, out_shape=(pltpu.VMEM((2 * TILE + 8, 4 * T...  1.81 us
  transfers between devices with their start and end apart: 3, of which 2 were waited for; matrix products, arithmetic and copies ran while one was open for 1% of the time, Pallas kernels for 1%

profile of v5, /device:TPU:1, one launch (start us, length us, event | category | flops | bytes accessed | tf_op | source)
XLA Modules:
  0.0 87.6 jit_solution(11891305781550893111)
XLA Ops:
  0.0 1.8 %prepare.1 = (s16[264,512]{1,0:T(8,128)(2,1)S(1)}, bf16[32,48,128]{2,1,0:T(8,128)(2,1)}) custom-call(s32[2,4]{1,0:T(2,128)} %mask_ref.1, bf16[256,512]{1,0:T(8,128)(2,1)} %w_ref.1), custom_call_target="tpu_custom_call" | custom-call | tf_op jit(solution)/shard_map/prepare/pallas_call | solution.py:73
  1.8 10.5 %all-to-all-start = ((bf16[32,48,128]{2,1,0:T(8,128)(2,1)}), bf16[32,48,128]{2,1,0:T(8,128)(2,1)S(1)}, u32[]{:S(2)}, u32[]{:S(2)}) async-start(bf16[32,48,128]{2,1,0:T(8,128)(2,1)} %get-tuple-element.38), calls=%async_computation | async-start | bytes 786432 | tf_op jit(solution)/shard_map/all_to_all | solution.py:29
  12.3 2.9 %collective-permute-start = (s16[264,512]{1,0:T(8,128)(2,1)S(1)}, s16[264,512]{1,0:T(8,128)(2,1)S(1)}, u32[]{:S(2)}, u32[]{:S(2)}) collective-permute-start(s16[264,512]{1,0:T(8,128)(2,1)S(1)} %get-tuple-element.39.panel_ref), channel_id=1, source_target_pairs={{0,1},{1,0},{2,3},{3,2},{4,5},{5,4},{6,7},{7,6},{8,9},{9,8},{10,11... | collective-permute-start | bytes 811016 | tf_op jit(solution)/shard_map/ppermute | solution.py:253
  15.2 1.1 %collective-permute-done.other_ref = s16[264,512]{1,0:T(8,128)(2,1)S(1)} collective-permute-done((s16[264,512]{1,0:T(8,128)(2,1)S(1)}, s16[264,512]{1,0:T(8,128)(2,1)S(1)}, u32[]{:S(2)}, u32[]{:S(2)}) %collective-permute-start) | collective-permute-done | bytes 270368 | tf_op jit(solution)/shard_map/ppermute | solution.py:253
  16.3 0.6 pack.1.packed_ref
  16.9 9.2 %all-to-all-done.got_ref = bf16[32,48,128]{2,1,0:T(8,128)(2,1)S(1)} async-done(((bf16[32,48,128]{2,1,0:T(8,128)(2,1)}), bf16[32,48,128]{2,1,0:T(8,128)(2,1)S(1)}, u32[]{:S(2)}, u32[]{:S(2)}) %all-to-all-start) | async-done | bytes 393248 | tf_op jit(solution)/shard_map/all_to_all | solution.py:29
  26.1 1.5 %place.1 = (bf16[32,8,16,128]{3,2,1,0:T(8,128)(2,1)}, s16[592,128]{1,0:T(8,128)(2,1)S(1)}) custom-call(s32[1]{0:T(128)} %bitcast.1.own_ref, bf16[32,48,128]{2,1,0:T(8,128)(2,1)S(1)} %all-to-all-done.got_ref, s16[592,128]{1,0:T(8,128)(2,1)S(1)} %pack.1.packed_ref), custom_call_target="tpu_custom_call" | custom-call | tf_op jit(solution)/shard_map/place/pallas_call | solution.py:165
  27.6 5.2 %all-to-all-start.1 = ((bf16[32,8,16,128]{3,2,1,0:T(8,128)(2,1)}), bf16[32,8,16,128]{3,2,1,0:T(8,128)(2,1)}, u32[]{:S(2)}, u32[]{:S(2)}) async-start(bf16[32,8,16,128]{3,2,1,0:T(8,128)(2,1)} %get-tuple-element.41), calls=%async_computation.1 | async-start | bytes 2097152 | tf_op jit(solution)/shard_map/all_to_all | solution.py:29
  32.8 0.1 fusion
  32.9 0.1 reshape.41
  32.9 0.1 reduce_window_sum.11
  33.0 0.1 copy.5
  33.1 0.1 copy.6
  33.2 31.6 %all-gather.5 = s16[9472,128]{1,0:T(8,128)(2,1)S(1)} all-gather(s16[592,128]{1,0:T(8,128)(2,1)S(1)} %get-tuple-element.40), channel_id=3, replica_groups=mesh['y'=8,'x'=4,'z'=8,'core'=2] {'z','core'}, dimensions={0}, use_global_device_ids=true | all-gather | bytes 2576384 | tf_op jit(solution)/shard_map/all_gather | solution.py:258
  64.9 0.6 reduce_max.9
  66.1 0.1 select_reduce_fusion
  66.3 0.0 all-to-all-done.1
  66.3 2.3 %conditional.1 = ((f32[256,512]{1,0:T(8,128)S(1)}, f32[32,1,512]{2,1,0:T(1,128)S(1)})) conditional(s32[]{:T(128)} %convert_element_type.39, (s32[8,4]{0,1:T(4,128)S(1)}, s32[8,16]{1,0:T(8,128)S(1)}, s16[16,592,128]{2,1,0:T(8,128)(2,1)S(1)}, bf16[32,8,16,128]{3,2,1,0:T(8,128)(2,1)}) %tuple.19, (s16[264,512]{1,0:T(8,128)(2,1)S(1)}, ...), branch_computations={%region_4.5_spmd, %region_5.6_spmd} | conditional | bytes 4595976 | solution.py:274
  66.3 0.1 copy.8.ids_ref
  66.4 2.2 %expand.1 = (f32[256,512]{1,0:T(8,128)S(1)}, f32[32,1,512]{2,1,0:T(1,128)S(1)}) custom-call(s32[8,4]{1,0:T(8,128)S(1)} %copy.8.ids_ref, s32[8,16]{1,0:T(8,128)S(1)} %get-tuple-element.24.slots_ref, s16[16,592,128]{2,1,0:T(8,128)(2,1)S(1)} %get-tuple-element.25.full_ref, bf16[32,8,16,128]{3,2,1,0:T(8,128)(2,1)} %get-tuple-element.26.refs_0_), custom_call_target="tpu_custom_call" | custom-call | tf_op jit(solution)/shard_map/cond/branch_0_fun/expand/pallas_call | solution.py:221
  68.6 18.1 %all_to_all.15.mass_ref = f32[32,1,512]{2,1,0:T(1,128)S(1)} all-to-all(f32[32,1,512]{2,1,0:T(1,128)S(1)} %get-tuple-element.43), channel_id=1, replica_groups=mesh['y'=8,'x'=4,'z'=8,'core'=2] {'y','x'}, dimensions={0} | all-to-all | bytes 131072 | tf_op jit(solution)/shard_map/all_to_all | solution.py:29
  86.7 0.9 %scale.1 = f32[256,512]{1,0:T(8,128)} custom-call(f32[256,512]{1,0:T(8,128)S(1)} %get-tuple-element.42.inflated_ref, f32[32,1,512]{2,1,0:T(1,128)S(1)} %all_to_all.15.mass_ref), custom_call_target="tpu_custom_call" | custom-call | tf_op jit(solution)/shard_map/scale/pallas_call | solution.py:241
  (6 shorter events, 0.1 us)
Async XLA Ops:
  1.8 24.3 %all-to-all-start = ((bf16[32,48,128]{2,1,0:T(8,128)(2,1)}), bf16[32,48,128]{2,1,0:T(8,128)(2,1)S(1)}, u32[]{:S(2)}, u32[]{:S(2)}) async-start(bf16[32,48,128]{2,1,0:T(8,128)(2,1)} %get-tuple-element.38), calls=%async_computation | async-start | bytes 786432 | tf_op jit(solution)/shard_map/all_to_all | solution.py:29
  12.3 4.0 %collective-permute-start = (s16[264,512]{1,0:T(8,128)(2,1)S(1)}, s16[264,512]{1,0:T(8,128)(2,1)S(1)}, u32[]{:S(2)}, u32[]{:S(2)}) collective-permute-start(s16[264,512]{1,0:T(8,128)(2,1)S(1)} %get-tuple-element.39.panel_ref), channel_id=1, source_target_pairs={{0,1},{1,0},{2,3},{3,2},{4,5},{5,4},{6,7},{7,6},{8,9},{9,8},{10,11... | collective-permute-start | bytes 811016 | tf_op jit(solution)/shard_map/ppermute | solution.py:253
  27.6 38.7 %all-to-all-start.1 = ((bf16[32,8,16,128]{3,2,1,0:T(8,128)(2,1)}), bf16[32,8,16,128]{3,2,1,0:T(8,128)(2,1)}, u32[]{:S(2)}, u32[]{:S(2)}) async-start(bf16[32,8,16,128]{3,2,1,0:T(8,128)(2,1)} %get-tuple-element.41), calls=%async_computation.1 | async-start | bytes 2097152 | tf_op jit(solution)/shard_map/all_to_all | solution.py:29

commit v6 on v5

--- a/solution.py
+++ b/solution.py
@@ -42,25 +42,21 @@
     return parts
 
 
-def prepare_kernel(mask_ref, w_ref, panel_ref, sent_ref):
+def slice_kernel(mask_ref, w_ref, sent_ref):
     lane = lax.broadcasted_iota(jnp.int32, (1, TILE), 1)
     packed = jnp.zeros((1, TILE), F32)
     sums, masks = [], []
     for c in range(4):
-        cols = pl.ds(c * TILE, TILE)
         total = jnp.zeros((1, TILE), F32)
         for t in range(2):
             on = mask_ref[t, c].astype(F32)
             masks.append(jnp.full((1, TILE), on, F32))
             packed = jnp.where(lane == t * 4 + c, on, packed)
-            tile = w_ref[pl.ds(t * TILE, TILE), cols].astype(F32) * on
+            tile = w_ref[pl.ds(t * TILE, TILE), pl.ds(c * TILE, TILE)].astype(F32) * on
             total = total + jnp.sum(tile, axis=0, keepdims=True)
-            panel_ref[pl.ds(t * TILE, TILE), cols] = (tile * UNIT).astype(jnp.int32).astype(I16)
             tile = tile.astype(BF16)
             for e in range(8):
                 sent_ref[8 * c + e, pl.ds(t * SLICE, SLICE)] = tile[e * SLICE : (e + 1) * SLICE]
-        rows = jnp.concatenate([*masks[2 * c : 2 * c + 2], jnp.zeros((6, TILE), F32)], axis=0)
-        panel_ref[pl.ds(2 * TILE, 8), cols] = rows.astype(jnp.int32).astype(I16)
         sums.append(split3(total))
     rows = [sums[c][p].astype(F32) for p in range(3) for c in range(4)]
     for c in range(4):
@@ -69,16 +65,36 @@
             sent_ref[8 * c + e, pl.ds(2 * SLICE, SLICE)] = extra
 
 
-def prepare(mask, weights):
-    return pl.pallas_call(
-        prepare_kernel,
-        out_shape=(
-            pltpu.VMEM((2 * TILE + 8, 4 * TILE), I16),
-            pltpu.VMEM((ROWS, 3 * SLICE, TILE), BF16),
-        ),
+def slices(mask, weights):
+    return pl.pallas_call(
+        slice_kernel,
+        out_shape=jax.ShapeDtypeStruct((ROWS, 3 * SLICE, TILE), BF16),
         in_specs=[SMEM, VMEM],
-        out_specs=(VMEM,) * 2,
-        name="prepare",
+        out_specs=VMEM,
+        name="slices",
+    )(mask, weights)
+
+
+def panel_kernel(mask_ref, w_ref, panel_ref):
+    for c in range(4):
+        cols = pl.ds(c * TILE, TILE)
+        masks = []
+        for t in range(2):
+            on = mask_ref[t, c].astype(F32)
+            masks.append(jnp.full((1, TILE), on, F32))
+            tile = w_ref[pl.ds(t * TILE, TILE), cols].astype(F32) * (on * UNIT)
+            panel_ref[pl.ds(t * TILE, TILE), cols] = tile.astype(jnp.int32).astype(I16)
+        rows = jnp.concatenate([*masks, jnp.zeros((6, TILE), F32)], axis=0)
+        panel_ref[pl.ds(2 * TILE, 8), cols] = rows.astype(jnp.int32).astype(I16)
+
+
+def fixed_panel(mask, weights):
+    return pl.pallas_call(
+        panel_kernel,
+        out_shape=pltpu.VMEM((2 * TILE + 8, 4 * TILE), I16),
+        in_specs=[SMEM, VMEM],
+        out_specs=VMEM,
+        name="panel",
     )(mask, weights)
 
 
@@ -122,7 +138,7 @@
     )(core, near(panel), near(other))
 
 
-def place_kernel(own_ref, got_ref, packed_ref, placed_ref, full_ref, slot_ref):
+def place_kernel(own_ref, got_ref, packed_ref, placed_ref, full_ref, ids_ref, slot_ref):
     total = jnp.zeros((SLICE, TILE), F32)
     masks, tiles = [], []
     for r in range(ROWS):
@@ -133,7 +149,19 @@
     degree = total[0:4] + (total[4:8] + total[8:12])
     high = jnp.floor(degree * 16.0)
     low = (degree * 16.0 - high) * UNIT
-    tiles = jnp.concatenate([*tiles, jnp.zeros((TILE - ROWS, TILE), F32)], axis=0).astype(BF16)
+    tiles = jnp.concatenate(tiles, axis=0)
+    row = lax.broadcasted_iota(jnp.int32, (ROWS, TILE), 0)
+    lower = lax.broadcasted_iota(jnp.int32, (ROWS, TILE), 1) // 4
+    pair = tiles + jnp.where(lower == 0, pltpu.roll(tiles, TILE - 4, 1), pltpu.roll(tiles, 4, 1))
+    above = lax.broadcasted_iota(jnp.int32, (ROWS, ROWS), 0) > lax.broadcasted_iota(jnp.int32, (ROWS, ROWS), 1)
+    rank = jnp.dot(above.astype(BF16), pair.astype(BF16), preferred_element_type=F32)
+    rank = rank + jnp.where(lower == 1, pltpu.roll(tiles, 4, 1), 0.0)
+    kept_row = (2 * row + lower).astype(F32)
+    for s in range(KEEP):
+        hit = jnp.where((tiles > 0) & (rank == s) & (lower < 2), kept_row, 0.0)
+        hit = jnp.sum(hit, axis=0, keepdims=True)
+        ids_ref[pl.ds(s, 1)] = (hit + pltpu.roll(hit, TILE - 4, 1)).astype(jnp.int32)
+    tiles = jnp.concatenate([tiles, jnp.zeros((TILE - ROWS, TILE), F32)], axis=0).astype(BF16)
     counts = lax.dot_general(
         jnp.ones((8, TILE), BF16), tiles, (((1,), (1,)), ((), ())), preferred_element_type=F32
     )
@@ -167,9 +195,10 @@
         out_shape=(
             pltpu.VMEM((ROWS, KEEP, SLICE, TILE), BF16),
             pltpu.VMEM((PACKED, TILE), I16),
+            jax.ShapeDtypeStruct((KEEP, TILE), jnp.int32),
         ),
         in_specs=[SMEM, VMEM, VMEM],
-        out_specs=(VMEM, VMEM),
+        out_specs=(VMEM, VMEM, VMEM),
         scratch_shapes=[pltpu.VMEM((64, TILE), F32)],
         name="place",
     )(own, near(got), near(packed))
@@ -240,7 +269,7 @@
 def scale(inflated, mass):
     return pl.pallas_call(
         scale_kernel,
-        out_shape=jax.ShapeDtypeStruct((2 * TILE, 4 * TILE), F32),
+        out_shape=pltpu.HBM((2 * TILE, 4 * TILE), F32),
         in_specs=[VMEM, VMEM],
         out_specs=VMEM,
         name="scale",
@@ -248,31 +277,27 @@
 
 
 def on_device(weights, tile_mask):
-    panel, sent = prepare(tile_mask, weights)
-    got = exchange(sent, ROW)
+    got = exchange(slices(tile_mask, weights), ROW)
+    panel = fixed_panel(tile_mask, weights)
     other = lax.ppermute(panel, "core", [(0, 1), (1, 0)])
     packed = pack(lax.axis_index("core").reshape(1), panel, other)
     own = (lax.axis_index("y") // 2).reshape(1)
-    placed, full = place(own, got, packed)
+    placed, full, ids = place(own, got, packed)
     right = exchange(placed, ROW)
     full = lax.all_gather(full, COL)
-    there = (got[:, 44, :8].reshape(64, 4) > 0).astype(jnp.int32)
-    rank = jnp.cumsum(there, axis=0) - there
-    tile_ids = lax.broadcasted_iota(jnp.int32, (KEEP, 64, 4), 1)
-    ranks = lax.broadcasted_iota(jnp.int32, (KEEP, 64, 4), 0)
-    chosen = (there == 1)[None] & (rank[None] == ranks)
-    ids = jnp.sum(jnp.where(chosen, tile_ids, 0), axis=1)
     slots = full[::2, META, :16].astype(jnp.int32)
+    inflated, mass = expand(ids, slots, full, right)
+    mass = exchange(mass, ROW)
     counts = full[:, META + 1, :ROWS].astype(jnp.int32).reshape(NZ, NC, ROWS).sum(axis=1)
 
     def overfull():
-        return expand(ids, slots, full, lax.all_gather(panel, COL), right)
+        inflated, mass = expand(ids, slots, full, lax.all_gather(panel, COL), right)
+        return scale(inflated, exchange(mass, ROW))
 
     def fits():
-        return expand(ids, slots, full, right)
-
-    inflated, mass = lax.cond(jnp.max(counts) > SLOTS, overfull, fits)
-    return scale(inflated, exchange(mass, ROW))
+        return scale(inflated, mass)
+
+    return lax.cond(jnp.max(counts) > SLOTS, overfull, fits)
 
 
 def solution(mesh):

time: 88 us -> 87 us (0.989)
  blocking collectives: 49.7 us -> 31.6 us
  starting transfers between devices: 18.5 us -> 27.9 us
  waiting for transfers between devices: 10.3 us -> 16.7 us
  Pallas kernels: 6.98 us -> 8.84 us
    all_to_all x1 -> x0, blocking collectives: 18.1 us -> none  [exchange(): return lax.all_to_all(blocks, axis, split_axis=0, concat_axis=0, tiled=True)]
    all_to_all x2 -> x3, starting transfers between devices: 15.7 us -> 25.1 us  [exchange(): return lax.all_to_all(blocks, axis, split_axis=0, concat_axis=0, tiled=True)]
    all_to_all x2 -> x3, waiting for transfers between devices: 9.19 us -> 15.6 us  [exchange(): return lax.all_to_all(blocks, axis, split_axis=0, concat_axis=0, tiled=True)]
    pallas_call x2 -> x3, Pallas kernels: 2.71 us -> 3.77 us  [the longest x1 1.81 us: slices(): pl.pallas_call(slice_kernel, out_shape=jax.ShapeDtypeStruct((ROWS, 3 * SL...]
  transfers between devices with their start and end apart: 3 -> 4, of which waited for: 2 -> 3; matrix products, arithmetic and copies ran while one was open for 1% -> 1% of each run, Pallas kernels for 1% -> 2%
where the time goes in v6:
time: 87 us; the launch traced here: 86.6 us
  blocking collectives  31.6 us (36%)
  starting transfers between devices  27.9 us (32%)
  waiting for transfers between devices  16.7 us (19%)
  Pallas kernels  8.84 us (10%)
    all_gather x1, blocking collectives, on_device(): full = lax.all_gather(full, COL)  31.6 us
    all_to_all x3, starting transfers between devices, exchange(): return lax.all_to_all(blocks, axis, split_axis=0, concat_axis=0, tiled=True)  25.1 us
    all_to_all x3, waiting for transfers between devices, exchange(): return lax.all_to_all(blocks, axis, split_axis=0, concat_axis=0, tiled=True)  15.6 us
    ppermute x1, starting transfers between devices, on_device(): other = lax.ppermute(panel, 'core', [(0, 1), (1, 0)])  2.86 us
    pallas_call x1, Pallas kernels, expand(): pl.pallas_call(functools.partial(expand_kernel, dense), out_shape=(pltpu....  2.8 us
    pallas_call x1, Pallas kernels, slices(): pl.pallas_call(slice_kernel, out_shape=jax.ShapeDtypeStruct((ROWS, 3 * SL...  1.81 us
  transfers between devices with their start and end apart: 4, of which 3 were waited for; matrix products, arithmetic and copies ran while one was open for 1% of the time, Pallas kernels for 2%

profile of v6, /device:TPU:1, one launch (start us, length us, event | category | flops | bytes accessed | tf_op | source)
XLA Modules:
  0.0 86.6 jit_solution(768364844077867519)
XLA Ops:
  0.0 1.8 %slices.1 = bf16[32,48,128]{2,1,0:T(8,128)(2,1)} custom-call(s32[2,4]{1,0:T(2,128)} %mask_ref.3, bf16[256,512]{1,0:T(8,128)(2,1)} %w_ref.3), custom_call_target="tpu_custom_call" | custom-call | tf_op jit(solution)/shard_map/slices/pallas_call | solution.py:69
  1.8 10.5 %all-to-all-start.1 = ((bf16[32,48,128]{2,1,0:T(8,128)(2,1)}), bf16[32,48,128]{2,1,0:T(8,128)(2,1)S(1)}, u32[]{:S(2)}, u32[]{:S(2)}) async-start(bf16[32,48,128]{2,1,0:T(8,128)(2,1)} %slices.1), calls=%async_computation.1 | async-start | bytes 786432 | tf_op jit(solution)/shard_map/all_to_all | solution.py:29
  12.3 1.1 %panel.1.panel_ref = s16[264,512]{1,0:T(8,128)(2,1)S(1)} custom-call(s32[2,4]{1,0:T(2,128)} %mask_ref.3, bf16[256,512]{1,0:T(8,128)(2,1)} %w_ref.3), custom_call_target="tpu_custom_call" | custom-call | tf_op jit(solution)/shard_map/panel/pallas_call | solution.py:92
  13.4 2.9 %collective-permute-start = (s16[264,512]{1,0:T(8,128)(2,1)S(1)}, s16[264,512]{1,0:T(8,128)(2,1)S(1)}, u32[]{:S(2)}, u32[]{:S(2)}) collective-permute-start(s16[264,512]{1,0:T(8,128)(2,1)S(1)} %panel.1.panel_ref), channel_id=1, source_target_pairs={{0,1},{1,0},{2,3},{3,2},{4,5},{5,4},{6,7},{7,6},{8,9},{9,8},{10,11... | collective-permute-start | bytes 811016 | tf_op jit(solution)/shard_map/ppermute | solution.py:282
  16.3 1.1 %collective-permute-done.other_ref = s16[264,512]{1,0:T(8,128)(2,1)S(1)} collective-permute-done((s16[264,512]{1,0:T(8,128)(2,1)S(1)}, s16[264,512]{1,0:T(8,128)(2,1)S(1)}, u32[]{:S(2)}, u32[]{:S(2)}) %collective-permute-start) | collective-permute-done | bytes 270368 | tf_op jit(solution)/shard_map/ppermute | solution.py:282
  17.4 0.6 pack.1.packed_ref
  18.0 8.1 %all-to-all-done.1.got_ref = bf16[32,48,128]{2,1,0:T(8,128)(2,1)S(1)} async-done(((bf16[32,48,128]{2,1,0:T(8,128)(2,1)}), bf16[32,48,128]{2,1,0:T(8,128)(2,1)S(1)}, u32[]{:S(2)}, u32[]{:S(2)}) %all-to-all-start.1) | async-done | bytes 393248 | tf_op jit(solution)/shard_map/all_to_all | solution.py:29
  26.1 1.7 %place.1 = (bf16[32,8,16,128]{3,2,1,0:T(8,128)(2,1)}, s16[592,128]{1,0:T(8,128)(2,1)S(1)}, s32[8,128]{1,0:T(8,128)S(1)}) custom-call(s32[1]{0:T(128)} %bitcast.1.own_ref, bf16[32,48,128]{2,1,0:T(8,128)(2,1)S(1)} %all-to-all-done.1.got_ref, s16[592,128]{1,0:T(8,128)(2,1)S(1)} %pack.1.packed_ref), custom_call_target="tpu_custom_call" | custom-call | tf_op jit(solution)/shard_map/place/pallas_call | solution.py:193
  27.8 5.2 %all-to-all-start.2 = ((bf16[32,8,16,128]{3,2,1,0:T(8,128)(2,1)}), bf16[32,8,16,128]{3,2,1,0:T(8,128)(2,1)}, u32[]{:S(2)}, u32[]{:S(2)}) async-start(bf16[32,8,16,128]{3,2,1,0:T(8,128)(2,1)} %get-tuple-element.38), calls=%async_computation.2 | async-start | bytes 2097152 | tf_op jit(solution)/shard_map/all_to_all | solution.py:29
  33.0 31.6 %all-gather.5 = s16[9472,128]{1,0:T(8,128)(2,1)S(1)} all-gather(s16[592,128]{1,0:T(8,128)(2,1)S(1)} %get-tuple-element.36), channel_id=3, replica_groups=mesh['y'=8,'x'=4,'z'=8,'core'=2] {'z','core'}, dimensions={0}, use_global_device_ids=true | all-gather | bytes 2576384 | tf_op jit(solution)/shard_map/all_gather | solution.py:287
  64.6 0.0 all-to-all-done.2.refs_0_
  64.6 2.8 %expand.1 = (f32[256,512]{1,0:T(8,128)S(1)}, f32[32,1,512]{2,1,0:T(1,128)}) custom-call(s32[8,128]{1,0:T(8,128)S(1)} %get-tuple-element.37.ids_ref, s32[8,16]{1,0:T(8,128)S(1)} %bitcast.11, s16[16,592,128]{2,1,0:T(8,128)(2,1)S(1)} %bitcast.8, bf16[32,8,16,128]{3,2,1,0:T(8,128)(2,1)} %all-to-all-done.2.refs_0_), custom_call_target="tpu_custom_call" | custom-call | tf_op jit(solution)/shard_map/expand/pallas_call | solution.py:250
  67.4 9.4 %all-to-all-start.3 = ((f32[32,1,512]{2,1,0:T(1,128)}), f32[32,1,512]{2,1,0:T(1,128)S(1)}, u32[]{:S(2)}, u32[]{:S(2)}) async-start(f32[32,1,512]{2,1,0:T(1,128)} %get-tuple-element.40), calls=%async_computation.3 | async-start | bytes 131072 | tf_op jit(solution)/shard_map/all_to_all | solution.py:29
  76.8 0.7 reduce_max.9
  78.2 7.5 %all-to-all-done.3 = f32[32,1,512]{2,1,0:T(1,128)S(1)} async-done(((f32[32,1,512]{2,1,0:T(1,128)}), f32[32,1,512]{2,1,0:T(1,128)S(1)}, u32[]{:S(2)}, u32[]{:S(2)}) %all-to-all-start.3) | async-done | bytes 65568 | tf_op jit(solution)/shard_map/all_to_all | solution.py:29
  85.7 0.9 %conditional.1 = (f32[256,512]{1,0:T(8,128)}) conditional(s32[]{:T(128)} %convert_element_type.21, (f32[256,512]{1,0:T(8,128)S(1)}, f32[32,1,512]{2,1,0:T(1,128)S(1)}) %tuple.11, (s16[264,512]{1,0:T(8,128)(2,1)S(1)}, s32[8,128]{1,0:T(8,128)S(1)}, s32[8,16]{1,0:T(8,128)S(1)}, s16[16,592,128]{2,1,0:T(8,128)(2,1)S(1)}, ...), branch_computations={%region_2.3_spmd, %region_3.4_spmd} | conditional | bytes 4726792 | solution.py:300
  85.7 0.9 %scale.2 = f32[256,512]{1,0:T(8,128)} custom-call(f32[256,512]{1,0:T(8,128)S(1)} %get-tuple-element.22.inflated_ref, f32[32,1,512]{2,1,0:T(1,128)S(1)} %get-tuple-element.23.mass_ref), custom_call_target="tpu_custom_call" | custom-call | tf_op jit(solution)/shard_map/cond/branch_0_fun/scale/pallas_call | solution.py:270
  (3 shorter events, 0.0 us)
Async XLA Ops:
  1.8 24.3 %all-to-all-start.1 = ((bf16[32,48,128]{2,1,0:T(8,128)(2,1)}), bf16[32,48,128]{2,1,0:T(8,128)(2,1)S(1)}, u32[]{:S(2)}, u32[]{:S(2)}) async-start(bf16[32,48,128]{2,1,0:T(8,128)(2,1)} %slices.1), calls=%async_computation.1 | async-start | bytes 786432 | tf_op jit(solution)/shard_map/all_to_all | solution.py:29
  13.4 4.0 %collective-permute-start = (s16[264,512]{1,0:T(8,128)(2,1)S(1)}, s16[264,512]{1,0:T(8,128)(2,1)S(1)}, u32[]{:S(2)}, u32[]{:S(2)}) collective-permute-start(s16[264,512]{1,0:T(8,128)(2,1)S(1)} %panel.1.panel_ref), channel_id=1, source_target_pairs={{0,1},{1,0},{2,3},{3,2},{4,5},{5,4},{6,7},{7,6},{8,9},{9,8},{10,11... | collective-permute-start | bytes 811016 | tf_op jit(solution)/shard_map/ppermute | solution.py:282
  27.8 36.8 %all-to-all-start.2 = ((bf16[32,8,16,128]{3,2,1,0:T(8,128)(2,1)}), bf16[32,8,16,128]{3,2,1,0:T(8,128)(2,1)}, u32[]{:S(2)}, u32[]{:S(2)}) async-start(bf16[32,8,16,128]{3,2,1,0:T(8,128)(2,1)} %get-tuple-element.38), calls=%async_computation.2 | async-start | bytes 2097152 | tf_op jit(solution)/shard_map/all_to_all | solution.py:29
  67.4 18.3 %all-to-all-start.3 = ((f32[32,1,512]{2,1,0:T(1,128)}), f32[32,1,512]{2,1,0:T(1,128)S(1)}, u32[]{:S(2)}, u32[]{:S(2)}) async-start(f32[32,1,512]{2,1,0:T(1,128)} %get-tuple-element.40), calls=%async_computation.3 | async-start | bytes 131072 | tf_op jit(solution)/shard_map/all_to_all | solution.py:29

commit v7 on v6

--- a/solution.py
+++ b/solution.py
@@ -21,6 +21,7 @@
 META = DEGREE + 8
 PACKED = META + 8
 COL = ("z", "core")
+LIMIT = pltpu.CompilerParams(vmem_limit_bytes=24 * 2**20)
 VMEM = pl.BlockSpec(memory_space=pltpu.VMEM)
 SMEM = pl.BlockSpec(memory_space=pltpu.SMEM)
 
@@ -206,10 +207,17 @@
 
 def expand_kernel(dense, ids_ref, slots_ref, full_ref, *refs):
     panel_ref = refs[0] if dense else None
-    right_ref, out_ref, mass_ref, inverse_ref = refs[-4:]
-    for col in range(NZ * NC):
-        parts = full_ref[col, pl.ds(DEGREE, 8)].astype(jnp.int32).astype(F32)
-        inverse_ref[col] = (16.0 / UNIT) / (parts[0:4] + parts[4:8] / UNIT)
+    right_ref, out_ref, mass_ref, most_ref, inverse_ref = refs[-5:]
+    most = jnp.zeros((8, TILE), jnp.int32)
+    for z in range(NZ):
+        held = jnp.zeros((8, TILE), jnp.int32)
+        for col in range(NC * z, NC * z + NC):
+            rows = full_ref[col, pl.ds(DEGREE, 16)].astype(jnp.int32)
+            parts = rows[0:8].astype(F32)
+            inverse_ref[col] = (16.0 / UNIT) / (parts[0:4] + parts[4:8] / UNIT)
+            held = held + rows[8:16]
+        most = jnp.maximum(most, held)
+    most_ref[0] = jnp.max(most[1:2, :ROWS])
     for c in range(4):
         cols = pl.ds(c * TILE, TILE)
         total = jnp.zeros((2 * TILE, TILE), F32)
@@ -251,12 +259,13 @@
         functools.partial(expand_kernel, dense),
         out_shape=(
             pltpu.VMEM((2 * TILE, 4 * TILE), F32),
-            pltpu.VMEM((ROWS, 1, 4 * TILE), F32),
+            jax.ShapeDtypeStruct((ROWS, 1, 4 * TILE), F32),
+            jax.ShapeDtypeStruct((1,), jnp.int32),
         ),
         in_specs=[SMEM, SMEM] + [VMEM] * (1 + len(panels_and_right)),
-        out_specs=(VMEM, VMEM),
+        out_specs=(VMEM, VMEM, SMEM),
         scratch_shapes=[pltpu.VMEM((NZ * NC, 4, TILE), F32)],
-        compiler_params=pltpu.CompilerParams(vmem_limit_bytes=24 * 2**20),
+        compiler_params=LIMIT,
         name="expand_dense" if dense else "expand",
     )(ids, slots, full, *panels_and_right)
 
@@ -286,18 +295,14 @@
     right = exchange(placed, ROW)
     full = lax.all_gather(full, COL)
     slots = full[::2, META, :16].astype(jnp.int32)
-    inflated, mass = expand(ids, slots, full, right)
+    inflated, mass, most = expand(ids, slots, full, right)
     mass = exchange(mass, ROW)
-    counts = full[:, META + 1, :ROWS].astype(jnp.int32).reshape(NZ, NC, ROWS).sum(axis=1)
 
     def overfull():
-        inflated, mass = expand(ids, slots, full, lax.all_gather(panel, COL), right)
+        inflated, mass, _ = expand(ids, slots, full, lax.all_gather(panel, COL), right)
         return scale(inflated, exchange(mass, ROW))
 
-    def fits():
-        return scale(inflated, mass)
-
-    return lax.cond(jnp.max(counts) > SLOTS, overfull, fits)
+    return lax.cond(most[0] > SLOTS, overfull, lambda: scale(inflated, mass))
 
 
 def solution(mesh):

time: 87 us -> 87 us (level)
  transfers between devices with their start and end apart: 4 -> 4, of which waited for: 3 -> 3; matrix products, arithmetic and copies ran while one was open for 1% -> 0% of each run, Pallas kernels for 2% -> 2%
where the time goes in v7:
time: 87 us; the launch traced here: 86.6 us
  blocking collectives  31.6 us (36%)
  starting transfers between devices  27.9 us (32%)
  waiting for transfers between devices  17.4 us (20%)
  Pallas kernels  8.82 us (10%)
    all_gather x1, blocking collectives, on_device(): full = lax.all_gather(full, COL)  31.6 us
    all_to_all x3, starting transfers between devices, exchange(): return lax.all_to_all(blocks, axis, split_axis=0, concat_axis=0, tiled=True)  25.1 us
    all_to_all x3, waiting for transfers between devices, exchange(): return lax.all_to_all(blocks, axis, split_axis=0, concat_axis=0, tiled=True)  16.3 us
    ppermute x1, starting transfers between devices, on_device(): other = lax.ppermute(panel, 'core', [(0, 1), (1, 0)])  2.86 us
    pallas_call x1, Pallas kernels, expand(): pl.pallas_call(functools.partial(expand_kernel, dense), out_shape=(pltpu....  2.81 us
    pallas_call x1, Pallas kernels, slices(): pl.pallas_call(slice_kernel, out_shape=jax.ShapeDtypeStruct((ROWS, 3 * SL...  1.81 us
  transfers between devices with their start and end apart: 4, of which 3 were waited for; matrix products, arithmetic and copies ran while one was open for 0% of the time, Pallas kernels for 2%

profile of v7, /device:TPU:1, one launch (start us, length us, event | category | flops | bytes accessed | tf_op | source)
XLA Modules:
  0.0 86.6 jit_solution(4179946008831280705)
XLA Ops:
  0.0 1.8 %slices.1 = bf16[32,48,128]{2,1,0:T(8,128)(2,1)} custom-call(s32[2,4]{1,0:T(2,128)} %mask_ref.3, bf16[256,512]{1,0:T(8,128)(2,1)} %w_ref.3), custom_call_target="tpu_custom_call" | custom-call | tf_op jit(solution)/shard_map/slices/pallas_call | solution.py:70
  1.8 10.5 %all-to-all-start.1 = ((bf16[32,48,128]{2,1,0:T(8,128)(2,1)}), bf16[32,48,128]{2,1,0:T(8,128)(2,1)S(1)}, u32[]{:S(2)}, u32[]{:S(2)}) async-start(bf16[32,48,128]{2,1,0:T(8,128)(2,1)} %slices.1), calls=%async_computation.1 | async-start | bytes 786432 | tf_op jit(solution)/shard_map/all_to_all | solution.py:30
  12.3 1.1 %panel.1.panel_ref = s16[264,512]{1,0:T(8,128)(2,1)S(1)} custom-call(s32[2,4]{1,0:T(2,128)} %mask_ref.3, bf16[256,512]{1,0:T(8,128)(2,1)} %w_ref.3), custom_call_target="tpu_custom_call" | custom-call | tf_op jit(solution)/shard_map/panel/pallas_call | solution.py:93
  13.4 2.9 %collective-permute-start = (s16[264,512]{1,0:T(8,128)(2,1)S(1)}, s16[264,512]{1,0:T(8,128)(2,1)S(1)}, u32[]{:S(2)}, u32[]{:S(2)}) collective-permute-start(s16[264,512]{1,0:T(8,128)(2,1)S(1)} %panel.1.panel_ref), channel_id=1, source_target_pairs={{0,1},{1,0},{2,3},{3,2},{4,5},{5,4},{6,7},{7,6},{8,9},{9,8},{10,11... | collective-permute-start | bytes 811016 | tf_op jit(solution)/shard_map/ppermute | solution.py:291
  16.3 1.1 %collective-permute-done.other_ref = s16[264,512]{1,0:T(8,128)(2,1)S(1)} collective-permute-done((s16[264,512]{1,0:T(8,128)(2,1)S(1)}, s16[264,512]{1,0:T(8,128)(2,1)S(1)}, u32[]{:S(2)}, u32[]{:S(2)}) %collective-permute-start) | collective-permute-done | bytes 270368 | tf_op jit(solution)/shard_map/ppermute | solution.py:291
  17.4 0.6 pack.1.packed_ref
  18.0 8.1 %all-to-all-done.1.got_ref = bf16[32,48,128]{2,1,0:T(8,128)(2,1)S(1)} async-done(((bf16[32,48,128]{2,1,0:T(8,128)(2,1)}), bf16[32,48,128]{2,1,0:T(8,128)(2,1)S(1)}, u32[]{:S(2)}, u32[]{:S(2)}) %all-to-all-start.1) | async-done | bytes 393248 | tf_op jit(solution)/shard_map/all_to_all | solution.py:30
  26.1 1.6 %place.1 = (bf16[32,8,16,128]{3,2,1,0:T(8,128)(2,1)}, s16[592,128]{1,0:T(8,128)(2,1)S(1)}, s32[8,128]{1,0:T(8,128)S(1)}) custom-call(s32[1]{0:T(128)} %bitcast.1.own_ref, bf16[32,48,128]{2,1,0:T(8,128)(2,1)S(1)} %all-to-all-done.1.got_ref, s16[592,128]{1,0:T(8,128)(2,1)S(1)} %pack.1.packed_ref), custom_call_target="tpu_custom_call" | custom-call | tf_op jit(solution)/shard_map/place/pallas_call | solution.py:194
  27.8 5.2 %all-to-all-start.2 = ((bf16[32,8,16,128]{3,2,1,0:T(8,128)(2,1)}), bf16[32,8,16,128]{3,2,1,0:T(8,128)(2,1)}, u32[]{:S(2)}, u32[]{:S(2)}) async-start(bf16[32,8,16,128]{3,2,1,0:T(8,128)(2,1)} %get-tuple-element.39), calls=%async_computation.2 | async-start | bytes 2097152 | tf_op jit(solution)/shard_map/all_to_all | solution.py:30
  32.9 31.6 %all-gather.5 = s16[9472,128]{1,0:T(8,128)(2,1)S(1)} all-gather(s16[592,128]{1,0:T(8,128)(2,1)S(1)} %get-tuple-element.38), channel_id=3, replica_groups=mesh['y'=8,'x'=4,'z'=8,'core'=2] {'z','core'}, dimensions={0}, use_global_device_ids=true | all-gather | bytes 2576384 | tf_op jit(solution)/shard_map/all_gather | solution.py:296
  64.6 0.0 all-to-all-done.2.refs_0_
  64.6 2.8 %expand.1 = (f32[256,512]{1,0:T(8,128)S(1)}, f32[32,1,512]{2,1,0:T(1,128)}, s32[1]{0:T(128)}) custom-call(s32[8,128]{1,0:T(8,128)S(1)} %get-tuple-element.37.ids_ref, s32[8,16]{1,0:T(8,128)S(1)} %bitcast.10, s16[16,592,128]{2,1,0:T(8,128)(2,1)S(1)} %bitcast.8, bf16[32,8,16,128]{3,2,1,0:T(8,128)(2,1)} %all-to-all-done.2.refs_0_), custom_call_target="tpu_custom_call" | custom-call | tf_op jit(solution)/shard_map/expand/pallas_call | solution.py:258
  67.4 9.4 %all-to-all-start.3 = ((f32[32,1,512]{2,1,0:T(1,128)}), f32[32,1,512]{2,1,0:T(1,128)S(1)}, u32[]{:S(2)}, u32[]{:S(2)}) async-start(f32[32,1,512]{2,1,0:T(1,128)} %get-tuple-element.42), calls=%async_computation.3 | async-start | bytes 131072 | tf_op jit(solution)/shard_map/all_to_all | solution.py:30
  77.5 8.2 %all-to-all-done.3 = f32[32,1,512]{2,1,0:T(1,128)S(1)} async-done(((f32[32,1,512]{2,1,0:T(1,128)}), f32[32,1,512]{2,1,0:T(1,128)S(1)}, u32[]{:S(2)}, u32[]{:S(2)}) %all-to-all-start.3) | async-done | bytes 65568 | tf_op jit(solution)/shard_map/all_to_all | solution.py:30
  85.7 0.9 %conditional.1 = (f32[256,512]{1,0:T(8,128)}) conditional(s32[]{:T(128)} %bitcast.5, (f32[256,512]{1,0:T(8,128)S(1)}, f32[32,1,512]{2,1,0:T(1,128)S(1)}) %tuple.11, (s16[264,512]{1,0:T(8,128)(2,1)S(1)}, s32[8,128]{1,0:T(8,128)S(1)}, s32[8,16]{1,0:T(8,128)S(1)}, s16[16,592,128]{2,1,0:T(8,128)(2,1)S(1)}, bf16[32,8,16,128]{3,2,1,0:T(8,128)(2,1)}) %tuple.18), branch_computations={%region_0.1_spmd, %region_1.2_spmd} | conditional | bytes 4726792 | solution.py:305
  85.7 0.9 %scale.2 = f32[256,512]{1,0:T(8,128)} custom-call(f32[256,512]{1,0:T(8,128)S(1)} %get-tuple-element.22.inflated_ref, f32[32,1,512]{2,1,0:T(1,128)S(1)} %get-tuple-element.23.mass_ref), custom_call_target="tpu_custom_call" | custom-call | tf_op jit(solution)/shard_map/cond/branch_0_fun/scale/pallas_call | solution.py:279
  (1 shorter events, 0.0 us)
Async XLA Ops:
  1.8 24.3 %all-to-all-start.1 = ((bf16[32,48,128]{2,1,0:T(8,128)(2,1)}), bf16[32,48,128]{2,1,0:T(8,128)(2,1)S(1)}, u32[]{:S(2)}, u32[]{:S(2)}) async-start(bf16[32,48,128]{2,1,0:T(8,128)(2,1)} %slices.1), calls=%async_computation.1 | async-start | bytes 786432 | tf_op jit(solution)/shard_map/all_to_all | solution.py:30
  13.4 4.0 %collective-permute-start = (s16[264,512]{1,0:T(8,128)(2,1)S(1)}, s16[264,512]{1,0:T(8,128)(2,1)S(1)}, u32[]{:S(2)}, u32[]{:S(2)}) collective-permute-start(s16[264,512]{1,0:T(8,128)(2,1)S(1)} %panel.1.panel_ref), channel_id=1, source_target_pairs={{0,1},{1,0},{2,3},{3,2},{4,5},{5,4},{6,7},{7,6},{8,9},{9,8},{10,11... | collective-permute-start | bytes 811016 | tf_op jit(solution)/shard_map/ppermute | solution.py:291
  27.8 36.8 %all-to-all-start.2 = ((bf16[32,8,16,128]{3,2,1,0:T(8,128)(2,1)}), bf16[32,8,16,128]{3,2,1,0:T(8,128)(2,1)}, u32[]{:S(2)}, u32[]{:S(2)}) async-start(bf16[32,8,16,128]{3,2,1,0:T(8,128)(2,1)} %get-tuple-element.39), calls=%async_computation.2 | async-start | bytes 2097152 | tf_op jit(solution)/shard_map/all_to_all | solution.py:30
  67.4 18.3 %all-to-all-start.3 = ((f32[32,1,512]{2,1,0:T(1,128)}), f32[32,1,512]{2,1,0:T(1,128)S(1)}, u32[]{:S(2)}, u32[]{:S(2)}) async-start(f32[32,1,512]{2,1,0:T(1,128)} %get-tuple-element.42), calls=%async_computation.3 | async-start | bytes 131072 | tf_op jit(solution)/shard_map/all_to_all | solution.py:30

commit v8 on v7

--- a/solution.py
+++ b/solution.py
@@ -12,7 +12,7 @@
 SLICE = 16
 NY, NX, NZ, NC = 8, 4, 8, 2
 ROWS = NY * NX
-ROW = ("y", "x")
+FIRST = ((4, 2), (0, 0), (4, 2))
 F32, BF16, I16 = jnp.float32, jnp.bfloat16, jnp.int16
 UNIT = 16384.0
 SLOTS = 9
@@ -26,8 +26,19 @@
 SMEM = pl.BlockSpec(memory_space=pltpu.SMEM)
 
 
-def exchange(blocks, axis):
-    return lax.all_to_all(blocks, axis, split_axis=0, concat_axis=0, tiled=True)
+def row_at(place, first):
+    return (place // NX + first[0]) % NY * NX + (place + first[1]) % NX
+
+
+def place_of(row, first):
+    return row_at(row, (-first[0], -first[1]))
+
+
+def exchange(blocks, first):
+    group = [row_at(place, first) for place in range(ROWS)]
+    return lax.all_to_all(
+        blocks, "row", split_axis=0, concat_axis=0, tiled=True, axis_index_groups=[group]
+    )
 
 
 def near(x):
@@ -57,13 +68,13 @@
             total = total + jnp.sum(tile, axis=0, keepdims=True)
             tile = tile.astype(BF16)
             for e in range(8):
-                sent_ref[8 * c + e, pl.ds(t * SLICE, SLICE)] = tile[e * SLICE : (e + 1) * SLICE]
+                sent_ref[place_of(8 * c + e, FIRST[0]), pl.ds(t * SLICE, SLICE)] = tile[e * SLICE : (e + 1) * SLICE]
         sums.append(split3(total))
     rows = [sums[c][p].astype(F32) for p in range(3) for c in range(4)]
     for c in range(4):
         extra = jnp.concatenate([*rows, packed, packed, *masks[2 * c : 2 * c + 2]], axis=0).astype(BF16)
         for e in range(8):
-            sent_ref[8 * c + e, pl.ds(2 * SLICE, SLICE)] = extra
+            sent_ref[place_of(8 * c + e, FIRST[0]), pl.ds(2 * SLICE, SLICE)] = extra
 
 
 def slices(mask, weights):
@@ -143,7 +154,7 @@
     total = jnp.zeros((SLICE, TILE), F32)
     masks, tiles = [], []
     for r in range(ROWS):
-        extra = got_ref[r, pl.ds(2 * SLICE, SLICE)].astype(F32)
+        extra = got_ref[place_of(r, FIRST[0]), pl.ds(2 * SLICE, SLICE)].astype(F32)
         total = total + extra
         tiles.append(extra[12:13])
         masks.append(extra[14:16])
@@ -180,7 +191,7 @@
         mine = jnp.where(own == c, degree[c : c + 1], mine)
     kept = [jnp.zeros((SLICE, TILE), F32) for _ in range(KEEP)]
     for k in range(64):
-        tile = got_ref[k // 2, pl.ds((k % 2) * SLICE, SLICE)].astype(F32)
+        tile = got_ref[place_of(k // 2, FIRST[0]), pl.ds((k % 2) * SLICE, SLICE)].astype(F32)
         slot = jnp.broadcast_to(slot_ref[pl.ds(k, 1)], (SLICE, TILE))
         for s in range(KEEP):
             kept[s] = jnp.where(slot == s, tile, kept[s])
@@ -240,7 +251,7 @@
                             part = full_ref[(k // 8) * NC + core, pl.ds(start, HALF)].astype(jnp.int32)
                             parts.append((part.astype(F32) * scaled).astype(BF16))
                     lefts.append(jnp.concatenate(parts, axis=0))
-                rights.append(right_ref[pl.ds(8 * c, 8), s].reshape(TILE, TILE))
+                rights.extend(right_ref[place_of(8 * c + e, FIRST[1]), s] for e in range(8))
             total = total + jnp.dot(
                 jnp.concatenate(lefts, axis=1),
                 jnp.concatenate(rights, axis=0),
@@ -286,28 +297,28 @@
 
 
 def on_device(weights, tile_mask):
-    got = exchange(slices(tile_mask, weights), ROW)
+    got = exchange(slices(tile_mask, weights), FIRST[0])
     panel = fixed_panel(tile_mask, weights)
     other = lax.ppermute(panel, "core", [(0, 1), (1, 0)])
     packed = pack(lax.axis_index("core").reshape(1), panel, other)
-    own = (lax.axis_index("y") // 2).reshape(1)
+    own = (lax.axis_index("row") // 8).reshape(1)
     placed, full, ids = place(own, got, packed)
-    right = exchange(placed, ROW)
+    right = exchange(placed, FIRST[1])
     full = lax.all_gather(full, COL)
     slots = full[::2, META, :16].astype(jnp.int32)
     inflated, mass, most = expand(ids, slots, full, right)
-    mass = exchange(mass, ROW)
+    mass = exchange(mass, FIRST[2])
 
     def overfull():
         inflated, mass, _ = expand(ids, slots, full, lax.all_gather(panel, COL), right)
-        return scale(inflated, exchange(mass, ROW))
+        return scale(inflated, exchange(mass, FIRST[2]))
 
     return lax.cond(most[0] > SLOTS, overfull, lambda: scale(inflated, mass))
 
 
 def solution(mesh):
-    split = Mesh(mesh.devices.reshape(NY, NX, NZ, NC), ("y", "x", "z", "core"))
-    placed = P(ROW, ("z", "core"))
+    split = Mesh(mesh.devices.reshape(ROWS, NZ, NC), ("row", "z", "core"))
+    placed = P("row", COL)
     return jax.shard_map(
         on_device, mesh=split, in_specs=(placed, placed), out_specs=placed, check_vma=False
     )

time: 87 us -> 81.9 us (0.941)
  waiting for transfers between devices: 17.4 us -> 2.9 us
  starting transfers between devices: 27.9 us -> 34.6 us
  blocking collectives: 31.6 us -> 34.3 us
    all_to_all x3, waiting for transfers between devices: 16.3 us -> 1.77 us  [exchange(): lax.all_to_all(blocks, 'row', split_axis=0, concat_axis=0, tiled=True, ax...]
    all_to_all x3, starting transfers between devices: 25.1 us -> 28.5 us  [exchange(): lax.all_to_all(blocks, 'row', split_axis=0, concat_axis=0, tiled=True, ax...]
    ppermute x1, starting transfers between devices: 2.86 us -> 6.05 us  [on_device(): other = lax.ppermute(panel, 'core', [(0, 1), (1, 0)])]
    all_gather x1, blocking collectives: 31.6 us -> 34.3 us  [on_device(): full = lax.all_gather(full, COL)]
  transfers between devices with their start and end apart: 4 -> 4, of which waited for: 3 -> 2; matrix products, arithmetic and copies ran while one was open for 0% -> 0% of each run, Pallas kernels for 2% -> 2%
where the time goes in v8:
time: 81.9 us; the launch traced here: 81.4 us
  starting transfers between devices  34.6 us (42%)
  blocking collectives  34.3 us (42%)
  Pallas kernels  8.82 us (11%)
  waiting for transfers between devices  2.9 us (4%)
    all_gather x1, blocking collectives, on_device(): full = lax.all_gather(full, COL)  34.3 us
    all_to_all x3, starting transfers between devices, exchange(): lax.all_to_all(blocks, 'row', split_axis=0, concat_axis=0, tiled=True, ax...  28.5 us
    ppermute x1, starting transfers between devices, on_device(): other = lax.ppermute(panel, 'core', [(0, 1), (1, 0)])  6.05 us
    pallas_call x1, Pallas kernels, expand(): pl.pallas_call(functools.partial(expand_kernel, dense), out_shape=(pltpu....  2.81 us
    pallas_call x1, Pallas kernels, slices(): pl.pallas_call(slice_kernel, out_shape=jax.ShapeDtypeStruct((ROWS, 3 * SL...  1.81 us
    all_to_all x3, waiting for transfers between devices, exchange(): lax.all_to_all(blocks, 'row', split_axis=0, concat_axis=0, tiled=True, ax...  1.77 us
  transfers between devices with their start and end apart: 4, of which 2 were waited for; matrix products, arithmetic and copies ran while one was open for 0% of the time, Pallas kernels for 2%

profile of v8, /device:TPU:1, one launch (start us, length us, event | category | flops | bytes accessed | tf_op | source)
XLA Modules:
  0.0 81.4 jit_solution(16085348593529269911)
XLA Ops:
  0.0 1.8 %slices.1 = bf16[32,48,128]{2,1,0:T(8,128)(2,1)} custom-call(s32[2,4]{1,0:T(2,128)} %mask_ref.3, bf16[256,512]{1,0:T(8,128)(2,1)} %w_ref.3), custom_call_target="tpu_custom_call" | custom-call | tf_op jit(solution)/shard_map/slices/pallas_call | solution.py:81
  1.8 12.5 %all-to-all-start.1 = ((bf16[32,48,128]{2,1,0:T(8,128)(2,1)}), bf16[32,48,128]{2,1,0:T(8,128)(2,1)S(1)}, u32[]{:S(2)}, u32[]{:S(2)}) async-start(bf16[32,48,128]{2,1,0:T(8,128)(2,1)} %slices.1), calls=%async_computation.1 | async-start | bytes 786432 | tf_op jit(solution)/shard_map/all_to_all | solution.py:39
  14.3 1.1 %panel.1.panel_ref = s16[264,512]{1,0:T(8,128)(2,1)S(1)} custom-call(s32[2,4]{1,0:T(2,128)} %mask_ref.3, bf16[256,512]{1,0:T(8,128)(2,1)} %w_ref.3), custom_call_target="tpu_custom_call" | custom-call | tf_op jit(solution)/shard_map/panel/pallas_call | solution.py:104
  15.4 6.1 %collective-permute-start = (s16[264,512]{1,0:T(8,128)(2,1)S(1)}, s16[264,512]{1,0:T(8,128)(2,1)S(1)}, u32[]{:S(2)}, u32[]{:S(2)}) collective-permute-start(s16[264,512]{1,0:T(8,128)(2,1)S(1)} %panel.1.panel_ref), channel_id=1, source_target_pairs={{0,1},{1,0},{2,3},{3,2},{4,5},{5,4},{6,7},{7,6},{8,9},{9,8},{10,11... | collective-permute-start | bytes 811016 | tf_op jit(solution)/shard_map/ppermute | solution.py:302
  21.4 1.1 %collective-permute-done.other_ref = s16[264,512]{1,0:T(8,128)(2,1)S(1)} collective-permute-done((s16[264,512]{1,0:T(8,128)(2,1)S(1)}, s16[264,512]{1,0:T(8,128)(2,1)S(1)}, u32[]{:S(2)}, u32[]{:S(2)}) %collective-permute-start) | collective-permute-done | bytes 270368 | tf_op jit(solution)/shard_map/ppermute | solution.py:302
  22.6 0.6 pack.1.packed_ref
  23.2 0.0 all-to-all-done.1.got_ref
  23.2 1.6 %place.1 = (bf16[32,8,16,128]{3,2,1,0:T(8,128)(2,1)}, s16[592,128]{1,0:T(8,128)(2,1)S(1)}, s32[8,128]{1,0:T(8,128)S(1)}) custom-call(s32[1]{0:T(128)} %bitcast.1.own_ref, bf16[32,48,128]{2,1,0:T(8,128)(2,1)S(1)} %all-to-all-done.1.got_ref, s16[592,128]{1,0:T(8,128)(2,1)S(1)} %pack.1.packed_ref), custom_call_target="tpu_custom_call" | custom-call | tf_op jit(solution)/shard_map/place/pallas_call | solution.py:205
  24.8 4.7 %all-to-all-start.2 = ((bf16[32,8,16,128]{3,2,1,0:T(8,128)(2,1)}), bf16[32,8,16,128]{3,2,1,0:T(8,128)(2,1)}, u32[]{:S(2)}, u32[]{:S(2)}) async-start(bf16[32,8,16,128]{3,2,1,0:T(8,128)(2,1)} %get-tuple-element.39), calls=%async_computation.2 | async-start | bytes 2097152 | tf_op jit(solution)/shard_map/all_to_all | solution.py:39
  29.5 34.3 %all-gather.5 = s16[9472,128]{1,0:T(8,128)(2,1)S(1)} all-gather(s16[592,128]{1,0:T(8,128)(2,1)S(1)} %get-tuple-element.38), channel_id=3, replica_groups=mesh['row'=32,'z'=8,'core'=2] {'z','core'}, dimensions={0}, use_global_device_ids=true | all-gather | bytes 2576384 | tf_op jit(solution)/shard_map/all_gather | solution.py:307
  63.8 0.0 all-to-all-done.2.refs_0_
  63.8 2.8 %expand.1 = (f32[256,512]{1,0:T(8,128)S(1)}, f32[32,1,512]{2,1,0:T(1,128)}, s32[1]{0:T(128)}) custom-call(s32[8,128]{1,0:T(8,128)S(1)} %get-tuple-element.37.ids_ref, s32[8,16]{1,0:T(8,128)S(1)} %bitcast.10, s16[16,592,128]{2,1,0:T(8,128)(2,1)S(1)} %bitcast.8, bf16[32,8,16,128]{3,2,1,0:T(8,128)(2,1)} %all-to-all-done.2.refs_0_), custom_call_target="tpu_custom_call" | custom-call | tf_op jit(solution)/shard_map/expand/pallas_call | solution.py:269
  66.6 11.4 %all-to-all-start.3 = ((f32[32,1,512]{2,1,0:T(1,128)}), f32[32,1,512]{2,1,0:T(1,128)S(1)}, u32[]{:S(2)}, u32[]{:S(2)}) async-start(f32[32,1,512]{2,1,0:T(1,128)} %get-tuple-element.42), calls=%async_computation.3 | async-start | bytes 131072 | tf_op jit(solution)/shard_map/all_to_all | solution.py:39
  78.7 1.8 %all-to-all-done.3 = f32[32,1,512]{2,1,0:T(1,128)S(1)} async-done(((f32[32,1,512]{2,1,0:T(1,128)}), f32[32,1,512]{2,1,0:T(1,128)S(1)}, u32[]{:S(2)}, u32[]{:S(2)}) %all-to-all-start.3) | async-done | bytes 65568 | tf_op jit(solution)/shard_map/all_to_all | solution.py:39
  80.5 0.9 %conditional.1 = (f32[256,512]{1,0:T(8,128)}) conditional(s32[]{:T(128)} %bitcast.5, (f32[256,512]{1,0:T(8,128)S(1)}, f32[32,1,512]{2,1,0:T(1,128)S(1)}) %tuple.11, (s16[264,512]{1,0:T(8,128)(2,1)S(1)}, s32[8,128]{1,0:T(8,128)S(1)}, s32[8,16]{1,0:T(8,128)S(1)}, s16[16,592,128]{2,1,0:T(8,128)(2,1)S(1)}, bf16[32,8,16,128]{3,2,1,0:T(8,128)(2,1)}) %tuple.18), branch_computations={%region_0.1_spmd, %region_1.2_spmd} | conditional | bytes 4726792 | solution.py:316
  80.5 0.9 %scale.2 = f32[256,512]{1,0:T(8,128)} custom-call(f32[256,512]{1,0:T(8,128)S(1)} %get-tuple-element.22.inflated_ref, f32[32,1,512]{2,1,0:T(1,128)S(1)} %get-tuple-element.23.mass_ref), custom_call_target="tpu_custom_call" | custom-call | tf_op jit(solution)/shard_map/cond/branch_0_fun/scale/pallas_call | solution.py:290
  (1 shorter events, 0.0 us)
Async XLA Ops:
  1.8 21.4 %all-to-all-start.1 = ((bf16[32,48,128]{2,1,0:T(8,128)(2,1)}), bf16[32,48,128]{2,1,0:T(8,128)(2,1)S(1)}, u32[]{:S(2)}, u32[]{:S(2)}) async-start(bf16[32,48,128]{2,1,0:T(8,128)(2,1)} %slices.1), calls=%async_computation.1 | async-start | bytes 786432 | tf_op jit(solution)/shard_map/all_to_all | solution.py:39
  15.4 7.2 %collective-permute-start = (s16[264,512]{1,0:T(8,128)(2,1)S(1)}, s16[264,512]{1,0:T(8,128)(2,1)S(1)}, u32[]{:S(2)}, u32[]{:S(2)}) collective-permute-start(s16[264,512]{1,0:T(8,128)(2,1)S(1)} %panel.1.panel_ref), channel_id=1, source_target_pairs={{0,1},{1,0},{2,3},{3,2},{4,5},{5,4},{6,7},{7,6},{8,9},{9,8},{10,11... | collective-permute-start | bytes 811016 | tf_op jit(solution)/shard_map/ppermute | solution.py:302
  24.8 39.0 %all-to-all-start.2 = ((bf16[32,8,16,128]{3,2,1,0:T(8,128)(2,1)}), bf16[32,8,16,128]{3,2,1,0:T(8,128)(2,1)}, u32[]{:S(2)}, u32[]{:S(2)}) async-start(bf16[32,8,16,128]{3,2,1,0:T(8,128)(2,1)} %get-tuple-element.39), calls=%async_computation.2 | async-start | bytes 2097152 | tf_op jit(solution)/shard_map/all_to_all | solution.py:39
  66.6 13.8 %all-to-all-start.3 = ((f32[32,1,512]{2,1,0:T(1,128)}), f32[32,1,512]{2,1,0:T(1,128)S(1)}, u32[]{:S(2)}, u32[]{:S(2)}) async-start(f32[32,1,512]{2,1,0:T(1,128)} %get-tuple-element.42), calls=%async_computation.3 | async-start | bytes 131072 | tf_op jit(solution)/shard_map/all_to_all | solution.py:39

commit v9 on v8

--- a/solution.py
+++ b/solution.py
@@ -12,7 +12,7 @@
 SLICE = 16
 NY, NX, NZ, NC = 8, 4, 8, 2
 ROWS = NY * NX
-FIRST = ((4, 2), (0, 0), (4, 2))
+FIRST = ((4, 2), (2, 1), (4, 2))
 F32, BF16, I16 = jnp.float32, jnp.bfloat16, jnp.int16
 UNIT = 16384.0
 SLOTS = 9
@@ -245,7 +245,7 @@
                     parts = []
                     for t in range(2):
                         slot = slots_ref[k // 8, 8 * t + k % 8]
-                        start = pl.multiple_of(jnp.maximum(slot, 0) * HALF, HALF)
+                        start = pl.multiple_of(jnp.clip(slot, 0, SLOTS - 1) * HALF, HALF)
                         scaled = jnp.where(slot >= 0, inverse, 0.0)
                         for core in range(NC):
                             part = full_ref[(k // 8) * NC + core, pl.ds(start, HALF)].astype(jnp.int32)

time: 81.9 us -> 81.2 us (level)
  starting transfers between devices: 34.6 us -> 33.6 us
    all_to_all x3, starting transfers between devices: 28.5 us -> 27.5 us  [exchange(): lax.all_to_all(blocks, 'row', split_axis=0, concat_axis=0, tiled=True, ax...]
where the time goes in v9:
time: 81.2 us; the launch traced here: 80.8 us
  blocking collectives  34.8 us (43%)
  starting transfers between devices  33.6 us (41%)
  Pallas kernels  8.87 us (11%)
  waiting for transfers between devices  2.73 us (3%)
    all_gather x1, blocking collectives, on_device(): full = lax.all_gather(full, COL)  34.8 us
    all_to_all x3, starting transfers between devices, exchange(): lax.all_to_all(blocks, 'row', split_axis=0, concat_axis=0, tiled=True, ax...  27.5 us
    ppermute x1, starting transfers between devices, on_device(): other = lax.ppermute(panel, 'core', [(0, 1), (1, 0)])  6.05 us
    pallas_call x1, Pallas kernels, expand(): pl.pallas_call(functools.partial(expand_kernel, dense), out_shape=(pltpu....  2.86 us
    pallas_call x1, Pallas kernels, slices(): pl.pallas_call(slice_kernel, out_shape=jax.ShapeDtypeStruct((ROWS, 3 * SL...  1.81 us
    pallas_call x1, Pallas kernels, place(): pl.pallas_call(place_kernel, out_shape=(pltpu.VMEM((ROWS, KEEP, SLICE, TI...  1.63 us
  transfers between devices with their start and end apart: 4, of which 2 were waited for; matrix products, arithmetic and copies ran while one was open for 0% of the time, Pallas kernels for 2%

profile of v9, /device:TPU:1, one launch (start us, length us, event | category | flops | bytes accessed | tf_op | source)
XLA Modules:
  0.0 80.8 jit_solution(5185142007199553269)
XLA Ops:
  0.0 1.8 %slices.1 = bf16[32,48,128]{2,1,0:T(8,128)(2,1)} custom-call(s32[2,4]{1,0:T(2,128)} %mask_ref.3, bf16[256,512]{1,0:T(8,128)(2,1)} %w_ref.3), custom_call_target="tpu_custom_call" | custom-call | tf_op jit(solution)/shard_map/slices/pallas_call | solution.py:81
  1.8 12.5 %all-to-all-start.1 = ((bf16[32,48,128]{2,1,0:T(8,128)(2,1)}), bf16[32,48,128]{2,1,0:T(8,128)(2,1)S(1)}, u32[]{:S(2)}, u32[]{:S(2)}) async-start(bf16[32,48,128]{2,1,0:T(8,128)(2,1)} %slices.1), calls=%async_computation.1 | async-start | bytes 786432 | tf_op jit(solution)/shard_map/all_to_all | solution.py:39
  14.3 1.1 %panel.1.panel_ref = s16[264,512]{1,0:T(8,128)(2,1)S(1)} custom-call(s32[2,4]{1,0:T(2,128)} %mask_ref.3, bf16[256,512]{1,0:T(8,128)(2,1)} %w_ref.3), custom_call_target="tpu_custom_call" | custom-call | tf_op jit(solution)/shard_map/panel/pallas_call | solution.py:104
  15.4 6.1 %collective-permute-start = (s16[264,512]{1,0:T(8,128)(2,1)S(1)}, s16[264,512]{1,0:T(8,128)(2,1)S(1)}, u32[]{:S(2)}, u32[]{:S(2)}) collective-permute-start(s16[264,512]{1,0:T(8,128)(2,1)S(1)} %panel.1.panel_ref), channel_id=1, source_target_pairs={{0,1},{1,0},{2,3},{3,2},{4,5},{5,4},{6,7},{7,6},{8,9},{9,8},{10,11... | collective-permute-start | bytes 811016 | tf_op jit(solution)/shard_map/ppermute | solution.py:302
  21.4 1.1 %collective-permute-done.other_ref = s16[264,512]{1,0:T(8,128)(2,1)S(1)} collective-permute-done((s16[264,512]{1,0:T(8,128)(2,1)S(1)}, s16[264,512]{1,0:T(8,128)(2,1)S(1)}, u32[]{:S(2)}, u32[]{:S(2)}) %collective-permute-start) | collective-permute-done | bytes 270368 | tf_op jit(solution)/shard_map/ppermute | solution.py:302
  22.6 0.6 pack.1.packed_ref
  23.2 0.0 all-to-all-done.1.got_ref
  23.2 1.6 %place.1 = (bf16[32,8,16,128]{3,2,1,0:T(8,128)(2,1)}, s16[592,128]{1,0:T(8,128)(2,1)S(1)}, s32[8,128]{1,0:T(8,128)S(1)}) custom-call(s32[1]{0:T(128)} %bitcast.1.own_ref, bf16[32,48,128]{2,1,0:T(8,128)(2,1)S(1)} %all-to-all-done.1.got_ref, s16[592,128]{1,0:T(8,128)(2,1)S(1)} %pack.1.packed_ref), custom_call_target="tpu_custom_call" | custom-call | tf_op jit(solution)/shard_map/place/pallas_call | solution.py:205
  24.8 5.2 %all-to-all-start.2 = ((bf16[32,8,16,128]{3,2,1,0:T(8,128)(2,1)}), bf16[32,8,16,128]{3,2,1,0:T(8,128)(2,1)}, u32[]{:S(2)}, u32[]{:S(2)}) async-start(bf16[32,8,16,128]{3,2,1,0:T(8,128)(2,1)} %get-tuple-element.39), calls=%async_computation.2 | async-start | bytes 2097152 | tf_op jit(solution)/shard_map/all_to_all | solution.py:39
  30.0 34.8 %all-gather.5 = s16[9472,128]{1,0:T(8,128)(2,1)S(1)} all-gather(s16[592,128]{1,0:T(8,128)(2,1)S(1)} %get-tuple-element.38), channel_id=3, replica_groups=mesh['row'=32,'z'=8,'core'=2] {'z','core'}, dimensions={0}, use_global_device_ids=true | all-gather | bytes 2576384 | tf_op jit(solution)/shard_map/all_gather | solution.py:307
  64.9 0.0 all-to-all-done.2.refs_0_
  64.9 2.9 %expand.1 = (f32[256,512]{1,0:T(8,128)S(1)}, f32[32,1,512]{2,1,0:T(1,128)}, s32[1]{0:T(128)}) custom-call(s32[8,128]{1,0:T(8,128)S(1)} %get-tuple-element.37.ids_ref, s32[8,16]{1,0:T(8,128)S(1)} %bitcast.10, s16[16,592,128]{2,1,0:T(8,128)(2,1)S(1)} %bitcast.8, bf16[32,8,16,128]{3,2,1,0:T(8,128)(2,1)} %all-to-all-done.2.refs_0_), custom_call_target="tpu_custom_call" | custom-call | tf_op jit(solution)/shard_map/expand/pallas_call | solution.py:269
  67.8 9.8 %all-to-all-start.3 = ((f32[32,1,512]{2,1,0:T(1,128)}), f32[32,1,512]{2,1,0:T(1,128)S(1)}, u32[]{:S(2)}, u32[]{:S(2)}) async-start(f32[32,1,512]{2,1,0:T(1,128)} %get-tuple-element.42), calls=%async_computation.3 | async-start | bytes 131072 | tf_op jit(solution)/shard_map/all_to_all | solution.py:39
  78.3 1.6 %all-to-all-done.3 = f32[32,1,512]{2,1,0:T(1,128)S(1)} async-done(((f32[32,1,512]{2,1,0:T(1,128)}), f32[32,1,512]{2,1,0:T(1,128)S(1)}, u32[]{:S(2)}, u32[]{:S(2)}) %all-to-all-start.3) | async-done | bytes 65568 | tf_op jit(solution)/shard_map/all_to_all | solution.py:39
  79.9 0.9 %conditional.1 = (f32[256,512]{1,0:T(8,128)}) conditional(s32[]{:T(128)} %bitcast.5, (f32[256,512]{1,0:T(8,128)S(1)}, f32[32,1,512]{2,1,0:T(1,128)S(1)}) %tuple.11, (s16[264,512]{1,0:T(8,128)(2,1)S(1)}, s32[8,128]{1,0:T(8,128)S(1)}, s32[8,16]{1,0:T(8,128)S(1)}, s16[16,592,128]{2,1,0:T(8,128)(2,1)S(1)}, bf16[32,8,16,128]{3,2,1,0:T(8,128)(2,1)}) %tuple.18), branch_computations={%region_0.1_spmd, %region_1.2_spmd} | conditional | bytes 4726792 | solution.py:316
  79.9 0.9 %scale.2 = f32[256,512]{1,0:T(8,128)} custom-call(f32[256,512]{1,0:T(8,128)S(1)} %get-tuple-element.22.inflated_ref, f32[32,1,512]{2,1,0:T(1,128)S(1)} %get-tuple-element.23.mass_ref), custom_call_target="tpu_custom_call" | custom-call | tf_op jit(solution)/shard_map/cond/branch_0_fun/scale/pallas_call | solution.py:290
  (1 shorter events, 0.0 us)
Async XLA Ops:
  1.8 21.4 %all-to-all-start.1 = ((bf16[32,48,128]{2,1,0:T(8,128)(2,1)}), bf16[32,48,128]{2,1,0:T(8,128)(2,1)S(1)}, u32[]{:S(2)}, u32[]{:S(2)}) async-start(bf16[32,48,128]{2,1,0:T(8,128)(2,1)} %slices.1), calls=%async_computation.1 | async-start | bytes 786432 | tf_op jit(solution)/shard_map/all_to_all | solution.py:39
  15.4 7.2 %collective-permute-start = (s16[264,512]{1,0:T(8,128)(2,1)S(1)}, s16[264,512]{1,0:T(8,128)(2,1)S(1)}, u32[]{:S(2)}, u32[]{:S(2)}) collective-permute-start(s16[264,512]{1,0:T(8,128)(2,1)S(1)} %panel.1.panel_ref), channel_id=1, source_target_pairs={{0,1},{1,0},{2,3},{3,2},{4,5},{5,4},{6,7},{7,6},{8,9},{9,8},{10,11... | collective-permute-start | bytes 811016 | tf_op jit(solution)/shard_map/ppermute | solution.py:302
  24.8 40.1 %all-to-all-start.2 = ((bf16[32,8,16,128]{3,2,1,0:T(8,128)(2,1)}), bf16[32,8,16,128]{3,2,1,0:T(8,128)(2,1)}, u32[]{:S(2)}, u32[]{:S(2)}) async-start(bf16[32,8,16,128]{3,2,1,0:T(8,128)(2,1)} %get-tuple-element.39), calls=%async_computation.2 | async-start | bytes 2097152 | tf_op jit(solution)/shard_map/all_to_all | solution.py:39
  67.8 12.1 %all-to-all-start.3 = ((f32[32,1,512]{2,1,0:T(1,128)}), f32[32,1,512]{2,1,0:T(1,128)S(1)}, u32[]{:S(2)}, u32[]{:S(2)}) async-start(f32[32,1,512]{2,1,0:T(1,128)} %get-tuple-element.42), calls=%async_computation.3 | async-start | bytes 131072 | tf_op jit(solution)/shard_map/all_to_all | solution.py:39

commit v10 on v9

--- a/solution.py
+++ b/solution.py
@@ -5,7 +5,7 @@
 from jax import lax
 from jax.experimental import pallas as pl
 from jax.experimental.pallas import tpu as pltpu
-from jax.sharding import Mesh, PartitionSpec as P
+from jax.sharding import PartitionSpec as P
 
 KEEP = 8
 TILE = 128
@@ -13,6 +13,7 @@
 NY, NX, NZ, NC = 8, 4, 8, 2
 ROWS = NY * NX
 FIRST = ((4, 2), (2, 1), (4, 2))
+FIRST_Z = 4
 F32, BF16, I16 = jnp.float32, jnp.bfloat16, jnp.int16
 UNIT = 16384.0
 SLOTS = 9
@@ -20,7 +21,7 @@
 DEGREE = SLOTS * HALF
 META = DEGREE + 8
 PACKED = META + 8
-COL = ("z", "core")
+COLS = NZ * NC
 LIMIT = pltpu.CompilerParams(vmem_limit_bytes=24 * 2**20)
 VMEM = pl.BlockSpec(memory_space=pltpu.VMEM)
 SMEM = pl.BlockSpec(memory_space=pltpu.SMEM)
@@ -236,7 +237,8 @@
             lefts, rights = [], []
             for s in (2 * pair, 2 * pair + 1):
                 k = ids_ref[s, c]
-                inverse = inverse_ref[k // 4, pl.ds(k % 4, 1), :]
+                chip = (k // 8 + NZ - FIRST_Z) % NZ
+                inverse = inverse_ref[NC * chip + 1 - k // 4 % NC, pl.ds(k % 4, 1), :]
                 if dense:
                     inside = pl.ds(pl.multiple_of((k % 4) * TILE, TILE), TILE)
                     left = panel_ref[k // 4, pl.ds(0, 2 * TILE), inside].astype(jnp.int32).astype(F32)
@@ -244,11 +246,11 @@
                 else:
                     parts = []
                     for t in range(2):
-                        slot = slots_ref[k // 8, 8 * t + k % 8]
+                        slot = slots_ref[chip, 8 * t + k % 8]
                         start = pl.multiple_of(jnp.clip(slot, 0, SLOTS - 1) * HALF, HALF)
                         scaled = jnp.where(slot >= 0, inverse, 0.0)
                         for core in range(NC):
-                            part = full_ref[(k // 8) * NC + core, pl.ds(start, HALF)].astype(jnp.int32)
+                            part = full_ref[chip * NC + 1 - core, pl.ds(start, HALF)].astype(jnp.int32)
                             parts.append((part.astype(F32) * scaled).astype(BF16))
                     lefts.append(jnp.concatenate(parts, axis=0))
                 rights.extend(right_ref[place_of(8 * c + e, FIRST[1]), s] for e in range(8))
@@ -299,26 +301,28 @@
 def on_device(weights, tile_mask):
     got = exchange(slices(tile_mask, weights), FIRST[0])
     panel = fixed_panel(tile_mask, weights)
-    other = lax.ppermute(panel, "core", [(0, 1), (1, 0)])
-    packed = pack(lax.axis_index("core").reshape(1), panel, other)
+    other = lax.ppermute(panel, "col", [(col, col ^ 1) for col in range(COLS)])
+    packed = pack((lax.axis_index("col") % NC).reshape(1), panel, other)
     own = (lax.axis_index("row") // 8).reshape(1)
     placed, full, ids = place(own, got, packed)
     right = exchange(placed, FIRST[1])
-    full = lax.all_gather(full, COL)
+    group = [(col + NC * FIRST_Z) % COLS ^ 1 for col in range(COLS)]
+    full = full.reshape(1, PACKED // 8, 8, TILE)
+    full = lax.all_gather(full, "col", axis=0, tiled=True, axis_index_groups=[group])
+    full = full.reshape(COLS, PACKED, TILE)
     slots = full[::2, META, :16].astype(jnp.int32)
     inflated, mass, most = expand(ids, slots, full, right)
     mass = exchange(mass, FIRST[2])
 
     def overfull():
-        inflated, mass, _ = expand(ids, slots, full, lax.all_gather(panel, COL), right)
+        inflated, mass, _ = expand(ids, slots, full, lax.all_gather(panel, "col"), right)
         return scale(inflated, exchange(mass, FIRST[2]))
 
     return lax.cond(most[0] > SLOTS, overfull, lambda: scale(inflated, mass))
 
 
 def solution(mesh):
-    split = Mesh(mesh.devices.reshape(ROWS, NZ, NC), ("row", "z", "core"))
-    placed = P("row", COL)
+    placed = P("row", "col")
     return jax.shard_map(
-        on_device, mesh=split, in_specs=(placed, placed), out_specs=placed, check_vma=False
+        on_device, mesh=mesh, in_specs=(placed, placed), out_specs=placed, check_vma=False
     )

time: 81.2 us -> 81.4 us (level)
  no operation moved by 1% of the time
where the time goes in v10:
time: 81.4 us; the launch traced here: 80.9 us
  blocking collectives  34.8 us (43%)
  starting transfers between devices  33.6 us (41%)
  Pallas kernels  9.04 us (11%)
  waiting for transfers between devices  2.72 us (3%)
    all_gather x1, blocking collectives, on_device(): lax.all_gather(full, 'col', axis=0, tiled=True, axis_index_groups=[group])  34.8 us
    all_to_all x3, starting transfers between devices, exchange(): lax.all_to_all(blocks, 'row', split_axis=0, concat_axis=0, tiled=True, ax...  27.5 us
    ppermute x1, starting transfers between devices, on_device(): other = lax.ppermute(panel, 'col', [(col, col ^ 1) for col in range(COLS)])  6.05 us
    pallas_call x1, Pallas kernels, expand(): pl.pallas_call(functools.partial(expand_kernel, dense), out_shape=(pltpu....  3.03 us
    pallas_call x1, Pallas kernels, slices(): pl.pallas_call(slice_kernel, out_shape=jax.ShapeDtypeStruct((ROWS, 3 * SL...  1.81 us
    pallas_call x1, Pallas kernels, place(): pl.pallas_call(place_kernel, out_shape=(pltpu.VMEM((ROWS, KEEP, SLICE, TI...  1.63 us
  transfers between devices with their start and end apart: 4, of which 2 were waited for; matrix products, arithmetic and copies ran while one was open for 0% of the time, Pallas kernels for 2%

profile of v10, /device:TPU:1, one launch (start us, length us, event | category | flops | bytes accessed | tf_op | source)
XLA Modules:
  0.0 80.9 jit_solution(4080851952058564412)
XLA Ops:
  0.0 1.8 %slices.1 = bf16[32,48,128]{2,1,0:T(8,128)(2,1)} custom-call(s32[2,4]{1,0:T(2,128)} %mask_ref.3, bf16[256,512]{1,0:T(8,128)(2,1)} %w_ref.3), custom_call_target="tpu_custom_call" | custom-call | tf_op jit(solution)/shard_map/slices/pallas_call | solution.py:82
  1.8 12.5 %all-to-all-start.1 = ((bf16[32,48,128]{2,1,0:T(8,128)(2,1)}), bf16[32,48,128]{2,1,0:T(8,128)(2,1)S(1)}, u32[]{:S(2)}, u32[]{:S(2)}) async-start(bf16[32,48,128]{2,1,0:T(8,128)(2,1)} %slices.1), calls=%async_computation.1 | async-start | bytes 786432 | tf_op jit(solution)/shard_map/all_to_all | solution.py:40
  14.3 1.1 %panel.1.panel_ref = s16[264,512]{1,0:T(8,128)(2,1)S(1)} custom-call(s32[2,4]{1,0:T(2,128)} %mask_ref.3, bf16[256,512]{1,0:T(8,128)(2,1)} %w_ref.3), custom_call_target="tpu_custom_call" | custom-call | tf_op jit(solution)/shard_map/panel/pallas_call | solution.py:105
  15.4 6.1 %collective-permute-start = (s16[264,512]{1,0:T(8,128)(2,1)S(1)}, s16[264,512]{1,0:T(8,128)(2,1)S(1)}, u32[]{:S(2)}, u32[]{:S(2)}) collective-permute-start(s16[264,512]{1,0:T(8,128)(2,1)S(1)} %panel.1.panel_ref), channel_id=1, source_target_pairs={{0,1},{1,0},{2,3},{3,2},{4,5},{5,4},{6,7},{7,6},{8,9},{9,8},{10,11... | collective-permute-start | bytes 811016 | tf_op jit(solution)/shard_map/ppermute | solution.py:304
  21.4 1.1 %collective-permute-done.other_ref = s16[264,512]{1,0:T(8,128)(2,1)S(1)} collective-permute-done((s16[264,512]{1,0:T(8,128)(2,1)S(1)}, s16[264,512]{1,0:T(8,128)(2,1)S(1)}, u32[]{:S(2)}, u32[]{:S(2)}) %collective-permute-start) | collective-permute-done | bytes 270368 | tf_op jit(solution)/shard_map/ppermute | solution.py:304
  22.6 0.6 pack.1.packed_ref
  23.2 0.0 all-to-all-done.1.got_ref
  23.2 1.6 %place.1 = (bf16[32,8,16,128]{3,2,1,0:T(8,128)(2,1)}, s16[592,128]{1,0:T(8,128)(2,1)S(1)}, s32[8,128]{1,0:T(8,128)S(1)}) custom-call(s32[1]{0:T(128)} %bitcast.1.own_ref, bf16[32,48,128]{2,1,0:T(8,128)(2,1)S(1)} %all-to-all-done.1.got_ref, s16[592,128]{1,0:T(8,128)(2,1)S(1)} %pack.1.packed_ref), custom_call_target="tpu_custom_call" | custom-call | tf_op jit(solution)/shard_map/place/pallas_call | solution.py:206
  24.8 5.2 %all-to-all-start.2 = ((bf16[32,8,16,128]{3,2,1,0:T(8,128)(2,1)}), bf16[32,8,16,128]{3,2,1,0:T(8,128)(2,1)}, u32[]{:S(2)}, u32[]{:S(2)}) async-start(bf16[32,8,16,128]{3,2,1,0:T(8,128)(2,1)} %get-tuple-element.39), calls=%async_computation.2 | async-start | bytes 2097152 | tf_op jit(solution)/shard_map/all_to_all | solution.py:40
  30.0 34.8 %all-gather.4 = s16[16,74,8,128]{3,2,1,0:T(8,128)(2,1)S(1)} all-gather(s16[1,74,8,128]{3,2,1,0:T(8,128)(2,1)S(1)} %bitcast.8), channel_id=1, replica_groups={{9,8,11,10,13,12,15,14,1,0,3,2,5,4,7,6},{25,24,27,26,29,28,31,30,17,16,..., dimensions={0}, use_global_device_ids=true | all-gather | bytes 2576384 | tf_op jit(solution)/shard_map/all_gather | solution.py:311
  64.9 0.0 all-to-all-done.2.refs_0_
  64.9 3.0 %expand.1 = (f32[256,512]{1,0:T(8,128)S(1)}, f32[32,1,512]{2,1,0:T(1,128)}, s32[1]{0:T(128)}) custom-call(s32[8,128]{1,0:T(8,128)S(1)} %get-tuple-element.37.ids_ref, s32[8,16]{1,0:T(8,128)S(1)} %bitcast.12, s16[16,592,128]{2,1,0:T(8,128)(2,1)S(1)} %bitcast.10, bf16[32,8,16,128]{3,2,1,0:T(8,128)(2,1)} %all-to-all-done.2.refs_0_), custom_call_target="tpu_custom_call" | custom-call | tf_op jit(solution)/shard_map/expand/pallas_call | solution.py:271
  67.9 9.8 %all-to-all-start.3 = ((f32[32,1,512]{2,1,0:T(1,128)}), f32[32,1,512]{2,1,0:T(1,128)S(1)}, u32[]{:S(2)}, u32[]{:S(2)}) async-start(f32[32,1,512]{2,1,0:T(1,128)} %get-tuple-element.42), calls=%async_computation.3 | async-start | bytes 131072 | tf_op jit(solution)/shard_map/all_to_all | solution.py:40
  78.4 1.6 %all-to-all-done.3 = f32[32,1,512]{2,1,0:T(1,128)S(1)} async-done(((f32[32,1,512]{2,1,0:T(1,128)}), f32[32,1,512]{2,1,0:T(1,128)S(1)}, u32[]{:S(2)}, u32[]{:S(2)}) %all-to-all-start.3) | async-done | bytes 65568 | tf_op jit(solution)/shard_map/all_to_all | solution.py:40
  80.0 0.9 %conditional.1 = (f32[256,512]{1,0:T(8,128)}) conditional(s32[]{:T(128)} %bitcast.6, (f32[256,512]{1,0:T(8,128)S(1)}, f32[32,1,512]{2,1,0:T(1,128)S(1)}) %tuple.11, (s16[264,512]{1,0:T(8,128)(2,1)S(1)}, s32[8,128]{1,0:T(8,128)S(1)}, s32[8,16]{1,0:T(8,128)S(1)}, s16[16,592,128]{2,1,0:T(8,128)(2,1)S(1)}, bf16[32,8,16,128]{3,2,1,0:T(8,128)(2,1)}) %tuple.18), branch_computations={%region_0.1_spmd, %region_1.2_spmd} | conditional | bytes 4726792 | solution.py:321
  80.0 0.9 %scale.2 = f32[256,512]{1,0:T(8,128)} custom-call(f32[256,512]{1,0:T(8,128)S(1)} %get-tuple-element.22.inflated_ref, f32[32,1,512]{2,1,0:T(1,128)S(1)} %get-tuple-element.23.mass_ref), custom_call_target="tpu_custom_call" | custom-call | tf_op jit(solution)/shard_map/cond/branch_0_fun/scale/pallas_call | solution.py:292
  (1 shorter events, 0.0 us)
Async XLA Ops:
  1.8 21.4 %all-to-all-start.1 = ((bf16[32,48,128]{2,1,0:T(8,128)(2,1)}), bf16[32,48,128]{2,1,0:T(8,128)(2,1)S(1)}, u32[]{:S(2)}, u32[]{:S(2)}) async-start(bf16[32,48,128]{2,1,0:T(8,128)(2,1)} %slices.1), calls=%async_computation.1 | async-start | bytes 786432 | tf_op jit(solution)/shard_map/all_to_all | solution.py:40
  15.4 7.2 %collective-permute-start = (s16[264,512]{1,0:T(8,128)(2,1)S(1)}, s16[264,512]{1,0:T(8,128)(2,1)S(1)}, u32[]{:S(2)}, u32[]{:S(2)}) collective-permute-start(s16[264,512]{1,0:T(8,128)(2,1)S(1)} %panel.1.panel_ref), channel_id=1, source_target_pairs={{0,1},{1,0},{2,3},{3,2},{4,5},{5,4},{6,7},{7,6},{8,9},{9,8},{10,11... | collective-permute-start | bytes 811016 | tf_op jit(solution)/shard_map/ppermute | solution.py:304
  24.8 40.1 %all-to-all-start.2 = ((bf16[32,8,16,128]{3,2,1,0:T(8,128)(2,1)}), bf16[32,8,16,128]{3,2,1,0:T(8,128)(2,1)}, u32[]{:S(2)}, u32[]{:S(2)}) async-start(bf16[32,8,16,128]{3,2,1,0:T(8,128)(2,1)} %get-tuple-element.39), calls=%async_computation.2 | async-start | bytes 2097152 | tf_op jit(solution)/shard_map/all_to_all | solution.py:40
  67.9 12.1 %all-to-all-start.3 = ((f32[32,1,512]{2,1,0:T(1,128)}), f32[32,1,512]{2,1,0:T(1,128)S(1)}, u32[]{:S(2)}, u32[]{:S(2)}) async-start(f32[32,1,512]{2,1,0:T(1,128)} %get-tuple-element.42), calls=%async_computation.3 | async-start | bytes 131072 | tf_op jit(solution)/shard_map/all_to_all | solution.py:40

commit v11 on v10

--- a/solution.py
+++ b/solution.py
@@ -16,7 +16,7 @@
 FIRST_Z = 4
 F32, BF16, I16 = jnp.float32, jnp.bfloat16, jnp.int16
 UNIT = 16384.0
-SLOTS = 9
+SLOTS = 8
 HALF = TILE // 2
 DEGREE = SLOTS * HALF
 META = DEGREE + 8

time: 81.4 us -> 80.7 us (level)
  no operation moved by 1% of the time
where the time goes in v11:
time: 80.7 us; the launch traced here: 80.2 us
  blocking collectives  34.1 us (42%)
  starting transfers between devices  33.6 us (42%)
  Pallas kernels  8.97 us (11%)
  waiting for transfers between devices  2.72 us (3%)
    all_gather x1, blocking collectives, on_device(): lax.all_gather(full, 'col', axis=0, tiled=True, axis_index_groups=[group])  34.1 us
    all_to_all x3, starting transfers between devices, exchange(): lax.all_to_all(blocks, 'row', split_axis=0, concat_axis=0, tiled=True, ax...  27.6 us
    ppermute x1, starting transfers between devices, on_device(): other = lax.ppermute(panel, 'col', [(col, col ^ 1) for col in range(COLS)])  6.05 us
    pallas_call x1, Pallas kernels, expand(): pl.pallas_call(functools.partial(expand_kernel, dense), out_shape=(pltpu....  3.03 us
    pallas_call x1, Pallas kernels, slices(): pl.pallas_call(slice_kernel, out_shape=jax.ShapeDtypeStruct((ROWS, 3 * SL...  1.81 us
    pallas_call x1, Pallas kernels, place(): pl.pallas_call(place_kernel, out_shape=(pltpu.VMEM((ROWS, KEEP, SLICE, TI...  1.63 us
  transfers between devices with their start and end apart: 4, of which 2 were waited for; matrix products, arithmetic and copies ran while one was open for 0% of the time, Pallas kernels for 2%

profile of v11, /device:TPU:1, one launch (start us, length us, event | category | flops | bytes accessed | tf_op | source)
XLA Modules:
  0.0 80.2 jit_solution(15073827881602954107)
XLA Ops:
  0.0 1.8 %slices.1 = bf16[32,48,128]{2,1,0:T(8,128)(2,1)} custom-call(s32[2,4]{1,0:T(2,128)} %mask_ref.3, bf16[256,512]{1,0:T(8,128)(2,1)} %w_ref.3), custom_call_target="tpu_custom_call" | custom-call | tf_op jit(solution)/shard_map/slices/pallas_call | solution.py:82
  1.8 12.5 %all-to-all-start.1 = ((bf16[32,48,128]{2,1,0:T(8,128)(2,1)}), bf16[32,48,128]{2,1,0:T(8,128)(2,1)S(1)}, u32[]{:S(2)}, u32[]{:S(2)}) async-start(bf16[32,48,128]{2,1,0:T(8,128)(2,1)} %slices.1), calls=%async_computation.1 | async-start | bytes 786432 | tf_op jit(solution)/shard_map/all_to_all | solution.py:40
  14.3 1.1 %panel.1.panel_ref = s16[264,512]{1,0:T(8,128)(2,1)S(1)} custom-call(s32[2,4]{1,0:T(2,128)} %mask_ref.3, bf16[256,512]{1,0:T(8,128)(2,1)} %w_ref.3), custom_call_target="tpu_custom_call" | custom-call | tf_op jit(solution)/shard_map/panel/pallas_call | solution.py:105
  15.4 6.1 %collective-permute-start = (s16[264,512]{1,0:T(8,128)(2,1)S(1)}, s16[264,512]{1,0:T(8,128)(2,1)S(1)}, u32[]{:S(2)}, u32[]{:S(2)}) collective-permute-start(s16[264,512]{1,0:T(8,128)(2,1)S(1)} %panel.1.panel_ref), channel_id=1, source_target_pairs={{0,1},{1,0},{2,3},{3,2},{4,5},{5,4},{6,7},{7,6},{8,9},{9,8},{10,11... | collective-permute-start | bytes 811016 | tf_op jit(solution)/shard_map/ppermute | solution.py:304
  21.4 1.1 %collective-permute-done.other_ref = s16[264,512]{1,0:T(8,128)(2,1)S(1)} collective-permute-done((s16[264,512]{1,0:T(8,128)(2,1)S(1)}, s16[264,512]{1,0:T(8,128)(2,1)S(1)}, u32[]{:S(2)}, u32[]{:S(2)}) %collective-permute-start) | collective-permute-done | bytes 270368 | tf_op jit(solution)/shard_map/ppermute | solution.py:304
  22.6 0.5 pack.1.packed_ref
  23.1 0.0 all-to-all-done.1.got_ref
  23.1 1.6 %place.1 = (bf16[32,8,16,128]{3,2,1,0:T(8,128)(2,1)}, s16[528,128]{1,0:T(8,128)(2,1)S(1)}, s32[8,128]{1,0:T(8,128)S(1)}) custom-call(s32[1]{0:T(128)} %bitcast.1.own_ref, bf16[32,48,128]{2,1,0:T(8,128)(2,1)S(1)} %all-to-all-done.1.got_ref, s16[528,128]{1,0:T(8,128)(2,1)S(1)} %pack.1.packed_ref), custom_call_target="tpu_custom_call" | custom-call | tf_op jit(solution)/shard_map/place/pallas_call | solution.py:206
  24.8 5.3 %all-to-all-start.2 = ((bf16[32,8,16,128]{3,2,1,0:T(8,128)(2,1)}), bf16[32,8,16,128]{3,2,1,0:T(8,128)(2,1)}, u32[]{:S(2)}, u32[]{:S(2)}) async-start(bf16[32,8,16,128]{3,2,1,0:T(8,128)(2,1)} %get-tuple-element.39), calls=%async_computation.2 | async-start | bytes 2097152 | tf_op jit(solution)/shard_map/all_to_all | solution.py:40
  30.0 34.1 %all-gather.4 = s16[16,66,8,128]{3,2,1,0:T(8,128)(2,1)S(1)} all-gather(s16[1,66,8,128]{3,2,1,0:T(8,128)(2,1)S(1)} %bitcast.8), channel_id=1, replica_groups={{9,8,11,10,13,12,15,14,1,0,3,2,5,4,7,6},{25,24,27,26,29,28,31,30,17,16,..., dimensions={0}, use_global_device_ids=true | all-gather | bytes 2297856 | tf_op jit(solution)/shard_map/all_gather | solution.py:311
  64.2 0.0 all-to-all-done.2.refs_0_
  64.2 3.0 %expand.1 = (f32[256,512]{1,0:T(8,128)S(1)}, f32[32,1,512]{2,1,0:T(1,128)}, s32[1]{0:T(128)}) custom-call(s32[8,128]{1,0:T(8,128)S(1)} %get-tuple-element.37.ids_ref, s32[8,16]{1,0:T(8,128)S(1)} %bitcast.12, s16[16,528,128]{2,1,0:T(8,128)(2,1)S(1)} %bitcast.10, bf16[32,8,16,128]{3,2,1,0:T(8,128)(2,1)} %all-to-all-done.2.refs_0_), custom_call_target="tpu_custom_call" | custom-call | tf_op jit(solution)/shard_map/expand/pallas_call | solution.py:271
  67.2 9.8 %all-to-all-start.3 = ((f32[32,1,512]{2,1,0:T(1,128)}), f32[32,1,512]{2,1,0:T(1,128)S(1)}, u32[]{:S(2)}, u32[]{:S(2)}) async-start(f32[32,1,512]{2,1,0:T(1,128)} %get-tuple-element.42), calls=%async_computation.3 | async-start | bytes 131072 | tf_op jit(solution)/shard_map/all_to_all | solution.py:40
  77.7 1.6 %all-to-all-done.3 = f32[32,1,512]{2,1,0:T(1,128)S(1)} async-done(((f32[32,1,512]{2,1,0:T(1,128)}), f32[32,1,512]{2,1,0:T(1,128)S(1)}, u32[]{:S(2)}, u32[]{:S(2)}) %all-to-all-start.3) | async-done | bytes 65568 | tf_op jit(solution)/shard_map/all_to_all | solution.py:40
  79.3 0.9 %conditional.1 = (f32[256,512]{1,0:T(8,128)}) conditional(s32[]{:T(128)} %bitcast.6, (f32[256,512]{1,0:T(8,128)S(1)}, f32[32,1,512]{2,1,0:T(1,128)S(1)}) %tuple.11, (s16[264,512]{1,0:T(8,128)(2,1)S(1)}, s32[8,128]{1,0:T(8,128)S(1)}, s32[8,16]{1,0:T(8,128)S(1)}, s16[16,528,128]{2,1,0:T(8,128)(2,1)S(1)}, bf16[32,8,16,128]{3,2,1,0:T(8,128)(2,1)}) %tuple.18), branch_computations={%region_0.1_spmd, %region_1.2_spmd} | conditional | bytes 4726792 | solution.py:321
  79.3 0.9 %scale.2 = f32[256,512]{1,0:T(8,128)} custom-call(f32[256,512]{1,0:T(8,128)S(1)} %get-tuple-element.22.inflated_ref, f32[32,1,512]{2,1,0:T(1,128)S(1)} %get-tuple-element.23.mass_ref), custom_call_target="tpu_custom_call" | custom-call | tf_op jit(solution)/shard_map/cond/branch_0_fun/scale/pallas_call | solution.py:292
  (1 shorter events, 0.0 us)
Async XLA Ops:
  1.8 21.3 %all-to-all-start.1 = ((bf16[32,48,128]{2,1,0:T(8,128)(2,1)}), bf16[32,48,128]{2,1,0:T(8,128)(2,1)S(1)}, u32[]{:S(2)}, u32[]{:S(2)}) async-start(bf16[32,48,128]{2,1,0:T(8,128)(2,1)} %slices.1), calls=%async_computation.1 | async-start | bytes 786432 | tf_op jit(solution)/shard_map/all_to_all | solution.py:40
  15.4 7.2 %collective-permute-start = (s16[264,512]{1,0:T(8,128)(2,1)S(1)}, s16[264,512]{1,0:T(8,128)(2,1)S(1)}, u32[]{:S(2)}, u32[]{:S(2)}) collective-permute-start(s16[264,512]{1,0:T(8,128)(2,1)S(1)} %panel.1.panel_ref), channel_id=1, source_target_pairs={{0,1},{1,0},{2,3},{3,2},{4,5},{5,4},{6,7},{7,6},{8,9},{9,8},{10,11... | collective-permute-start | bytes 811016 | tf_op jit(solution)/shard_map/ppermute | solution.py:304
  24.8 39.4 %all-to-all-start.2 = ((bf16[32,8,16,128]{3,2,1,0:T(8,128)(2,1)}), bf16[32,8,16,128]{3,2,1,0:T(8,128)(2,1)}, u32[]{:S(2)}, u32[]{:S(2)}) async-start(bf16[32,8,16,128]{3,2,1,0:T(8,128)(2,1)} %get-tuple-element.39), calls=%async_computation.2 | async-start | bytes 2097152 | tf_op jit(solution)/shard_map/all_to_all | solution.py:40
  67.2 12.1 %all-to-all-start.3 = ((f32[32,1,512]{2,1,0:T(1,128)}), f32[32,1,512]{2,1,0:T(1,128)S(1)}, u32[]{:S(2)}, u32[]{:S(2)}) async-start(f32[32,1,512]{2,1,0:T(1,128)} %get-tuple-element.42), calls=%async_computation.3 | async-start | bytes 131072 | tf_op jit(solution)/shard_map/all_to_all | solution.py:40
